TPU v7x, 256 devices: a whole 4x4x8 slice. The times are simulated.
256 devices in a mesh: dp: 32 (over z, x), mp: 4 (over y), mc: 2 (over core).
Axes of the slice: x: 4, y: 4, z: 8, core: 2. Of those that a mesh axis runs over, the one named last changes fastest.
Arguments:
- features: bfloat16 [12608, 768], P('dp'), may hold values from -6 to 6
- out_cotangent: bfloat16 [2, 12608, 768], P('mc', 'dp'), may hold values from -6 to 6
- mean_up: float32 [768, 3072], P('dp', 'mp'), may hold values from -0.21875 to 0.21875
- precision_up: float32 [768, 3072], P('dp', 'mp'), may hold values from 4 to 64
- noise_up: float32 [2, 768, 3072], P('mc', 'dp', 'mp'), may hold values from -6 to 6
- mean_down: float32 [768, 3072], P('dp', 'mp'), may hold values from -0.109375 to 0.109375
- precision_down: float32 [768, 3072], P('dp', 'mp'), may hold values from 4 to 64
- noise_down: float32 [2, 768, 3072], P('mc', 'dp', 'mp'), may hold values from -6 to 6
Outputs:
- mean_new_up: float32 [768, 3072], P('dp', 'mp')
- precision_new_up: float32 [768, 3072], P('dp', 'mp')
- mean_new_down: float32 [768, 3072], P('dp', 'mp')
- precision_new_down: float32 [768, 3072], P('dp', 'mp')
- input_grad: bfloat16 [2, 12608, 768], P('mc', 'dp', 'mp')
All inputs are finite; a program needn't handle non-finite values.
Results may differ from a plain program's by a relative error of at most 0.0015.
The roundings to bfloat16 on the way count: a program that leaves them out, or rounds other values in their place, can miss the bound.
Values may be sent and summed in bfloat16 or wider, within the bound.
No kernel may reach another device: no remote copies, remote signals or barrier semaphores. Data moves between devices by JAX's collectives and lax.ppermute only.
A program may use at most 64 MiB of HBM per device.

v0:
```python
import jax
import jax.numpy as jnp
from jax import lax
from jax.experimental import pallas as pl
from jax.experimental.pallas import tpu as pltpu
from jax.sharding import Mesh
from jax.sharding import PartitionSpec as P


D = 768
FF = 3072
PATCHES = 197
ROWS = 2 * PATCHES
HEAD = 208
TAIL = ROWS - HEAD
FULL = 400
HALF = D // 2
DP = ("z", "x")
ZXY = ("z", "x", "mp")

reciprocal_root = 0.7071067811865476
normal_peak = 0.3989422804014327
tempering = 100.0
damping = 4.0
average_rate = 0.25
step_rate = 0.05
clip_level = 0.01
square_unit = 256.0
grad_unit = 8.0

SMEM = pl.BlockSpec(memory_space=pltpu.SMEM)
VMEM = pl.BlockSpec(memory_space=pltpu.VMEM)


def shift(value, axis, k):
    n = lax.axis_size(axis)
    return lax.ppermute(value, axis, [(i, (i + k) % n) for i in range(n)])


def sample_kernel(mu_ref, pu_ref, nu_ref, md_ref, pd_ref, nd_ref, out_ref):
    nz, nx, _, width = out_ref.shape

    def drawn(m, p, n):
        spread = 1.0 / jnp.sqrt(tempering * (p[...] + damping))
        return m[...] + spread * n[...]

    up, down = drawn(mu_ref, pu_ref, nu_ref), drawn(md_ref, pd_ref, nd_ref)
    wide = width // 2
    for i in range(nx):
        cut = slice(i * wide, (i + 1) * wide)
        both = jnp.concatenate([up[:, cut], down[:, cut]], axis=1).astype(jnp.bfloat16)
        for k in range(nz):
            out_ref[k, i] = both


def stage_kernel(core_ref, f_ref, c_ref, head_ref, tail_ref):
    first = core_ref[0] == 0
    for out, cut in ((head_ref, slice(0, HEAD)), (tail_ref, slice(HEAD, ROWS))):
        out[:, 0:HALF] = jnp.where(first, f_ref[cut, 0:HALF], f_ref[cut, HALF:D])
        out[:, HALF:] = c_ref[cut, :]


def dot_rows(left, right):
    return lax.dot_general(
        left, right, (((0,), (0,)), ((), ())), preferred_element_type=jnp.float32
    )


def pack_lanes(value, rows):
    return jnp.concatenate([value[:rows], value[value.shape[0] - rows :]], axis=1)


def groups_kernel(core_ref, wu_ref, wd_ref, *refs, swapped, last):
    core = core_ref[0]
    if last:
        u0, u1, near, acc_in = refs[:4]
        mine_ref, other_ref, parcel, f_s, c_s, acc = refs[4:]
        pairs = [(u0, u1, swapped[0], parcel)]
    else:
        f_ref, c_ref, r0, r1, l0, l1, near = refs[:7]
        acc, pg_ref, parcel_r, parcel_l, f_s, c_s = refs[7:]
        acc_in = None
        pairs = [
            (None, None, None, pg_ref),
            (r0, r1, swapped[0], parcel_r),
            (l0, l1, swapped[1], parcel_l),
        ]
    up_at, down_at = core, 1 - core
    wide = wu_ref.shape[1]
    row = lax.broadcasted_iota(jnp.int32, (HEAD, wide), 0)
    f_s[FULL - 16 : FULL, :] = jnp.zeros((16, D), jnp.bfloat16)
    c_s[FULL - 16 : FULL, :] = jnp.zeros((16, D), jnp.bfloat16)
    for g, (u0, u1, spots, out) in enumerate(pairs):
        if u0 is None:
            f_s[0:ROWS, :] = f_ref[...]
            c_s[0:ROWS, :] = c_ref[...]
            at = [0, HALF]
        else:
            f_s[0:HEAD, 0:HALF] = u0[:, 0:HALF]
            f_s[HEAD:ROWS, 0:HALF] = u1[:, 0:HALF]
            f_s[0:HEAD, HALF:D] = near[spots[0] : spots[0] + HEAD, :]
            f_s[HEAD:ROWS, HALF:D] = near[spots[1] : spots[1] + TAIL, :]
            c_s[0:HEAD, :] = u0[:, HALF:]
            c_s[HEAD:ROWS, :] = u1[:, HALF:]
            at = [pl.multiple_of(a, HALF) for a in (core * HALF, (1 - core) * HALF)]
        preact = sum(
            jnp.dot(
                f_s[:, i * HALF : (i + 1) * HALF],
                wu_ref[pl.ds(at[i], HALF), :],
                preferred_element_type=jnp.float32,
            )
            for i in range(2)
        )
        cumulative = 0.5 * (1.0 + lax.erf(preact * reciprocal_root))
        density = normal_peak * jnp.exp(-0.5 * preact * preact)
        hidden = (preact * cumulative).astype(jnp.bfloat16)
        back = jnp.dot(c_s[...], wd_ref[...], preferred_element_type=jnp.float32)
        pg = (back * (cumulative + preact * density)).astype(jnp.bfloat16)
        if u0 is None:
            out[...] = pg[:ROWS]
        else:
            out[0:HALF, :] = pack_lanes(wu_ref[...], HALF)
            out[HALF:, :] = pack_lanes(pg, HEAD)
        zero = jnp.zeros((), jnp.bfloat16)
        cuts = (slice(0, HEAD), slice(FULL - HEAD, FULL))
        keep = (row < PATCHES, row >= PATCHES - (FULL - HEAD))

        def add(index, at, source, lanes, right):
            each = [dot_rows(source[cut, lanes], right[i]) for i, cut in enumerate(cuts)]
            total = jnp.concatenate(
                [each[0] + each[1], each[0] * each[0] + each[1] * each[1]], axis=1
            )
            span = pl.ds(at, HALF)
            if g == 0 and last:
                acc[index, span, :] = acc_in[index, span, :] + total
            elif g == 0:
                acc[index, span, :] = total
            else:
                acc[index, span, :] = acc[index, span, :] + total

        by_image = [
            [jnp.where(k, v[cut], zero) for cut, k in zip(cuts, keep)] for v in (pg, hidden)
        ]
        for i in range(2):
            lanes = slice(i * HALF, (i + 1) * HALF)
            add(up_at, at[i], f_s, lanes, by_image[0])
            add(down_at, i * HALF, c_s, lanes, by_image[1])
    if last:
        mine_ref[...] = acc[0]
        other_ref[...] = acc[1]


def run_groups(core, w_up, w_down, ins, swapped, last):
    wide = w_up.shape[1]
    sums = jax.ShapeDtypeStruct((D, 2 * wide), jnp.float32)
    parcel = jax.ShapeDtypeStruct((HALF + HEAD, 2 * wide), jnp.bfloat16)
    pair = pltpu.VMEM((FULL, D), jnp.bfloat16)
    if last:
        out_shape, scratch = [sums, sums, parcel], [pltpu.VMEM((2, D, 2 * wide), jnp.float32)]
    else:
        out_shape = [
            jax.ShapeDtypeStruct((2, D, 2 * wide), jnp.float32),
            jax.ShapeDtypeStruct((ROWS, wide), jnp.bfloat16),
            parcel,
            parcel,
        ]
        scratch = []
    groups = 1 if last else 3
    return pl.pallas_call(
        lambda *refs: groups_kernel(*refs, swapped=swapped, last=last),
        out_shape=out_shape,
        in_specs=[SMEM] + [VMEM] * (len(ins) + 2),
        out_specs=[VMEM] * len(out_shape),
        scratch_shapes=[pair, pair] + scratch,
        cost_estimate=pl.CostEstimate(
            flops=groups * ROWS * D * wide * 8,
            transcendentals=2 * groups * ROWS * wide,
            bytes_accessed=6 << 20,
        ),
    )(core, w_up, w_down, *ins)


def input_kernel(at_ref, pg_ref, up_ref, *refs):
    parcels, outs, (up_s, pg_s) = refs[:3], refs[3:-2], refs[-2:]
    wide = pg_ref.shape[1]
    for i, parcel in enumerate(parcels):
        up_s[i, 0:HALF] = parcel[0:HALF, 0:wide]
        up_s[i, HALF:D] = parcel[0:HALF, wide:]
        pg_s[i, 0:HEAD] = parcel[HALF:, 0:wide]
        pg_s[i, FULL - HEAD : FULL] = parcel[HALF:, wide:]
    for k, out in enumerate(outs):
        at = pl.multiple_of(((at_ref[0] + k) % len(outs)) * wide, wide)
        span = pl.ds(at, wide)

        def product(left, right):
            return lax.dot_general(
                left, right, (((1,), (1,)), ((), ())), preferred_element_type=jnp.float32
            )

        value = product(pg_ref[...], up_ref[span, :])
        for i in range(len(parcels)):
            value = value + product(pg_s[i, 0:ROWS], up_s[i, span, :])
        out[...] = value


def shards(
    features, out_cotangent, mean_up, precision_up, noise_up, mean_down, precision_down, noise_down
):
    core = lax.axis_index("mc").astype(jnp.int32)
    nz, nx, ny = lax.axis_size("z"), lax.axis_size("x"), lax.axis_size("mp")
    rows, cols = mean_up.shape
    wide = cols // nx
    core_at = core.reshape(1)
    cotangent = out_cotangent[0]

    u0, u1 = pl.pallas_call(
        stage_kernel,
        out_shape=[
            jax.ShapeDtypeStruct((HEAD, HALF + D), jnp.bfloat16),
            jax.ShapeDtypeStruct((TAIL, HALF + D), jnp.bfloat16),
        ],
        in_specs=[SMEM, VMEM, VMEM],
        out_specs=[VMEM, VMEM],
        name="stage",
    )(core_at, features, cotangent)
    r0 = shift(u0, "x", 1)
    l1 = shift(u1, "x", -1)
    r1 = shift(u1, "x", 1)
    l0 = shift(u0, "x", -1)

    payload = pl.pallas_call(
        sample_kernel,
        out_shape=jax.ShapeDtypeStruct((nz, nx, rows, 2 * wide), jnp.bfloat16),
        in_specs=[VMEM] * 6,
        out_specs=VMEM,
        name="sample",
    )(mean_up, precision_up, noise_up[0], mean_down, precision_down, noise_down[0])
    weights = lax.all_to_all(
        payload.reshape(nz * nx, rows, 2 * wide), DP, 0, 0, tiled=True
    ).reshape(D, 2 * wide)
    w_up, w_down = weights[:, :wide], weights[:, wide:]

    f0 = shift(r0, "x", 1)
    f1 = shift(l1, "x", -1)
    gap = jnp.zeros((FULL - HEAD - TAIL, HALF), jnp.bfloat16)
    near = jnp.concatenate([r0[:, :HALF], l0[:, :HALF], r1[:, :HALF], gap, l1[:, :HALF]])
    near = shift(near, "mc", 1)
    spots = ((0, 2 * HEAD), (HEAD, HEAD + FULL))
    far = shift(jnp.concatenate([f0[:, :HALF], f1[:, :HALF]]), "mc", 1)

    acc, pg, parcel_r, parcel_l = run_groups(
        core_at, w_up, w_down, [features, cotangent, r0, r1, l0, l1, near], spots, False
    )
    parcel_r = shift(parcel_r, "x", -1)
    parcel_l = shift(parcel_l, "x", 1)
    mine, other, parcel_f = run_groups(
        core_at, w_up, w_down, [f0, f1, far, acc], ((0, HEAD),), True
    )

    both = mine + shift(other, "mc", 1)
    parcel_f = shift(parcel_f, "x", 2)
    is_grad = lax.broadcasted_iota(jnp.int32, both.shape, 1) < wide
    root = jnp.sqrt(jnp.abs(both)) * jnp.where(is_grad, grad_unit, 1.0 / square_unit)
    packed = jnp.where(both < 0.0, -root, root).astype(jnp.float16)
    got = lax.all_to_all(packed.reshape(nz * nx, rows, 2 * wide), DP, 0, 0, tiled=True)
    got = got.astype(jnp.float32).reshape(nz, nx, rows, 2 * wide)
    is_grad = lax.broadcasted_iota(jnp.int32, got.shape, 3) < wide
    got = jnp.where(
        is_grad, got * jnp.abs(got) / (grad_unit * grad_unit), (square_unit * got) * (square_unit * got)
    )
    total = jnp.sum(got, axis=0).reshape(nx, rows, 2, wide)
    total = jnp.transpose(total, (2, 1, 0, 3)).reshape(2, rows, cols)
    totals = lax.all_gather(total, "mc", axis=0)

    tile = jax.ShapeDtypeStruct((ROWS, D // ny), jnp.float32)
    tiles = pl.pallas_call(
        input_kernel,
        out_shape=[tile] * ny,
        in_specs=[SMEM] + [VMEM] * 5,
        out_specs=[VMEM] * ny,
        scratch_shapes=[
            pltpu.VMEM((3, D, wide), jnp.bfloat16),
            pltpu.VMEM((3, FULL, wide), jnp.bfloat16),
        ],
        cost_estimate=pl.CostEstimate(
            flops=ROWS * D * cols * 2, transcendentals=0, bytes_accessed=4 << 20
        ),
        name="input_grad",
    )(lax.axis_index("mp").astype(jnp.int32).reshape(1), pg, w_up, parcel_r, parcel_l, parcel_f)
    tiles = [tiles[0]] + [shift(tiles[k], "mp", k) for k in range(1, ny)]
    input_grad = sum(tiles[1:], tiles[0]).astype(jnp.bfloat16)[None]

    images_all = 2 * nz * nx
    grad_up, square_up = totals[0, 0] / 2, totals[0, 1] / (2 * images_all)
    grad_down, square_down = totals[1, 0] / 2, totals[1, 1] / (2 * images_all)
    precision_new_up = (1.0 - average_rate) * precision_up + average_rate * square_up
    precision_new_down = (1.0 - average_rate) * precision_down + average_rate * square_down
    raw_up = grad_up / (precision_new_up + damping)
    raw_down = grad_down / (precision_new_down + damping)
    local = jnp.sum(raw_up * raw_up + raw_down * raw_down, axis=0, keepdims=True)
    local = jnp.sum(local.reshape(1, cols // 128, 128), axis=1, keepdims=True)
    group = nz * nx * ny
    everyone = lax.all_to_all(jnp.broadcast_to(local, (group, 1, 128)), ZXY, 0, 0, tiled=True)
    root_mean = jnp.sqrt(jnp.sum(everyone) / (2 * D * FF))
    factor = 1.0 / jnp.maximum(clip_level, root_mean)
    mean_new_up = mean_up - step_rate * factor * raw_up
    mean_new_down = mean_down - step_rate * factor * raw_down
    return (mean_new_up, precision_new_up, mean_new_down, precision_new_down, input_grad)


def solution(mesh):
    split = Mesh(
        mesh.devices.reshape(8, 4, mesh.shape["mp"], mesh.shape["mc"]), ("z", "x", "mp", "mc")
    )
    placed = (
        P(DP, None),
        P("mc", DP, None),
        P(DP, "mp"),
        P(DP, "mp"),
        P("mc", DP, "mp"),
        P(DP, "mp"),
        P(DP, "mp"),
        P("mc", DP, "mp"),
    )

    def step(*args):
        return shards(*args)

    step = jax.shard_map(
        step,
        mesh=split,
        in_specs=placed,
        out_specs=(P(DP, "mp"), P(DP, "mp"), P(DP, "mp"), P(DP, "mp"), P("mc", DP, "mp")),
        check_vma=False,
    )
    return step
```

profile of v0, /device:TPU:2, one launch (start us, length us, event | category | flops | bytes accessed | tf_op | source)
XLA Modules:
  0.0 149.2 jit_solution(13522578102032696005)
XLA Ops:
  0.6 2.0 %sample.1 = bf16[8,4,24,384]{3,2,1,0:T(8,128)(2,1)} custom-call(f32[24,768]{1,0:T(8,128)} %mu_ref.1, f32[24,768]{1,0:T(8,128)} %pu_ref.1, f32[24,768]{1,0:T(8,128)} %bitcast.49, f32[24,768]{1,0:T(8,128)} %md_ref.1, f32[24,768]{1,0:T(8,128)} %pd_ref.1, f32[24,768]{1,0:T(8,128)} %bitcast.50), custom_call_target="tpu_custom_call" | custom-call | tf_op jit(solution)/shard_map/sample/pallas_call | solution.py:231
  2.6 11.6 %all-to-all-start = ((bf16[32,24,384]{2,1,0:T(8,128)(2,1)}), bf16[32,24,384]{2,1,0:T(8,128)(2,1)S(1)}, u32[]{:S(2)}, u32[]{:S(2)}) async-start(bf16[32,24,384]{2,1,0:T(8,128)(2,1)} %bitcast.43), calls=%async_computation | async-start | bytes 1179648 | tf_op jit(solution)/shard_map/all_to_all | solution.py:238
  14.3 2.3 %stage.1 = (bf16[208,1152]{1,0:T(8,128)(2,1)}, bf16[186,1152]{1,0:T(8,128)(2,1)}) custom-call(s32[1]{0:T(128)} %bitcast.core_ref.refs_0_, bf16[394,768]{1,0:T(8,128)(2,1)} %refs_3_.1, bf16[394,768]{1,0:T(8,128)(2,1)} %bitcast.46), custom_call_target="tpu_custom_call" | custom-call | tf_op jit(solution)/shard_map/stage/pallas_call | solution.py:216
  16.6 1.5 collective-permute-start
  18.0 0.6 collective-permute-start.2
  18.6 1.4 collective-permute-start.6
  20.0 0.6 collective-permute-start.5
  20.6 13.8 %collective-permute-done.refs_5_ = bf16[208,1152]{1,0:T(8,128)(2,1)S(1)} collective-permute-done((bf16[208,1152]{1,0:T(8,128)(2,1)}, bf16[208,1152]{1,0:T(8,128)(2,1)S(1)}, u32[]{:S(2)}, u32[]{:S(2)}) %collective-permute-start) | collective-permute-done | bytes 479264 | tf_op jit(solution)/shard_map/ppermute | solution.py:37
  34.5 1.5 collective-permute-start.1
  35.9 0.9 collective-permute-start.3
  36.8 1.0 slice.55
  37.8 6.2 %collective-permute-done.5.refs_6_ = bf16[186,1152]{1,0:T(8,128)(2,1)S(1)} collective-permute-done((bf16[186,1152]{1,0:T(8,128)(2,1)}, bf16[186,1152]{1,0:T(8,128)(2,1)S(1)}, u32[]{:S(2)}, u32[]{:S(2)}) %collective-permute-start.5) | collective-permute-done | bytes 428576 | tf_op jit(solution)/shard_map/ppermute | solution.py:37
  44.0 1.9 %collective-permute-done.6.refs_7_ = bf16[208,1152]{1,0:T(8,128)(2,1)S(1)} collective-permute-done((bf16[208,1152]{1,0:T(8,128)(2,1)}, bf16[208,1152]{1,0:T(8,128)(2,1)S(1)}, u32[]{:S(2)}, u32[]{:S(2)}) %collective-permute-start.6) | collective-permute-done | bytes 479264 | tf_op jit(solution)/shard_map/ppermute | solution.py:37
  45.9 0.7 copy-done.14
  46.6 0.4 concatenate.7
  47.2 6.8 %collective-permute-done.3.refs_4_ = bf16[186,1152]{1,0:T(8,128)(2,1)S(1)} collective-permute-done((bf16[186,1152]{1,0:T(8,128)(2,1)}, bf16[186,1152]{1,0:T(8,128)(2,1)S(1)}, u32[]{:S(2)}, u32[]{:S(2)}) %collective-permute-start.3) | collective-permute-done | bytes 428576 | tf_op jit(solution)/shard_map/ppermute | solution.py:37
  54.1 0.3 collective-permute-start.4
  54.4 1.0 fusion.16
  55.4 7.4 %shard_map.119 = (f32[2,768,384]{2,1,0:T(8,128)}, bf16[394,192]{1,0:T(8,128)(2,1)}, bf16[592,384]{1,0:T(8,128)(2,1)}, bf16[592,384]{1,0:T(8,128)(2,1)}) custom-call(s32[1]{0:T(128)} %bitcast.core_ref.refs_0_, bf16[768,192]{1,0:T(8,128)(2,1)} %get-tuple-element.65.refs_1_.up_ref, bf16[768,192]{1,0:T(8,128)(2,1)} %get-tuple-element.64.refs_2_, ...), custom_call_target="tpu_custom_call" | custom-call | flops 1394343936 | bytes 6291456 | tf_op jit(solution)/shard_map/pallas_call | solution.py:169
  62.8 0.7 copy-done.6
  63.6 5.5 %shard_map.120 = (f32[768,384]{1,0:T(8,128)}, f32[768,384]{1,0:T(8,128)}, bf16[592,384]{1,0:T(8,128)(2,1)}) custom-call(s32[1]{0:T(128)} %bitcast.core_ref.refs_0_, bf16[768,192]{1,0:T(8,128)(2,1)} %get-tuple-element.65.refs_1_.up_ref, bf16[768,192]{1,0:T(8,128)(2,1)} %get-tuple-element.64.refs_2_, bf16[208,1152]{1,0:T(8,128)(2,1)} %copy-done, ...), custom_call_target="tpu_custom_call" | custom-call | flops 464781312 | bytes 6291456 | tf_op jit(solution)/shard_map/pallas_call | solution.py:169
  69.0 0.5 collective-permute-start.8
  69.5 2.7 %collective-permute-done.8 = f32[768,384]{1,0:T(8,128)S(1)} collective-permute-done((f32[768,384]{1,0:T(8,128)}, f32[768,384]{1,0:T(8,128)S(1)}, u32[]{:S(2)}, u32[]{:S(2)}) %collective-permute-start.8) | collective-permute-done | bytes 1179680 | tf_op jit(solution)/shard_map/ppermute | solution.py:37
  72.2 2.7 %fusion = f16[768,384]{1,0:T(8,128)(2,1)} fusion(f32[768,384]{1,0:T(8,128)} %get-tuple-element.21, f32[768,384]{1,0:T(8,128)S(1)} %collective-permute-done.8, f32[384]{0:T(512)S(1)} %broadcast_select_fusion), kind=kLoop, calls=%fused_computation.4 | loop fusion | flops 2064384 | bytes 2950656 | tf_op jit(solution)/shard_map/convert_element_type | solution.py:264
  74.9 8.3 %all-to-all-start.1 = ((f16[32,24,384]{2,1,0:T(8,128)(2,1)}), f16[32,24,384]{2,1,0:T(8,128)(2,1)S(1)}, u32[]{:S(2)}, u32[]{:S(2)}) async-start(f16[32,24,384]{2,1,0:T(8,128)(2,1)} %bitcast.6), calls=%async_computation.1 | async-start | bytes 1179648 | tf_op jit(solution)/shard_map/all_to_all | solution.py:265
  83.2 1.5 %collective-permute-start.10 = (bf16[592,384]{1,0:T(8,128)(2,1)S(1)}, bf16[592,384]{1,0:T(8,128)(2,1)S(1)}, u32[]{:S(2)}, u32[]{:S(2)}) collective-permute-start(bf16[592,384]{1,0:T(8,128)(2,1)S(1)} %copy-done.17), channel_id=1, source_target_pairs={{0,8},{8,16},{16,24},{24,0},{1,9},{9,17},{17,25},{25,1},{2,10},{10... | collective-permute-start | bytes 1363976 | tf_op jit(solution)/shard_map/ppermute | solution.py:37
  84.8 0.6 collective-permute-start.9
  85.3 2.1 %collective-permute-start.11 = (bf16[592,384]{1,0:T(8,128)(2,1)S(1)}, bf16[592,384]{1,0:T(8,128)(2,1)S(1)}, u32[]{:S(2)}, u32[]{:S(2)}) collective-permute-start(bf16[592,384]{1,0:T(8,128)(2,1)S(1)} %copy-done.18), channel_id=1, source_target_pairs={{0,16},{8,24},{16,0},{24,8},{1,17},{9,25},{17,1},{25,9},{2,18},{10... | collective-permute-start | bytes 1363976 | tf_op jit(solution)/shard_map/ppermute | solution.py:37
  87.4 14.4 %collective-permute-done.10.refs_1_ = bf16[592,384]{1,0:T(8,128)(2,1)S(1)} collective-permute-done((bf16[592,384]{1,0:T(8,128)(2,1)S(1)}, bf16[592,384]{1,0:T(8,128)(2,1)S(1)}, u32[]{:S(2)}, u32[]{:S(2)}) %collective-permute-start.10) | collective-permute-done | bytes 454688 | tf_op jit(solution)/shard_map/ppermute | solution.py:37
  101.8 1.2 collective-permute-done.9.refs_0_
  103.0 9.5 %collective-permute-done.11.refs_2_ = bf16[592,384]{1,0:T(8,128)(2,1)S(1)} collective-permute-done((bf16[592,384]{1,0:T(8,128)(2,1)S(1)}, bf16[592,384]{1,0:T(8,128)(2,1)S(1)}, u32[]{:S(2)}, u32[]{:S(2)}) %collective-permute-start.11) | collective-permute-done | bytes 454688 | tf_op jit(solution)/shard_map/ppermute | solution.py:37
  112.5 0.8 copy-done.4
  113.3 3.6 %input_grad.1 = (f32[394,192]{1,0:T(8,128)}, f32[394,192]{1,0:T(8,128)}, f32[394,192]{1,0:T(8,128)}, f32[394,192]{1,0:T(8,128)}) custom-call(s32[1]{0:T(128)} %bitcast.16.at_ref, bf16[394,192]{1,0:T(8,128)(2,1)} %get-tuple-element.23.pg_ref, bf16[768,192]{1,0:T(8,128)(2,1)} %get-tuple-element.65.refs_1_.up_ref, bf16[592,384]{1,0:T(8,128)(2,1)} %copy-done.3, ...), custom_call_target="tpu_custom_call" | custom-call | flops 464781312 | bytes 4194304 | tf_op jit(solution)/shard_map/input_grad/pallas_call | solution.py:276
  116.9 1.6 %collective-permute-start.12 = (f32[394,192]{1,0:T(8,128)}, f32[394,192]{1,0:T(8,128)S(1)}, u32[]{:S(2)}, u32[]{:S(2)}) collective-permute-start(f32[394,192]{1,0:T(8,128)} %get-tuple-element.28), channel_id=1, source_target_pairs={{0,2},{2,4},{4,6},{6,0},{1,3},{3,5},{5,7},{7,1},{8,10},{10,12},{12... | collective-permute-start | bytes 907784 | tf_op jit(solution)/shard_map/ppermute | solution.py:37
  118.5 2.9 %collective-permute-start.13 = (f32[394,192]{1,0:T(8,128)}, f32[394,192]{1,0:T(8,128)S(1)}, u32[]{:S(2)}, u32[]{:S(2)}) collective-permute-start(f32[394,192]{1,0:T(8,128)} %get-tuple-element.29), channel_id=1, source_target_pairs={{0,4},{2,6},{4,0},{6,2},{1,5},{3,7},{5,1},{7,3},{8,12},{10,14},{12... | collective-permute-start | bytes 907784 | tf_op jit(solution)/shard_map/ppermute | solution.py:37
  121.4 1.3 collective-permute-start.14
  122.7 0.3 fusion.3
  123.0 0.2 reshape.53
  123.2 0.1 copy.21
  123.4 0.1 all_gather_reshape.3
  123.5 2.0 %all_gather.3 = f32[2,2,24,768]{3,2,1,0:T(8,128)S(1)} all-gather(f32[1,2,24,768]{3,2,1,0:T(8,128)S(1)} %all_gather_reshape.3), channel_id=1, replica_groups=mesh['z'=8,'x'=4,'mp'=4,'mc'=2] {'mc'}, dimensions={0}, use_global_device_ids=true | all-gather | bytes 442368 | tf_op jit(solution)/shard_map/all_gather | solution.py:273
  125.6 0.7 broadcast_in_dim.23
  126.3 9.5 %all-to-all-start.2 = ((f32[128,1,128]{2,1,0:T(1,128)}), f32[128,1,128]{2,1,0:T(1,128)S(1)}, u32[]{:S(2)}, u32[]{:S(2)}) async-start(f32[128,1,128]{2,1,0:T(1,128)} %broadcast_in_dim.23), calls=%async_computation.2 | async-start | bytes 131072 | tf_op jit(solution)/shard_map/all_to_all | solution.py:303
  135.9 2.9 %collective-permute-done.13 = f32[394,192]{1,0:T(8,128)S(1)} collective-permute-done((f32[394,192]{1,0:T(8,128)}, f32[394,192]{1,0:T(8,128)S(1)}, u32[]{:S(2)}, u32[]{:S(2)}) %collective-permute-start.13) | collective-permute-done | bytes 302624 | tf_op jit(solution)/shard_map/ppermute | solution.py:37
  138.9 0.8 copy.23
  139.7 7.4 %all-to-all-done.2 = f32[128,1,128]{2,1,0:T(1,128)S(1)} async-done(((f32[128,1,128]{2,1,0:T(1,128)}), f32[128,1,128]{2,1,0:T(1,128)S(1)}, u32[]{:S(2)}, u32[]{:S(2)}) %all-to-all-start.2) | async-done | bytes 65568 | tf_op jit(solution)/shard_map/all_to_all | solution.py:303
  147.2 0.6 reduce_sum.39
  148.5 0.7 multiply_subtract_fusion
  (56 shorter events, 0.5 us)
Async XLA Ops:
  2.6 51.8 %all-to-all-start = ((bf16[32,24,384]{2,1,0:T(8,128)(2,1)}), bf16[32,24,384]{2,1,0:T(8,128)(2,1)S(1)}, u32[]{:S(2)}, u32[]{:S(2)}) async-start(bf16[32,24,384]{2,1,0:T(8,128)(2,1)} %bitcast.43), calls=%async_computation | async-start | bytes 1179648 | tf_op jit(solution)/shard_map/all_to_all | solution.py:238
  16.6 17.9 %collective-permute-start = (bf16[208,1152]{1,0:T(8,128)(2,1)}, bf16[208,1152]{1,0:T(8,128)(2,1)S(1)}, u32[]{:S(2)}, u32[]{:S(2)}) collective-permute-start(bf16[208,1152]{1,0:T(8,128)(2,1)} %get-tuple-element.18), channel_id=1, source_target_pairs={{0,8},{8,16},{16,24},{24,0},{1,9},{9,17},{17,25},{25,1},{2,10},{10... | collective-permute-start | bytes 1437704 | tf_op jit(solution)/shard_map/ppermute | solution.py:37
  18.0 17.9 %collective-permute-start.2 = (bf16[186,1152]{1,0:T(8,128)(2,1)}, bf16[186,1152]{1,0:T(8,128)(2,1)}, u32[]{:S(2)}, u32[]{:S(2)}) collective-permute-start(bf16[186,1152]{1,0:T(8,128)(2,1)} %get-tuple-element.19), channel_id=1, source_target_pairs={{0,24},{8,0},{16,8},{24,16},{1,25},{9,1},{17,9},{25,17},{2,26},{10... | collective-permute-start | bytes 1285640 | tf_op jit(solution)/shard_map/ppermute | solution.py:37
  18.6 27.3 %collective-permute-start.6 = (bf16[208,1152]{1,0:T(8,128)(2,1)}, bf16[208,1152]{1,0:T(8,128)(2,1)S(1)}, u32[]{:S(2)}, u32[]{:S(2)}) collective-permute-start(bf16[208,1152]{1,0:T(8,128)(2,1)} %get-tuple-element.18), channel_id=1, source_target_pairs={{0,24},{8,0},{16,8},{24,16},{1,25},{9,1},{17,9},{25,17},{2,26},{10... | collective-permute-start | bytes 1437704 | tf_op jit(solution)/shard_map/ppermute | solution.py:37
  20.0 23.9 %collective-permute-start.5 = (bf16[186,1152]{1,0:T(8,128)(2,1)}, bf16[186,1152]{1,0:T(8,128)(2,1)S(1)}, u32[]{:S(2)}, u32[]{:S(2)}) collective-permute-start(bf16[186,1152]{1,0:T(8,128)(2,1)} %get-tuple-element.19), channel_id=1, source_target_pairs={{0,8},{8,16},{16,24},{24,0},{1,9},{9,17},{17,25},{25,1},{2,10},{10... | collective-permute-start | bytes 1285640 | tf_op jit(solution)/shard_map/ppermute | solution.py:37
  34.5 12.6 %copy-start.13 = (bf16[208,1152]{1,0:T(8,128)(2,1)}, bf16[208,1152]{1,0:T(8,128)(2,1)S(1)}, u32[]{:S(2)}) copy-start(bf16[208,1152]{1,0:T(8,128)(2,1)S(1)} %collective-permute-done.refs_5_) | copy-start | bytes 1437700
  34.5 19.6 %collective-permute-start.1 = (bf16[208,1152]{1,0:T(8,128)(2,1)S(1)}, bf16[208,1152]{1,0:T(8,128)(2,1)S(1)}, u32[]{:S(2)}, u32[]{:S(2)}) collective-permute-start(bf16[208,1152]{1,0:T(8,128)(2,1)S(1)} %collective-permute-done.refs_5_), channel_id=1, source_target_pairs={{0,8},{8,16},{16,24},{24,0},{1,9},{9,17},{17,25},{25,1},{2,10},{10... | collective-permute-start | bytes 1437704 | tf_op jit(solution)/shard_map/ppermute | solution.py:37
  35.9 18.1 %collective-permute-start.3 = (bf16[186,1152]{1,0:T(8,128)(2,1)}, bf16[186,1152]{1,0:T(8,128)(2,1)S(1)}, u32[]{:S(2)}, u32[]{:S(2)}) collective-permute-start(bf16[186,1152]{1,0:T(8,128)(2,1)} %collective-permute-done.2.refs_8_), channel_id=1, source_target_pairs={{0,24},{8,0},{16,8},{24,16},{1,25},{9,1},{17,9},{25,17},{2,26},{10... | collective-permute-start | bytes 1285640 | tf_op jit(solution)/shard_map/ppermute | solution.py:37
  43.9 2.0 %copy-start.15 = (bf16[186,1152]{1,0:T(8,128)(2,1)}, bf16[186,1152]{1,0:T(8,128)(2,1)S(1)}, u32[]{:S(2)}) copy-start(bf16[186,1152]{1,0:T(8,128)(2,1)S(1)} %collective-permute-done.5.refs_6_) | copy-start | bytes 1285636
  45.9 0.8 copy-start.14
  47.1 8.4 %collective-permute-start.7 = (bf16[794,384]{1,0:T(8,128)(2,1)S(1)}, bf16[794,384]{1,0:T(8,128)(2,1)}, u32[]{:S(2)}, u32[]{:S(2)}) collective-permute-start(bf16[794,384]{1,0:T(8,128)(2,1)S(1)} %concatenate.7), channel_id=1, source_target_pairs={{0,1},{1,0},{2,3},{3,2},{4,5},{5,4},{6,7},{7,6},{8,9},{9,8},{10,11... | collective-permute-start | bytes 1829384 | tf_op jit(solution)/shard_map/ppermute | solution.py:37
  54.0 1.4 copy-start.1
  54.0 1.4 copy-start
  54.1 8.7 %collective-permute-start.4 = (bf16[394,384]{1,0:T(8,128)(2,1)S(1)}, bf16[394,384]{1,0:T(8,128)(2,1)S(1)}, u32[]{:S(2)}, u32[]{:S(2)}) collective-permute-start(bf16[394,384]{1,0:T(8,128)(2,1)S(1)} %pad_maximum_fusion), channel_id=1, source_target_pairs={{0,1},{1,0},{2,3},{3,2},{4,5},{5,4},{6,7},{7,6},{8,9},{9,8},{10,11... | collective-permute-start | bytes 907784 | tf_op jit(solution)/shard_map/ppermute | solution.py:37
  62.8 0.8 copy-start.6
  69.0 3.2 %collective-permute-start.8 = (f32[768,384]{1,0:T(8,128)}, f32[768,384]{1,0:T(8,128)S(1)}, u32[]{:S(2)}, u32[]{:S(2)}) collective-permute-start(f32[768,384]{1,0:T(8,128)} %get-tuple-element.22), channel_id=1, source_target_pairs={{0,1},{1,0},{2,3},{3,2},{4,5},{5,4},{6,7},{7,6},{8,9},{9,8},{10,11... | collective-permute-start | bytes 3538952 | tf_op jit(solution)/shard_map/ppermute | solution.py:37
  72.2 13.1 %copy-start.18 = (bf16[592,384]{1,0:T(8,128)(2,1)S(1)}, bf16[592,384]{1,0:T(8,128)(2,1)}, u32[]{:S(2)}) copy-start(bf16[592,384]{1,0:T(8,128)(2,1)} %get-tuple-element.26) | copy-start | bytes 1363972
  74.9 8.3 %copy-start.17 = (bf16[592,384]{1,0:T(8,128)(2,1)S(1)}, bf16[592,384]{1,0:T(8,128)(2,1)}, u32[]{:S(2)}) copy-start(bf16[592,384]{1,0:T(8,128)(2,1)} %get-tuple-element.25) | copy-start | bytes 1363972
  74.9 9.9 %copy-start.16 = (bf16[592,384]{1,0:T(8,128)(2,1)S(1)}, bf16[592,384]{1,0:T(8,128)(2,1)}, u32[]{:S(2)}) copy-start(bf16[592,384]{1,0:T(8,128)(2,1)} %get-tuple-element.24) | copy-start | bytes 1363972
  74.9 47.8 %all-to-all-start.1 = ((f16[32,24,384]{2,1,0:T(8,128)(2,1)}), f16[32,24,384]{2,1,0:T(8,128)(2,1)S(1)}, u32[]{:S(2)}, u32[]{:S(2)}) async-start(f16[32,24,384]{2,1,0:T(8,128)(2,1)} %bitcast.6), calls=%async_computation.1 | async-start | bytes 1179648 | tf_op jit(solution)/shard_map/all_to_all | solution.py:265
  83.2 18.5 %collective-permute-start.10 = (bf16[592,384]{1,0:T(8,128)(2,1)S(1)}, bf16[592,384]{1,0:T(8,128)(2,1)S(1)}, u32[]{:S(2)}, u32[]{:S(2)}) collective-permute-start(bf16[592,384]{1,0:T(8,128)(2,1)S(1)} %copy-done.17), channel_id=1, source_target_pairs={{0,8},{8,16},{16,24},{24,0},{1,9},{9,17},{17,25},{25,1},{2,10},{10... | collective-permute-start | bytes 1363976 | tf_op jit(solution)/shard_map/ppermute | solution.py:37
  84.8 18.2 %collective-permute-start.9 = (bf16[592,384]{1,0:T(8,128)(2,1)S(1)}, bf16[592,384]{1,0:T(8,128)(2,1)S(1)}, u32[]{:S(2)}, u32[]{:S(2)}) collective-permute-start(bf16[592,384]{1,0:T(8,128)(2,1)S(1)} %copy-done.16), channel_id=1, source_target_pairs={{0,24},{8,0},{16,8},{24,16},{1,25},{9,1},{17,9},{25,17},{2,26},{10... | collective-permute-start | bytes 1363976 | tf_op jit(solution)/shard_map/ppermute | solution.py:37
  85.3 27.2 %collective-permute-start.11 = (bf16[592,384]{1,0:T(8,128)(2,1)S(1)}, bf16[592,384]{1,0:T(8,128)(2,1)S(1)}, u32[]{:S(2)}, u32[]{:S(2)}) collective-permute-start(bf16[592,384]{1,0:T(8,128)(2,1)S(1)} %copy-done.18), channel_id=1, source_target_pairs={{0,16},{8,24},{16,0},{24,8},{1,17},{9,25},{17,1},{25,9},{2,18},{10... | collective-permute-start | bytes 1363976 | tf_op jit(solution)/shard_map/ppermute | solution.py:37
  101.8 10.7 %copy-start.2 = (bf16[592,384]{1,0:T(8,128)(2,1)}, bf16[592,384]{1,0:T(8,128)(2,1)S(1)}, u32[]{:S(2)}) copy-start(bf16[592,384]{1,0:T(8,128)(2,1)S(1)} %collective-permute-done.10.refs_1_) | copy-start | bytes 1363972
  103.0 9.5 %copy-start.3 = (bf16[592,384]{1,0:T(8,128)(2,1)}, bf16[592,384]{1,0:T(8,128)(2,1)S(1)}, u32[]{:S(2)}) copy-start(bf16[592,384]{1,0:T(8,128)(2,1)S(1)} %collective-permute-done.9.refs_0_) | copy-start | bytes 1363972
  112.5 0.8 copy-start.4
  116.9 8.6 %copy-start.7 = (f32[24,768]{1,0:T(8,128)S(1)}, f32[24,768]{1,0:T(8,128)}, u32[]{:S(2)}) copy-start(f32[24,768]{1,0:T(8,128)} %pu_ref.1) | copy-start | bytes 221188
  116.9 8.6 %copy-start.8 = (f32[24,768]{1,0:T(8,128)S(1)}, f32[24,768]{1,0:T(8,128)}, u32[]{:S(2)}) copy-start(f32[24,768]{1,0:T(8,128)} %pd_ref.1) | copy-start | bytes 221188
  116.9 19.0 %collective-permute-start.12 = (f32[394,192]{1,0:T(8,128)}, f32[394,192]{1,0:T(8,128)S(1)}, u32[]{:S(2)}, u32[]{:S(2)}) collective-permute-start(f32[394,192]{1,0:T(8,128)} %get-tuple-element.28), channel_id=1, source_target_pairs={{0,2},{2,4},{4,6},{6,0},{1,3},{3,5},{5,7},{7,1},{8,10},{10,12},{12... | collective-permute-start | bytes 907784 | tf_op jit(solution)/shard_map/ppermute | solution.py:37
  118.5 20.3 %collective-permute-start.13 = (f32[394,192]{1,0:T(8,128)}, f32[394,192]{1,0:T(8,128)S(1)}, u32[]{:S(2)}, u32[]{:S(2)}) collective-permute-start(f32[394,192]{1,0:T(8,128)} %get-tuple-element.29), channel_id=1, source_target_pairs={{0,4},{2,6},{4,0},{6,2},{1,5},{3,7},{5,1},{7,3},{8,12},{10,14},{12... | collective-permute-start | bytes 907784 | tf_op jit(solution)/shard_map/ppermute | solution.py:37
  121.4 17.4 %collective-permute-start.14 = (f32[394,192]{1,0:T(8,128)}, f32[394,192]{1,0:T(8,128)S(1)}, u32[]{:S(2)}, u32[]{:S(2)}) collective-permute-start(f32[394,192]{1,0:T(8,128)} %get-tuple-element.30), channel_id=1, source_target_pairs={{0,6},{2,0},{4,2},{6,4},{1,7},{3,1},{5,3},{7,5},{8,14},{10,8},{12,... | collective-permute-start | bytes 907784 | tf_op jit(solution)/shard_map/ppermute | solution.py:37
  123.0 15.8 %copy-start.5 = (f32[394,192]{1,0:T(8,128)S(1)}, f32[394,192]{1,0:T(8,128)}, u32[]{:S(2)}) copy-start(f32[394,192]{1,0:T(8,128)} %get-tuple-element.27) | copy-start | bytes 907780
  125.6 22.9 %copy-start.11 = (f32[24,768]{1,0:T(8,128)}, f32[24,768]{1,0:T(8,128)S(1)}, u32[]{:S(2)}) copy-start(f32[24,768]{1,0:T(8,128)S(1)} %get-tuple-element.62) | copy-start | bytes 221188
  125.6 22.9 %copy-start.12 = (f32[24,768]{1,0:T(8,128)}, f32[24,768]{1,0:T(8,128)S(1)}, u32[]{:S(2)}) copy-start(f32[24,768]{1,0:T(8,128)S(1)} %get-tuple-element.63) | copy-start | bytes 221188
  126.3 20.9 %all-to-all-start.2 = ((f32[128,1,128]{2,1,0:T(1,128)}), f32[128,1,128]{2,1,0:T(1,128)S(1)}, u32[]{:S(2)}, u32[]{:S(2)}) async-start(f32[128,1,128]{2,1,0:T(1,128)} %broadcast_in_dim.23), calls=%async_computation.2 | async-start | bytes 131072 | tf_op jit(solution)/shard_map/all_to_all | solution.py:303
  135.9 12.7 %copy-start.9 = (f32[24,768]{1,0:T(8,128)S(1)}, f32[24,768]{1,0:T(8,128)}, u32[]{:S(2)}) copy-start(f32[24,768]{1,0:T(8,128)} %md_ref.1) | copy-start | bytes 221188
  135.9 12.7 %copy-start.10 = (f32[24,768]{1,0:T(8,128)S(1)}, f32[24,768]{1,0:T(8,128)}, u32[]{:S(2)}) copy-start(f32[24,768]{1,0:T(8,128)} %mu_ref.1) | copy-start | bytes 221188
where the time goes:
time: 150 us; the launch traced here: 149 us
  waiting for transfers between devices  66.9 us (45%)
  starting transfers between devices  46.7 us (31%)
  Pallas kernels  20.8 us (14%)
  local copies, waits for them, and re-layouts  6.69 us (4%)
  other arithmetic  4.57 us (3%)
  blocking collectives  2.01 us (1%)
  between operations  1.65 us (1%)
    ppermute x15, waiting for transfers between devices, shift(): return lax.ppermute(value, axis, [(i, (i + k) % n) for i in range(n)])  59.4 us
    ppermute x15, starting transfers between devices, shift(): return lax.ppermute(value, axis, [(i, (i + k) % n) for i in range(n)])  17.2 us
    pallas_call x2, Pallas kernels, run_groups(): pl.pallas_call(lambda *refs: groups_kernel(*refs, swapped=swapped, last=l...  12.8 us
    all_to_all x1, starting transfers between devices, shards(): lax.all_to_all(payload.reshape(nz * nx, rows, 2 * wide), DP, 0, 0, tiled=...  11.6 us
    all_to_all x1, starting transfers between devices, shards(): lax.all_to_all(jnp.broadcast_to(local, (group, 1, 128)), ZXY, 0, 0, tiled...  9.55 us
    all_to_all x1, starting transfers between devices, shards(): lax.all_to_all(packed.reshape(nz * nx, rows, 2 * wide), DP, 0, 0, tiled=T...  8.29 us
    all_to_all x1, waiting for transfers between devices, shards(): lax.all_to_all(jnp.broadcast_to(local, (group, 1, 128)), ZXY, 0, 0, tiled...  7.44 us
    pallas_call x1, Pallas kernels, shards(): pl.pallas_call(input_kernel, out_shape=[tile] * ny, in_specs=[SMEM] + [VM...  3.64 us
  transfers between devices with their start and end apart: 18, of which 10 were waited for; matrix products, arithmetic and copies ran while one was open for 3% of the time, Pallas kernels for 9%

commit v1 on v0

--- a/solution.py
+++ b/solution.py
@@ -37,8 +37,14 @@
     return lax.ppermute(value, axis, [(i, (i + k) % n) for i in range(n)])
 
 
-def sample_kernel(mu_ref, pu_ref, nu_ref, md_ref, pd_ref, nd_ref, out_ref):
-    nz, nx, _, width = out_ref.shape
+def prepare_kernel(
+    core_ref, f_ref, c_ref, mu_ref, pu_ref, nu_ref, md_ref, pd_ref, nd_ref, head_ref, tail_ref, w_ref
+):
+    first = core_ref[0] == 0
+    for out, cut in ((head_ref, slice(0, HEAD)), (tail_ref, slice(HEAD, ROWS))):
+        out[:, 0:HALF] = jnp.where(first, f_ref[cut, 0:HALF], f_ref[cut, HALF:D])
+        out[:, HALF:] = c_ref[cut, :]
+    nz, nx, _, width = w_ref.shape
 
     def drawn(m, p, n):
         spread = 1.0 / jnp.sqrt(tempering * (p[...] + damping))
@@ -50,14 +56,7 @@
         cut = slice(i * wide, (i + 1) * wide)
         both = jnp.concatenate([up[:, cut], down[:, cut]], axis=1).astype(jnp.bfloat16)
         for k in range(nz):
-            out_ref[k, i] = both
-
-
-def stage_kernel(core_ref, f_ref, c_ref, head_ref, tail_ref):
-    first = core_ref[0] == 0
-    for out, cut in ((head_ref, slice(0, HEAD)), (tail_ref, slice(HEAD, ROWS))):
-        out[:, 0:HALF] = jnp.where(first, f_ref[cut, 0:HALF], f_ref[cut, HALF:D])
-        out[:, HALF:] = c_ref[cut, :]
+            w_ref[k, i] = both
 
 
 def dot_rows(left, right):
@@ -66,19 +65,26 @@
     )
 
 
+def gather_kernel(*refs):
+    at = 0
+    for ref in refs[:-1]:
+        refs[-1][at : at + ref.shape[0], :] = ref[:, 0:HALF]
+        at += -(-ref.shape[0] // 16) * 16
+
+
 def pack_lanes(value, rows):
     return jnp.concatenate([value[:rows], value[value.shape[0] - rows :]], axis=1)
 
 
-def groups_kernel(core_ref, wu_ref, wd_ref, *refs, swapped, last):
+def groups_kernel(core_ref, w_ref, *refs, swapped, last):
     core = core_ref[0]
     if last:
         u0, u1, near, acc_in = refs[:4]
-        mine_ref, other_ref, parcel, f_s, c_s, acc = refs[4:]
+        mine_ref, other_ref, parcel, f_s, c_s, wd_ref, acc = refs[4:]
         pairs = [(u0, u1, swapped[0], parcel)]
     else:
         f_ref, c_ref, r0, r1, l0, l1, near = refs[:7]
-        acc, pg_ref, parcel_r, parcel_l, f_s, c_s = refs[7:]
+        acc, pg_ref, parcel_r, parcel_l, f_s, c_s, wd_ref = refs[7:]
         acc_in = None
         pairs = [
             (None, None, None, pg_ref),
@@ -86,7 +92,8 @@
             (l0, l1, swapped[1], parcel_l),
         ]
     up_at, down_at = core, 1 - core
-    wide = wu_ref.shape[1]
+    wide = w_ref.shape[1] // 2
+    wd_ref[...] = w_ref[:, wide:]
     row = lax.broadcasted_iota(jnp.int32, (HEAD, wide), 0)
     f_s[FULL - 16 : FULL, :] = jnp.zeros((16, D), jnp.bfloat16)
     c_s[FULL - 16 : FULL, :] = jnp.zeros((16, D), jnp.bfloat16)
@@ -106,7 +113,7 @@
         preact = sum(
             jnp.dot(
                 f_s[:, i * HALF : (i + 1) * HALF],
-                wu_ref[pl.ds(at[i], HALF), :],
+                w_ref[pl.ds(at[i], HALF), 0:wide],
                 preferred_element_type=jnp.float32,
             )
             for i in range(2)
@@ -119,7 +126,7 @@
         if u0 is None:
             out[...] = pg[:ROWS]
         else:
-            out[0:HALF, :] = pack_lanes(wu_ref[...], HALF)
+            out[0:HALF, :] = pack_lanes(w_ref[:, 0:wide], HALF)
             out[HALF:, :] = pack_lanes(pg, HEAD)
         zero = jnp.zeros((), jnp.bfloat16)
         cuts = (slice(0, HEAD), slice(FULL - HEAD, FULL))
@@ -150,37 +157,53 @@
         other_ref[...] = acc[1]
 
 
-def run_groups(core, w_up, w_down, ins, swapped, last):
-    wide = w_up.shape[1]
-    sums = jax.ShapeDtypeStruct((D, 2 * wide), jnp.float32)
-    parcel = jax.ShapeDtypeStruct((HALF + HEAD, 2 * wide), jnp.bfloat16)
+def inside(array):
+    return pltpu.with_memory_space_constraint(array, pltpu.VMEM)
+
+
+def gathered(parts):
+    return pl.pallas_call(
+        gather_kernel,
+        out_shape=pltpu.VMEM((sum(-(-p.shape[0] // 16) * 16 for p in parts), HALF), jnp.bfloat16),
+        in_specs=[VMEM] * len(parts),
+        out_specs=VMEM,
+        compiler_params=pltpu.CompilerParams(vmem_limit_bytes=4 << 20),
+    )(*map(inside, parts))
+
+
+def run_groups(core, weights, ins, swapped, last):
+    wide = weights.shape[1] // 2
+    sums = pltpu.VMEM((D, 2 * wide), jnp.float32)
+    parcel = pltpu.VMEM((HALF + HEAD, 2 * wide), jnp.bfloat16)
     pair = pltpu.VMEM((FULL, D), jnp.bfloat16)
+    scratch = [pair, pair, pltpu.VMEM((D, wide), jnp.bfloat16)]
     if last:
-        out_shape, scratch = [sums, sums, parcel], [pltpu.VMEM((2, D, 2 * wide), jnp.float32)]
+        out_shape = [sums, sums, parcel]
+        scratch.append(pltpu.VMEM((2, D, 2 * wide), jnp.float32))
     else:
         out_shape = [
-            jax.ShapeDtypeStruct((2, D, 2 * wide), jnp.float32),
-            jax.ShapeDtypeStruct((ROWS, wide), jnp.bfloat16),
+            pltpu.VMEM((2, D, 2 * wide), jnp.float32),
+            pltpu.VMEM((ROWS, wide), jnp.bfloat16),
             parcel,
             parcel,
         ]
-        scratch = []
     groups = 1 if last else 3
     return pl.pallas_call(
         lambda *refs: groups_kernel(*refs, swapped=swapped, last=last),
         out_shape=out_shape,
-        in_specs=[SMEM] + [VMEM] * (len(ins) + 2),
+        in_specs=[SMEM] + [VMEM] * (len(ins) + 1),
         out_specs=[VMEM] * len(out_shape),
-        scratch_shapes=[pair, pair] + scratch,
+        scratch_shapes=scratch,
+        compiler_params=pltpu.CompilerParams(vmem_limit_bytes=24 << 20),
         cost_estimate=pl.CostEstimate(
             flops=groups * ROWS * D * wide * 8,
             transcendentals=2 * groups * ROWS * wide,
             bytes_accessed=6 << 20,
         ),
-    )(core, w_up, w_down, *ins)
-
-
-def input_kernel(at_ref, pg_ref, up_ref, *refs):
+    )(core, inside(weights), *[inside(a) for a in ins])
+
+
+def input_kernel(at_ref, pg_ref, w_ref, *refs):
     parcels, outs, (up_s, pg_s) = refs[:3], refs[3:-2], refs[-2:]
     wide = pg_ref.shape[1]
     for i, parcel in enumerate(parcels):
@@ -197,7 +220,7 @@
                 left, right, (((1,), (1,)), ((), ())), preferred_element_type=jnp.float32
             )
 
-        value = product(pg_ref[...], up_ref[span, :])
+        value = product(pg_ref[...], w_ref[span, 0:wide])
         for i in range(len(parcels)):
             value = value + product(pg_s[i, 0:ROWS], up_s[i, span, :])
         out[...] = value
@@ -213,48 +236,50 @@
     core_at = core.reshape(1)
     cotangent = out_cotangent[0]
 
-    u0, u1 = pl.pallas_call(
-        stage_kernel,
+    u0, u1, payload = pl.pallas_call(
+        prepare_kernel,
         out_shape=[
-            jax.ShapeDtypeStruct((HEAD, HALF + D), jnp.bfloat16),
-            jax.ShapeDtypeStruct((TAIL, HALF + D), jnp.bfloat16),
+            pltpu.VMEM((HEAD, HALF + D), jnp.bfloat16),
+            pltpu.VMEM((TAIL, HALF + D), jnp.bfloat16),
+            pltpu.VMEM((nz, nx, rows, 2 * wide), jnp.bfloat16),
         ],
-        in_specs=[SMEM, VMEM, VMEM],
-        out_specs=[VMEM, VMEM],
-        name="stage",
-    )(core_at, features, cotangent)
+        in_specs=[SMEM] + [VMEM] * 8,
+        out_specs=[VMEM] * 3,
+        compiler_params=pltpu.CompilerParams(vmem_limit_bytes=16 << 20),
+        name="prepare",
+    )(
+        core_at,
+        *[
+            pltpu.with_memory_space_constraint(a, pltpu.HBM)
+            for a in (
+                features, cotangent, mean_up, precision_up, noise_up[0],
+                mean_down, precision_down, noise_down[0],
+            )
+        ],
+    )
     r0 = shift(u0, "x", 1)
     l1 = shift(u1, "x", -1)
     r1 = shift(u1, "x", 1)
     l0 = shift(u0, "x", -1)
 
-    payload = pl.pallas_call(
-        sample_kernel,
-        out_shape=jax.ShapeDtypeStruct((nz, nx, rows, 2 * wide), jnp.bfloat16),
-        in_specs=[VMEM] * 6,
-        out_specs=VMEM,
-        name="sample",
-    )(mean_up, precision_up, noise_up[0], mean_down, precision_down, noise_down[0])
     weights = lax.all_to_all(
         payload.reshape(nz * nx, rows, 2 * wide), DP, 0, 0, tiled=True
     ).reshape(D, 2 * wide)
-    w_up, w_down = weights[:, :wide], weights[:, wide:]
 
     f0 = shift(r0, "x", 1)
     f1 = shift(l1, "x", -1)
-    gap = jnp.zeros((FULL - HEAD - TAIL, HALF), jnp.bfloat16)
-    near = jnp.concatenate([r0[:, :HALF], l0[:, :HALF], r1[:, :HALF], gap, l1[:, :HALF]])
+    near = gathered([r0, l0, r1, l1])
     near = shift(near, "mc", 1)
     spots = ((0, 2 * HEAD), (HEAD, HEAD + FULL))
-    far = shift(jnp.concatenate([f0[:, :HALF], f1[:, :HALF]]), "mc", 1)
+    far = shift(gathered([f0, f1]), "mc", 1)
 
     acc, pg, parcel_r, parcel_l = run_groups(
-        core_at, w_up, w_down, [features, cotangent, r0, r1, l0, l1, near], spots, False
+        core_at, weights, [features, cotangent, r0, r1, l0, l1, near], spots, False
     )
     parcel_r = shift(parcel_r, "x", -1)
     parcel_l = shift(parcel_l, "x", 1)
     mine, other, parcel_f = run_groups(
-        core_at, w_up, w_down, [f0, f1, far, acc], ((0, HEAD),), True
+        core_at, weights, [f0, f1, far, acc], ((0, HEAD),), True
     )
 
     both = mine + shift(other, "mc", 1)
@@ -272,7 +297,7 @@
     total = jnp.transpose(total, (2, 1, 0, 3)).reshape(2, rows, cols)
     totals = lax.all_gather(total, "mc", axis=0)
 
-    tile = jax.ShapeDtypeStruct((ROWS, D // ny), jnp.float32)
+    tile = pltpu.VMEM((ROWS, D // ny), jnp.float32)
     tiles = pl.pallas_call(
         input_kernel,
         out_shape=[tile] * ny,
@@ -282,11 +307,12 @@
             pltpu.VMEM((3, D, wide), jnp.bfloat16),
             pltpu.VMEM((3, FULL, wide), jnp.bfloat16),
         ],
+        compiler_params=pltpu.CompilerParams(vmem_limit_bytes=16 << 20),
         cost_estimate=pl.CostEstimate(
             flops=ROWS * D * cols * 2, transcendentals=0, bytes_accessed=4 << 20
         ),
         name="input_grad",
-    )(lax.axis_index("mp").astype(jnp.int32).reshape(1), pg, w_up, parcel_r, parcel_l, parcel_f)
+    )(lax.axis_index("mp").astype(jnp.int32).reshape(1), *map(inside, (pg, weights, parcel_r, parcel_l, parcel_f)))
     tiles = [tiles[0]] + [shift(tiles[k], "mp", k) for k in range(1, ny)]
     input_grad = sum(tiles[1:], tiles[0]).astype(jnp.bfloat16)[None]
 

time: 150 us -> 152 us (1.013)
  Pallas kernels: 20.8 us -> 11.2 us
  waiting for transfers between devices: 66.9 us -> 71.7 us
  local copies, waits for them, and re-layouts: 6.69 us -> 10.9 us
  starting transfers between devices: 46.7 us -> 49.2 us
    unnamed x39 -> x47, local copies, waits for them, and re-layouts: 3.12 us -> 9.79 us
    pallas_call x2, Pallas kernels: 12.8 us -> 6.68 us  [run_groups(): pl.pallas_call(lambda *refs: groups_kernel(*refs, swapped=swapped, last=l...]
    ppermute x15, waiting for transfers between devices: 59.4 us -> 63 us  [shift(): return lax.ppermute(value, axis, [(i, (i + k) % n) for i in range(n)])]
    slice x7 -> x0, local copies, waits for them, and re-layouts: 2.06 us -> none  [the longest x1 1.02 us: shards(): w_up, w_down = (weights[:, :wide], weights[:, wide:])]
    pallas_call x2 -> x3, Pallas kernels: 4.3 us -> 2.51 us  [the longest x1 2.43 us: shards(): pl.pallas_call(prepare_kernel, out_shape=[pltpu.VMEM((HEAD, HALF + D), jn...]
    pallas_call x1, Pallas kernels: 3.64 us -> 2.03 us  [shards(): pl.pallas_call(input_kernel, out_shape=[tile] * ny, in_specs=[SMEM] + [VM...]
  transfers between devices with their start and end apart: 18 -> 18, of which waited for: 10 -> 9; matrix products, arithmetic and copies ran while one was open for 3% -> 2% of each run, Pallas kernels for 9% -> 4%
where the time goes in v1:
time: 152 us; the launch traced here: 151 us
  waiting for transfers between devices  71.7 us (47%)
  starting transfers between devices  49.2 us (32%)
  Pallas kernels  11.2 us (7%)
  local copies, waits for them, and re-layouts  10.9 us (7%)
  other arithmetic  4.3 us (3%)
  blocking collectives  2.01 us (1%)
  between operations  1.62 us (1%)
    ppermute x15, waiting for transfers between devices, shift(): return lax.ppermute(value, axis, [(i, (i + k) % n) for i in range(n)])  63 us
    ppermute x15, starting transfers between devices, shift(): return lax.ppermute(value, axis, [(i, (i + k) % n) for i in range(n)])  18.2 us
    all_to_all x1, starting transfers between devices, shards(): lax.all_to_all(payload.reshape(nz * nx, rows, 2 * wide), DP, 0, 0, tiled=...  11.6 us
    all_to_all x1, starting transfers between devices, shards(): lax.all_to_all(packed.reshape(nz * nx, rows, 2 * wide), DP, 0, 0, tiled=T...  9.81 us
    unnamed x47, local copies, waits for them, and re-layouts  9.79 us
    all_to_all x1, starting transfers between devices, shards(): lax.all_to_all(jnp.broadcast_to(local, (group, 1, 128)), ZXY, 0, 0, tiled...  9.51 us
    all_to_all x1, waiting for transfers between devices, shards(): lax.all_to_all(jnp.broadcast_to(local, (group, 1, 128)), ZXY, 0, 0, tiled...  8.72 us
    pallas_call x2, Pallas kernels, run_groups(): pl.pallas_call(lambda *refs: groups_kernel(*refs, swapped=swapped, last=l...  6.68 us
  transfers between devices with their start and end apart: 18, of which 9 were waited for; matrix products, arithmetic and copies ran while one was open for 2% of the time, Pallas kernels for 4%

profile of v1, /device:TPU:2, one launch (start us, length us, event | category | flops | bytes accessed | tf_op | source)
XLA Modules:
  0.0 150.9 jit_solution(16753567269790659025)
XLA Ops:
  0.6 2.4 %prepare.1 = (bf16[208,1152]{1,0:T(8,128)(2,1)S(1)}, bf16[186,1152]{1,0:T(8,128)(2,1)S(1)}, bf16[8,4,24,384]{3,2,1,0:T(8,128)(2,1)}) custom-call(s32[1]{0:T(128)} %bitcast.core_ref.refs_0_, bf16[394,768]{1,0:T(8,128)(2,1)} %refs_2_.1, bf16[394,768]{1,0:T(8,128)(2,1)} %bitcast.45, f32[24,768]{1,0:T(8,128)} %mu_ref.1, f32[24,768]{1,0:T(8,128)} %pu_ref.1, ...), custom_call_target="tpu_custom_call" | custom-call | tf_op jit(solution)/shard_map/prepare/pallas_call | solution.py:239
  3.1 11.6 %all-to-all-start = ((bf16[32,24,384]{2,1,0:T(8,128)(2,1)}), bf16[32,24,384]{2,1,0:T(8,128)(2,1)S(1)}, u32[]{:S(2)}, u32[]{:S(2)}) async-start(bf16[32,24,384]{2,1,0:T(8,128)(2,1)} %bitcast.4), calls=%async_computation | async-start | bytes 1179648 | tf_op jit(solution)/shard_map/all_to_all | solution.py:265
  14.7 1.5 %collective-permute-start = (bf16[208,1152]{1,0:T(8,128)(2,1)S(1)}, bf16[208,1152]{1,0:T(8,128)(2,1)S(1)}, u32[]{:S(2)}, u32[]{:S(2)}) collective-permute-start(bf16[208,1152]{1,0:T(8,128)(2,1)S(1)} %get-tuple-element.20), channel_id=1, source_target_pairs={{0,8},{8,16},{16,24},{24,0},{1,9},{9,17},{17,25},{25,1},{2,10},{10... | collective-permute-start | bytes 1437704 | tf_op jit(solution)/shard_map/ppermute | solution.py:37
  16.2 0.6 collective-permute-start.6
  16.8 1.4 collective-permute-start.2
  18.2 0.6 collective-permute-start.5
  18.8 14.7 %collective-permute-done.refs_0_.refs_4_ = bf16[208,1152]{1,0:T(8,128)(2,1)S(1)} collective-permute-done((bf16[208,1152]{1,0:T(8,128)(2,1)S(1)}, bf16[208,1152]{1,0:T(8,128)(2,1)S(1)}, u32[]{:S(2)}, u32[]{:S(2)}) %collective-permute-start) | collective-permute-done | bytes 479264 | tf_op jit(solution)/shard_map/ppermute | solution.py:37
  33.5 1.5 collective-permute-start.1
  35.0 8.4 %collective-permute-done.2.refs_3_.refs_7_ = bf16[186,1152]{1,0:T(8,128)(2,1)S(1)} collective-permute-done((bf16[186,1152]{1,0:T(8,128)(2,1)S(1)}, bf16[186,1152]{1,0:T(8,128)(2,1)S(1)}, u32[]{:S(2)}, u32[]{:S(2)}) %collective-permute-start.2) | collective-permute-done | bytes 428576 | tf_op jit(solution)/shard_map/ppermute | solution.py:37
  43.6 0.7 copy-done.6
  44.6 1.9 %collective-permute-start.3 = (bf16[186,1152]{1,0:T(8,128)(2,1)S(1)}, bf16[186,1152]{1,0:T(8,128)(2,1)S(1)}, u32[]{:S(2)}, u32[]{:S(2)}) collective-permute-start(bf16[186,1152]{1,0:T(8,128)(2,1)S(1)} %collective-permute-done.2.refs_3_.refs_7_), channel_id=1, source_target_pairs={{0,24},{8,0},{16,8},{24,16},{1,25},{9,1},{17,9},{25,17},{2,26},{10... | collective-permute-start | bytes 1285640 | tf_op jit(solution)/shard_map/ppermute | solution.py:37
  46.5 10.6 %collective-permute-done.3.refs_1_.refs_3_ = bf16[186,1152]{1,0:T(8,128)(2,1)S(1)} collective-permute-done((bf16[186,1152]{1,0:T(8,128)(2,1)S(1)}, bf16[186,1152]{1,0:T(8,128)(2,1)S(1)}, u32[]{:S(2)}, u32[]{:S(2)}) %collective-permute-start.3) | collective-permute-done | bytes 428576 | tf_op jit(solution)/shard_map/ppermute | solution.py:37
  57.1 0.3 collective-permute-start.4
  57.4 0.8 copy-done.10
  58.2 1.0 copy-done.3
  59.2 1.0 copy-done.5
  60.3 1.0 copy-done.7
  61.3 1.1 copy-done.11
  62.3 4.0 %shard_map.121 = (f32[2,768,384]{2,1,0:T(8,128)S(1)}, bf16[394,192]{1,0:T(8,128)(2,1)S(1)}, bf16[592,384]{1,0:T(8,128)(2,1)S(1)}, bf16[592,384]{1,0:T(8,128)(2,1)S(1)}) custom-call(s32[1]{0:T(128)} %bitcast.core_ref.refs_0_, bf16[768,384]{1,0:T(8,128)(2,1)S(1)} %bitcast.42, bf16[394,768]{1,0:T(8,128)(2,1)S(1)} %copy-done, bf16[394,768]{1,0:T(8,128)(2,1)S(1)} %bitcast.46, ...), custom_call_target="tpu_custom_call" | custom-call | flops 1394343936 | bytes 6291456 | tf_op jit(solution)/shard_map/pallas_call | solution.py:191
  66.4 0.7 copy-done.8
  67.1 0.8 copy-done.12
  67.8 0.8 copy-done.14
  68.6 2.6 %shard_map.122 = (f32[768,384]{1,0:T(8,128)S(1)}, f32[768,384]{1,0:T(8,128)S(1)}, bf16[592,384]{1,0:T(8,128)(2,1)S(1)}) custom-call(s32[1]{0:T(128)} %bitcast.core_ref.refs_0_, bf16[768,384]{1,0:T(8,128)(2,1)S(1)} %bitcast.43, bf16[208,1152]{1,0:T(8,128)(2,1)S(1)} %collective-permute-done.1.refs_0_.refs_2_, ...), custom_call_target="tpu_custom_call" | custom-call | flops 464781312 | bytes 6291456 | tf_op jit(solution)/shard_map/pallas_call | solution.py:191
  71.3 0.8 copy-done.16
  72.1 0.5 collective-permute-start.8
  72.5 2.5 %collective-permute-done.8 = f32[768,384]{1,0:T(8,128)S(1)} collective-permute-done((f32[768,384]{1,0:T(8,128)S(1)}, f32[768,384]{1,0:T(8,128)S(1)}, u32[]{:S(2)}, u32[]{:S(2)}) %collective-permute-start.8) | collective-permute-done | bytes 1179680 | tf_op jit(solution)/shard_map/ppermute | solution.py:37
  75.0 1.4 fusion
  76.4 9.8 %all-to-all-start.1 = ((f16[32,24,384]{2,1,0:T(8,128)(2,1)}), f16[32,24,384]{2,1,0:T(8,128)(2,1)}, u32[]{:S(2)}, u32[]{:S(2)}) async-start(f16[32,24,384]{2,1,0:T(8,128)(2,1)} %bitcast.6), calls=%async_computation.1 | async-start | bytes 1179648 | tf_op jit(solution)/shard_map/all_to_all | solution.py:290
  86.2 1.5 %collective-permute-start.10 = (bf16[592,384]{1,0:T(8,128)(2,1)S(1)}, bf16[592,384]{1,0:T(8,128)(2,1)S(1)}, u32[]{:S(2)}, u32[]{:S(2)}) collective-permute-start(bf16[592,384]{1,0:T(8,128)(2,1)S(1)} %copy-done.15), channel_id=1, source_target_pairs={{0,8},{8,16},{16,24},{24,0},{1,9},{9,17},{17,25},{25,1},{2,10},{10... | collective-permute-start | bytes 1363976 | tf_op jit(solution)/shard_map/ppermute | solution.py:37
  87.8 0.6 collective-permute-start.9
  88.4 2.1 %collective-permute-start.11 = (bf16[592,384]{1,0:T(8,128)(2,1)}, bf16[592,384]{1,0:T(8,128)(2,1)S(1)}, u32[]{:S(2)}, u32[]{:S(2)}) collective-permute-start(bf16[592,384]{1,0:T(8,128)(2,1)} %copy-done.16), channel_id=1, source_target_pairs={{0,16},{8,24},{16,0},{24,8},{1,17},{9,25},{17,1},{25,9},{2,18},{10... | collective-permute-start | bytes 1363976 | tf_op jit(solution)/shard_map/ppermute | solution.py:37
  90.4 14.4 %collective-permute-done.10.refs_1_ = bf16[592,384]{1,0:T(8,128)(2,1)S(1)} collective-permute-done((bf16[592,384]{1,0:T(8,128)(2,1)S(1)}, bf16[592,384]{1,0:T(8,128)(2,1)S(1)}, u32[]{:S(2)}, u32[]{:S(2)}) %collective-permute-start.10) | collective-permute-done | bytes 454688 | tf_op jit(solution)/shard_map/ppermute | solution.py:37
  104.8 1.2 collective-permute-done.9.refs_0_
  106.0 9.5 %collective-permute-done.11.refs_2_ = bf16[592,384]{1,0:T(8,128)(2,1)S(1)} collective-permute-done((bf16[592,384]{1,0:T(8,128)(2,1)}, bf16[592,384]{1,0:T(8,128)(2,1)S(1)}, u32[]{:S(2)}, u32[]{:S(2)}) %collective-permute-start.11) | collective-permute-done | bytes 454688 | tf_op jit(solution)/shard_map/ppermute | solution.py:37
  115.5 2.0 %input_grad.1 = (f32[394,192]{1,0:T(8,128)S(1)}, f32[394,192]{1,0:T(8,128)S(1)}, f32[394,192]{1,0:T(8,128)S(1)}, f32[394,192]{1,0:T(8,128)}) custom-call(s32[1]{0:T(128)} %bitcast.16.at_ref, bf16[394,192]{1,0:T(8,128)(2,1)S(1)} %copy-done.9, bf16[768,384]{1,0:T(8,128)(2,1)S(1)} %bitcast.44, bf16[592,384]{1,0:T(8,128)(2,1)S(1)} %collective-permute-done.9.refs_0_, ...), custom_call_target="tpu_custom_call" | custom-call | flops 464781312 | bytes 4194304 | tf_op jit(solution)/shard_map/input_grad/pallas_call | solution.py:301
  117.6 1.6 %collective-permute-start.12 = (f32[394,192]{1,0:T(8,128)S(1)}, f32[394,192]{1,0:T(8,128)S(1)}, u32[]{:S(2)}, u32[]{:S(2)}) collective-permute-start(f32[394,192]{1,0:T(8,128)S(1)} %get-tuple-element.30), channel_id=1, source_target_pairs={{0,2},{2,4},{4,6},{6,0},{1,3},{3,5},{5,7},{7,1},{8,10},{10,12},{12... | collective-permute-start | bytes 907784 | tf_op jit(solution)/shard_map/ppermute | solution.py:37
  119.1 2.9 %collective-permute-start.13 = (f32[394,192]{1,0:T(8,128)S(1)}, f32[394,192]{1,0:T(8,128)S(1)}, u32[]{:S(2)}, u32[]{:S(2)}) collective-permute-start(f32[394,192]{1,0:T(8,128)S(1)} %get-tuple-element.31), channel_id=1, source_target_pairs={{0,4},{2,6},{4,0},{6,2},{1,5},{3,7},{5,1},{7,3},{8,12},{10,14},{12... | collective-permute-start | bytes 907784 | tf_op jit(solution)/shard_map/ppermute | solution.py:37
  122.0 1.3 collective-permute-start.14
  123.4 1.4 fusion.3
  124.8 0.2 reshape.53
  125.2 2.0 %all_gather.3 = f32[2,2,24,768]{3,2,1,0:T(8,128)S(1)} all-gather(f32[1,2,24,768]{3,2,1,0:T(8,128)S(1)} %all_gather_reshape.3), channel_id=1, replica_groups=mesh['z'=8,'x'=4,'mp'=4,'mc'=2] {'mc'}, dimensions={0}, use_global_device_ids=true | all-gather | bytes 442368 | tf_op jit(solution)/shard_map/all_gather | solution.py:298
  127.4 0.7 broadcast_in_dim.19
  128.0 9.5 %all-to-all-start.2 = ((f32[128,1,128]{2,1,0:T(1,128)}), f32[128,1,128]{2,1,0:T(1,128)S(1)}, u32[]{:S(2)}, u32[]{:S(2)}) async-start(f32[128,1,128]{2,1,0:T(1,128)} %broadcast_in_dim.19), calls=%async_computation.2 | async-start | bytes 131072 | tf_op jit(solution)/shard_map/all_to_all | solution.py:329
  137.6 1.6 %collective-permute-done.13 = f32[394,192]{1,0:T(8,128)S(1)} collective-permute-done((f32[394,192]{1,0:T(8,128)S(1)}, f32[394,192]{1,0:T(8,128)S(1)}, u32[]{:S(2)}, u32[]{:S(2)}) %collective-permute-start.13) | collective-permute-done | bytes 302624 | tf_op jit(solution)/shard_map/ppermute | solution.py:37
  139.3 0.8 copy.23
  140.1 8.7 %all-to-all-done.2 = f32[128,1,128]{2,1,0:T(1,128)S(1)} async-done(((f32[128,1,128]{2,1,0:T(1,128)}), f32[128,1,128]{2,1,0:T(1,128)S(1)}, u32[]{:S(2)}, u32[]{:S(2)}) %all-to-all-start.2) | async-done | bytes 65568 | tf_op jit(solution)/shard_map/all_to_all | solution.py:329
  148.9 0.6 reduce_sum.39
  150.2 0.7 multiply_subtract_fusion
  (55 shorter events, 1.0 us)
Async XLA Ops:
  3.1 55.1 %all-to-all-start = ((bf16[32,24,384]{2,1,0:T(8,128)(2,1)}), bf16[32,24,384]{2,1,0:T(8,128)(2,1)S(1)}, u32[]{:S(2)}, u32[]{:S(2)}) async-start(bf16[32,24,384]{2,1,0:T(8,128)(2,1)} %bitcast.4), calls=%async_computation | async-start | bytes 1179648 | tf_op jit(solution)/shard_map/all_to_all | solution.py:265
  14.7 18.9 %collective-permute-start = (bf16[208,1152]{1,0:T(8,128)(2,1)S(1)}, bf16[208,1152]{1,0:T(8,128)(2,1)S(1)}, u32[]{:S(2)}, u32[]{:S(2)}) collective-permute-start(bf16[208,1152]{1,0:T(8,128)(2,1)S(1)} %get-tuple-element.20), channel_id=1, source_target_pairs={{0,8},{8,16},{16,24},{24,0},{1,9},{9,17},{17,25},{25,1},{2,10},{10... | collective-permute-start | bytes 1437704 | tf_op jit(solution)/shard_map/ppermute | solution.py:37
  16.2 27.3 %collective-permute-start.6 = (bf16[208,1152]{1,0:T(8,128)(2,1)S(1)}, bf16[208,1152]{1,0:T(8,128)(2,1)S(1)}, u32[]{:S(2)}, u32[]{:S(2)}) collective-permute-start(bf16[208,1152]{1,0:T(8,128)(2,1)S(1)} %get-tuple-element.20), channel_id=1, source_target_pairs={{0,24},{8,0},{16,8},{24,16},{1,25},{9,1},{17,9},{25,17},{2,26},{10... | collective-permute-start | bytes 1437704 | tf_op jit(solution)/shard_map/ppermute | solution.py:37
  16.8 26.7 %collective-permute-start.2 = (bf16[186,1152]{1,0:T(8,128)(2,1)S(1)}, bf16[186,1152]{1,0:T(8,128)(2,1)S(1)}, u32[]{:S(2)}, u32[]{:S(2)}) collective-permute-start(bf16[186,1152]{1,0:T(8,128)(2,1)S(1)} %get-tuple-element.21), channel_id=1, source_target_pairs={{0,24},{8,0},{16,8},{24,16},{1,25},{9,1},{17,9},{25,17},{2,26},{10... | collective-permute-start | bytes 1285640 | tf_op jit(solution)/shard_map/ppermute | solution.py:37
  18.2 25.3 %collective-permute-start.5 = (bf16[186,1152]{1,0:T(8,128)(2,1)S(1)}, bf16[186,1152]{1,0:T(8,128)(2,1)S(1)}, u32[]{:S(2)}, u32[]{:S(2)}) collective-permute-start(bf16[186,1152]{1,0:T(8,128)(2,1)S(1)} %get-tuple-element.21), channel_id=1, source_target_pairs={{0,8},{8,16},{16,24},{24,0},{1,9},{9,17},{17,25},{25,1},{2,10},{10... | collective-permute-start | bytes 1285640 | tf_op jit(solution)/shard_map/ppermute | solution.py:37
  33.5 23.5 %collective-permute-start.1 = (bf16[208,1152]{1,0:T(8,128)(2,1)S(1)}, bf16[208,1152]{1,0:T(8,128)(2,1)S(1)}, u32[]{:S(2)}, u32[]{:S(2)}) collective-permute-start(bf16[208,1152]{1,0:T(8,128)(2,1)S(1)} %collective-permute-done.refs_0_.refs_4_), channel_id=1, source_target_pairs={{0,8},{8,16},{16,24},{24,0},{1,9},{9,17},{17,25},{25,1},{2,10},{10... | collective-permute-start | bytes 1437704 | tf_op jit(solution)/shard_map/ppermute | solution.py:37
  43.5 1.1 copy-start.4
  43.5 0.8 copy-start.6
  43.5 1.0 copy-start.2
  44.5 13.7 %copy-start = (bf16[394,768]{1,0:T(8,128)(2,1)S(1)}, bf16[394,768]{1,0:T(8,128)(2,1)}, u32[]{:S(2)}) copy-start(bf16[394,768]{1,0:T(8,128)(2,1)} %refs_2_.1) | copy-start | bytes 1815556
  44.5 13.7 %copy-start.1 = (bf16[1,394,768]{2,1,0:T(8,128)(2,1)S(1)}, bf16[1,394,768]{2,1,0:T(8,128)(2,1)}, u32[]{:S(2)}) copy-start(bf16[1,394,768]{2,1,0:T(8,128)(2,1)} %param.9) | copy-start | bytes 1815556
  44.5 12.9 %collective-permute-start.7 = (bf16[800,384]{1,0:T(8,128)(2,1)S(1)}, bf16[800,384]{1,0:T(8,128)(2,1)S(1)}, u32[]{:S(2)}, u32[]{:S(2)}) collective-permute-start(bf16[800,384]{1,0:T(8,128)(2,1)S(1)} %shard_map.120), channel_id=1, source_target_pairs={{0,1},{1,0},{2,3},{3,2},{4,5},{5,4},{6,7},{7,6},{8,9},{9,8},{10,11... | collective-permute-start | bytes 1843208 | tf_op jit(solution)/shard_map/ppermute | solution.py:37
  44.6 12.5 %collective-permute-start.3 = (bf16[186,1152]{1,0:T(8,128)(2,1)S(1)}, bf16[186,1152]{1,0:T(8,128)(2,1)S(1)}, u32[]{:S(2)}, u32[]{:S(2)}) collective-permute-start(bf16[186,1152]{1,0:T(8,128)(2,1)S(1)} %collective-permute-done.2.refs_3_.refs_7_), channel_id=1, source_target_pairs={{0,24},{8,0},{16,8},{24,16},{1,25},{9,1},{17,9},{25,17},{2,26},{10... | collective-permute-start | bytes 1285640 | tf_op jit(solution)/shard_map/ppermute | solution.py:37
  57.1 11.5 %collective-permute-start.4 = (bf16[400,384]{1,0:T(8,128)(2,1)S(1)}, bf16[400,384]{1,0:T(8,128)(2,1)}, u32[]{:S(2)}, u32[]{:S(2)}) collective-permute-start(bf16[400,384]{1,0:T(8,128)(2,1)S(1)} %shard_map.119), channel_id=1, source_target_pairs={{0,1},{1,0},{2,3},{3,2},{4,5},{5,4},{6,7},{7,6},{8,9},{9,8},{10,11... | collective-permute-start | bytes 921608 | tf_op jit(solution)/shard_map/ppermute | solution.py:37
  57.4 0.8 copy-start.10
  58.2 1.0 copy-start.3
  59.2 1.0 copy-start.5
  60.2 1.0 copy-start.7
  61.3 1.1 copy-start.11
  66.4 0.7 copy-start.8
  67.1 0.8 copy-start.12
  67.8 0.8 copy-start.14
  71.3 0.8 copy-start.16
  72.1 3.0 %collective-permute-start.8 = (f32[768,384]{1,0:T(8,128)S(1)}, f32[768,384]{1,0:T(8,128)S(1)}, u32[]{:S(2)}, u32[]{:S(2)}) collective-permute-start(f32[768,384]{1,0:T(8,128)S(1)} %get-tuple-element.24), channel_id=1, source_target_pairs={{0,1},{1,0},{2,3},{3,2},{4,5},{5,4},{6,7},{7,6},{8,9},{9,8},{10,11... | collective-permute-start | bytes 3538952 | tf_op jit(solution)/shard_map/ppermute | solution.py:37
  76.4 9.8 %copy-start.15 = (bf16[592,384]{1,0:T(8,128)(2,1)S(1)}, bf16[592,384]{1,0:T(8,128)(2,1)}, u32[]{:S(2)}) copy-start(bf16[592,384]{1,0:T(8,128)(2,1)} %copy-done.14) | copy-start | bytes 1363972
  76.4 11.4 %copy-start.13 = (bf16[592,384]{1,0:T(8,128)(2,1)S(1)}, bf16[592,384]{1,0:T(8,128)(2,1)}, u32[]{:S(2)}) copy-start(bf16[592,384]{1,0:T(8,128)(2,1)} %copy-done.12) | copy-start | bytes 1363972
  76.4 39.1 %copy-start.9 = (bf16[394,192]{1,0:T(8,128)(2,1)S(1)}, bf16[394,192]{1,0:T(8,128)(2,1)}, u32[]{:S(2)}) copy-start(bf16[394,192]{1,0:T(8,128)(2,1)} %copy-done.8) | copy-start | bytes 453892
  76.4 47.0 %all-to-all-start.1 = ((f16[32,24,384]{2,1,0:T(8,128)(2,1)}), f16[32,24,384]{2,1,0:T(8,128)(2,1)}, u32[]{:S(2)}, u32[]{:S(2)}) async-start(f16[32,24,384]{2,1,0:T(8,128)(2,1)} %bitcast.6), calls=%async_computation.1 | async-start | bytes 1179648 | tf_op jit(solution)/shard_map/all_to_all | solution.py:290
  86.2 18.5 %collective-permute-start.10 = (bf16[592,384]{1,0:T(8,128)(2,1)S(1)}, bf16[592,384]{1,0:T(8,128)(2,1)S(1)}, u32[]{:S(2)}, u32[]{:S(2)}) collective-permute-start(bf16[592,384]{1,0:T(8,128)(2,1)S(1)} %copy-done.15), channel_id=1, source_target_pairs={{0,8},{8,16},{16,24},{24,0},{1,9},{9,17},{17,25},{25,1},{2,10},{10... | collective-permute-start | bytes 1363976 | tf_op jit(solution)/shard_map/ppermute | solution.py:37
  87.8 18.2 %collective-permute-start.9 = (bf16[592,384]{1,0:T(8,128)(2,1)S(1)}, bf16[592,384]{1,0:T(8,128)(2,1)S(1)}, u32[]{:S(2)}, u32[]{:S(2)}) collective-permute-start(bf16[592,384]{1,0:T(8,128)(2,1)S(1)} %copy-done.13), channel_id=1, source_target_pairs={{0,24},{8,0},{16,8},{24,16},{1,25},{9,1},{17,9},{25,17},{2,26},{10... | collective-permute-start | bytes 1363976 | tf_op jit(solution)/shard_map/ppermute | solution.py:37
  88.4 27.2 %collective-permute-start.11 = (bf16[592,384]{1,0:T(8,128)(2,1)}, bf16[592,384]{1,0:T(8,128)(2,1)S(1)}, u32[]{:S(2)}, u32[]{:S(2)}) collective-permute-start(bf16[592,384]{1,0:T(8,128)(2,1)} %copy-done.16), channel_id=1, source_target_pairs={{0,16},{8,24},{16,0},{24,8},{1,17},{9,25},{17,1},{25,9},{2,18},{10... | collective-permute-start | bytes 1363976 | tf_op jit(solution)/shard_map/ppermute | solution.py:37
  117.6 9.7 %copy-start.17 = (f32[24,768]{1,0:T(8,128)S(1)}, f32[24,768]{1,0:T(8,128)}, u32[]{:S(2)}) copy-start(f32[24,768]{1,0:T(8,128)} %pu_ref.1) | copy-start | bytes 221188
  117.6 9.7 %copy-start.18 = (f32[24,768]{1,0:T(8,128)S(1)}, f32[24,768]{1,0:T(8,128)}, u32[]{:S(2)}) copy-start(f32[24,768]{1,0:T(8,128)} %pd_ref.1) | copy-start | bytes 221188
  117.6 20.0 %collective-permute-start.12 = (f32[394,192]{1,0:T(8,128)S(1)}, f32[394,192]{1,0:T(8,128)S(1)}, u32[]{:S(2)}, u32[]{:S(2)}) collective-permute-start(f32[394,192]{1,0:T(8,128)S(1)} %get-tuple-element.30), channel_id=1, source_target_pairs={{0,2},{2,4},{4,6},{6,0},{1,3},{3,5},{5,7},{7,1},{8,10},{10,12},{12... | collective-permute-start | bytes 907784 | tf_op jit(solution)/shard_map/ppermute | solution.py:37
  119.1 20.1 %collective-permute-start.13 = (f32[394,192]{1,0:T(8,128)S(1)}, f32[394,192]{1,0:T(8,128)S(1)}, u32[]{:S(2)}, u32[]{:S(2)}) collective-permute-start(f32[394,192]{1,0:T(8,128)S(1)} %get-tuple-element.31), channel_id=1, source_target_pairs={{0,4},{2,6},{4,0},{6,2},{1,5},{3,7},{5,1},{7,3},{8,12},{10,14},{12... | collective-permute-start | bytes 907784 | tf_op jit(solution)/shard_map/ppermute | solution.py:37
  122.0 17.2 %collective-permute-start.14 = (f32[394,192]{1,0:T(8,128)}, f32[394,192]{1,0:T(8,128)S(1)}, u32[]{:S(2)}, u32[]{:S(2)}) collective-permute-start(f32[394,192]{1,0:T(8,128)} %get-tuple-element.32), channel_id=1, source_target_pairs={{0,6},{2,0},{4,2},{6,4},{1,7},{3,1},{5,3},{7,5},{8,14},{10,8},{12,... | collective-permute-start | bytes 907784 | tf_op jit(solution)/shard_map/ppermute | solution.py:37
  127.3 22.9 %copy-start.21 = (f32[24,768]{1,0:T(8,128)}, f32[24,768]{1,0:T(8,128)S(1)}, u32[]{:S(2)}) copy-start(f32[24,768]{1,0:T(8,128)S(1)} %get-tuple-element.64) | copy-start | bytes 221188
  127.3 22.9 %copy-start.22 = (f32[24,768]{1,0:T(8,128)}, f32[24,768]{1,0:T(8,128)S(1)}, u32[]{:S(2)}) copy-start(f32[24,768]{1,0:T(8,128)S(1)} %get-tuple-element.65) | copy-start | bytes 221188
  128.0 20.8 %all-to-all-start.2 = ((f32[128,1,128]{2,1,0:T(1,128)}), f32[128,1,128]{2,1,0:T(1,128)S(1)}, u32[]{:S(2)}, u32[]{:S(2)}) async-start(f32[128,1,128]{2,1,0:T(1,128)} %broadcast_in_dim.19), calls=%async_computation.2 | async-start | bytes 131072 | tf_op jit(solution)/shard_map/all_to_all | solution.py:329
  137.6 12.7 %copy-start.19 = (f32[24,768]{1,0:T(8,128)S(1)}, f32[24,768]{1,0:T(8,128)}, u32[]{:S(2)}) copy-start(f32[24,768]{1,0:T(8,128)} %md_ref.1) | copy-start | bytes 221188
  137.6 12.7 %copy-start.20 = (f32[24,768]{1,0:T(8,128)S(1)}, f32[24,768]{1,0:T(8,128)}, u32[]{:S(2)}) copy-start(f32[24,768]{1,0:T(8,128)} %mu_ref.1) | copy-start | bytes 221188

commit v2 on v1

--- a/solution.py
+++ b/solution.py
@@ -30,6 +30,7 @@
 
 SMEM = pl.BlockSpec(memory_space=pltpu.SMEM)
 VMEM = pl.BlockSpec(memory_space=pltpu.VMEM)
+ANY = pl.BlockSpec(memory_space=pl.ANY)
 
 
 def shift(value, axis, k):
@@ -83,8 +84,16 @@
         mine_ref, other_ref, parcel, f_s, c_s, wd_ref, acc = refs[4:]
         pairs = [(u0, u1, swapped[0], parcel)]
     else:
-        f_ref, c_ref, r0, r1, l0, l1, near = refs[:7]
-        acc, pg_ref, parcel_r, parcel_l, f_s, c_s, wd_ref = refs[7:]
+        near, sources, refs = refs[0], refs[1:7], refs[7:]
+        (acc, pg_ref, parcel_r, parcel_l), refs = refs[:4], refs[4:]
+        held, (sems, f_s, c_s, wd_ref) = refs[:6], refs[6:]
+        copies = [
+            pltpu.make_async_copy(source, place, sems.at[i])
+            for i, (source, place) in enumerate(zip(sources, held))
+        ]
+        for copy in copies:
+            copy.start()
+        f_ref, c_ref, r0, r1, l0, l1 = held
         acc_in = None
         pairs = [
             (None, None, None, pg_ref),
@@ -98,6 +107,9 @@
     f_s[FULL - 16 : FULL, :] = jnp.zeros((16, D), jnp.bfloat16)
     c_s[FULL - 16 : FULL, :] = jnp.zeros((16, D), jnp.bfloat16)
     for g, (u0, u1, spots, out) in enumerate(pairs):
+        if not last:
+            copies[2 * g].wait()
+            copies[2 * g + 1].wait()
         if u0 is None:
             f_s[0:ROWS, :] = f_ref[...]
             c_s[0:ROWS, :] = c_ref[...]
@@ -161,22 +173,29 @@
     return pltpu.with_memory_space_constraint(array, pltpu.VMEM)
 
 
-def gathered(parts):
+def outside(array):
+    return pltpu.with_memory_space_constraint(array, pltpu.HBM)
+
+
+def gathered(parts, place):
     return pl.pallas_call(
         gather_kernel,
         out_shape=pltpu.VMEM((sum(-(-p.shape[0] // 16) * 16 for p in parts), HALF), jnp.bfloat16),
         in_specs=[VMEM] * len(parts),
         out_specs=VMEM,
         compiler_params=pltpu.CompilerParams(vmem_limit_bytes=4 << 20),
-    )(*map(inside, parts))
-
-
-def run_groups(core, weights, ins, swapped, last):
+    )(*map(place, parts))
+
+
+def run_groups(core, weights, ins, far_ins, swapped, last):
     wide = weights.shape[1] // 2
     sums = pltpu.VMEM((D, 2 * wide), jnp.float32)
     parcel = pltpu.VMEM((HALF + HEAD, 2 * wide), jnp.bfloat16)
     pair = pltpu.VMEM((FULL, D), jnp.bfloat16)
-    scratch = [pair, pair, pltpu.VMEM((D, wide), jnp.bfloat16)]
+    scratch = [pltpu.VMEM(a.shape, a.dtype) for a in far_ins]
+    if far_ins:
+        scratch.append(pltpu.SemaphoreType.DMA((len(far_ins),)))
+    scratch += [pair, pair, pltpu.VMEM((D, wide), jnp.bfloat16)]
     if last:
         out_shape = [sums, sums, parcel]
         scratch.append(pltpu.VMEM((2, D, 2 * wide), jnp.float32))
@@ -191,7 +210,7 @@
     return pl.pallas_call(
         lambda *refs: groups_kernel(*refs, swapped=swapped, last=last),
         out_shape=out_shape,
-        in_specs=[SMEM] + [VMEM] * (len(ins) + 1),
+        in_specs=[SMEM] + [VMEM] * (len(ins) + 1) + [ANY] * len(far_ins),
         out_specs=[VMEM] * len(out_shape),
         scratch_shapes=scratch,
         compiler_params=pltpu.CompilerParams(vmem_limit_bytes=24 << 20),
@@ -200,7 +219,7 @@
             transcendentals=2 * groups * ROWS * wide,
             bytes_accessed=6 << 20,
         ),
-    )(core, inside(weights), *[inside(a) for a in ins])
+    )(core, inside(weights), *map(inside, ins), *map(outside, far_ins))
 
 
 def input_kernel(at_ref, pg_ref, w_ref, *refs):
@@ -224,6 +243,41 @@
         for i in range(len(parcels)):
             value = value + product(pg_s[i, 0:ROWS], up_s[i, span, :])
         out[...] = value
+
+
+def statistics_kernel(
+    core_ref, mine_ref, other_ref, pu_ref, pd_ref, ru_ref, rd_ref, nu_ref, nd_ref, sum_ref, *, count
+):
+    first = core_ref[0] == 0
+    blocks, _, width = mine_ref.shape
+    wide = width // 2
+
+    def laid(ref):
+        tiles = [ref[i] for i in range(blocks)]
+        return [
+            jnp.concatenate([t[:, cut] for t in tiles], axis=1)
+            for cut in (slice(0, wide), slice(wide, width))
+        ]
+
+    mine, other = laid(mine_ref), laid(other_ref)
+    local = None
+    for ours, p_ref, raw_ref, new_ref in ((first, pu_ref, ru_ref, nu_ref), (~first, pd_ref, rd_ref, nd_ref)):
+        grad, square = (jnp.where(ours, m, o) for m, o in zip(mine, other))
+        new = (1.0 - average_rate) * p_ref[...] + average_rate * (square / (2 * count))
+        raw = (grad / 2) / (new + damping)
+        new_ref[...] = new
+        raw_ref[...] = raw
+        part = jnp.sum(raw * raw, axis=0, keepdims=True)
+        local = part if local is None else local + part
+    folded = sum(local[:, i : i + 128] for i in range(0, local.shape[1], 128))
+    sum_ref[...] = jnp.broadcast_to(folded.reshape(1, 1, 128), sum_ref.shape)
+
+
+def update_kernel(sum_ref, mu_ref, md_ref, ru_ref, rd_ref, nu_ref, nd_ref):
+    root_mean = jnp.sqrt(jnp.sum(sum_ref[...], keepdims=True)[0] / (2 * D * FF))
+    factor = step_rate * (1.0 / jnp.maximum(clip_level, root_mean))
+    nu_ref[...] = mu_ref[...] - factor * ru_ref[...]
+    nd_ref[...] = md_ref[...] - factor * rd_ref[...]
 
 
 def shards(
@@ -268,19 +322,17 @@
 
     f0 = shift(r0, "x", 1)
     f1 = shift(l1, "x", -1)
-    near = gathered([r0, l0, r1, l1])
+    near = gathered([r0, l0, r1, l1], outside)
     near = shift(near, "mc", 1)
     spots = ((0, 2 * HEAD), (HEAD, HEAD + FULL))
-    far = shift(gathered([f0, f1]), "mc", 1)
+    far = shift(gathered([f0, f1], inside), "mc", 1)
 
     acc, pg, parcel_r, parcel_l = run_groups(
-        core_at, weights, [features, cotangent, r0, r1, l0, l1, near], spots, False
+        core_at, weights, [near], [features, cotangent, r0, r1, l0, l1], spots, False
     )
     parcel_r = shift(parcel_r, "x", -1)
     parcel_l = shift(parcel_l, "x", 1)
-    mine, other, parcel_f = run_groups(
-        core_at, weights, [f0, f1, far, acc], ((0, HEAD),), True
-    )
+    mine, other, parcel_f = run_groups(core_at, weights, [f0, f1, far, acc], [], ((0, HEAD),), True)
 
     both = mine + shift(other, "mc", 1)
     parcel_f = shift(parcel_f, "x", 2)
@@ -293,9 +345,8 @@
     got = jnp.where(
         is_grad, got * jnp.abs(got) / (grad_unit * grad_unit), (square_unit * got) * (square_unit * got)
     )
-    total = jnp.sum(got, axis=0).reshape(nx, rows, 2, wide)
-    total = jnp.transpose(total, (2, 1, 0, 3)).reshape(2, rows, cols)
-    totals = lax.all_gather(total, "mc", axis=0)
+    total = jnp.sum(got, axis=0)
+    traded = shift(total, "mc", 1)
 
     tile = pltpu.VMEM((ROWS, D // ny), jnp.float32)
     tiles = pl.pallas_call(
@@ -316,21 +367,26 @@
     tiles = [tiles[0]] + [shift(tiles[k], "mp", k) for k in range(1, ny)]
     input_grad = sum(tiles[1:], tiles[0]).astype(jnp.bfloat16)[None]
 
-    images_all = 2 * nz * nx
-    grad_up, square_up = totals[0, 0] / 2, totals[0, 1] / (2 * images_all)
-    grad_down, square_down = totals[1, 0] / 2, totals[1, 1] / (2 * images_all)
-    precision_new_up = (1.0 - average_rate) * precision_up + average_rate * square_up
-    precision_new_down = (1.0 - average_rate) * precision_down + average_rate * square_down
-    raw_up = grad_up / (precision_new_up + damping)
-    raw_down = grad_down / (precision_new_down + damping)
-    local = jnp.sum(raw_up * raw_up + raw_down * raw_down, axis=0, keepdims=True)
-    local = jnp.sum(local.reshape(1, cols // 128, 128), axis=1, keepdims=True)
     group = nz * nx * ny
-    everyone = lax.all_to_all(jnp.broadcast_to(local, (group, 1, 128)), ZXY, 0, 0, tiled=True)
-    root_mean = jnp.sqrt(jnp.sum(everyone) / (2 * D * FF))
-    factor = 1.0 / jnp.maximum(clip_level, root_mean)
-    mean_new_up = mean_up - step_rate * factor * raw_up
-    mean_new_down = mean_down - step_rate * factor * raw_down
+    whole = jax.ShapeDtypeStruct((rows, cols), jnp.float32)
+    kept = pltpu.VMEM((rows, cols), jnp.float32)
+    raw_up, raw_down, precision_new_up, precision_new_down, local = pl.pallas_call(
+        lambda *refs: statistics_kernel(*refs, count=2 * nz * nx),
+        out_shape=[kept, kept, whole, whole, jax.ShapeDtypeStruct((group, 1, 128), jnp.float32)],
+        in_specs=[SMEM] + [VMEM] * 4,
+        out_specs=[VMEM] * 5,
+        compiler_params=pltpu.CompilerParams(vmem_limit_bytes=8 << 20),
+        name="statistics",
+    )(core.reshape(1), inside(total), inside(traded), inside(precision_up), inside(precision_down))
+    everyone = lax.all_to_all(local, ZXY, 0, 0, tiled=True)
+    mean_new_up, mean_new_down = pl.pallas_call(
+        update_kernel,
+        out_shape=[whole, whole],
+        in_specs=[VMEM] * 5,
+        out_specs=[VMEM] * 2,
+        compiler_params=pltpu.CompilerParams(vmem_limit_bytes=8 << 20),
+        name="update",
+    )(*map(inside, (everyone, mean_up, mean_down, raw_up, raw_down)))
     return (mean_new_up, precision_new_up, mean_new_down, precision_new_down, input_grad)
 
 

time: 152 us -> 146 us (0.961)
  local copies, waits for them, and re-layouts: 10.9 us -> 3.29 us
  Pallas kernels: 11.2 us -> 15 us
  blocking collectives: 2.01 us -> 0 us
  starting transfers between devices: 49.2 us -> 51.1 us
    unnamed x47 -> x27, local copies, waits for them, and re-layouts: 9.79 us -> 3.29 us
    all_gather x1 -> x0, blocking collectives: 2.01 us -> none  [shards(): totals = lax.all_gather(total, 'mc', axis=0)]
    pallas_call x0 -> x2, Pallas kernels: none -> 1.74 us  [the longest x1 0.93 us: shards(): pl.pallas_call(update_kernel, out_shape=[whole, whole], in_specs=[VMEM] *...]
    ppermute x15 -> x16, starting transfers between devices: 18.2 us -> 19.6 us  [shift(): return lax.ppermute(value, axis, [(i, (i + k) % n) for i in range(n)])]
    ppermute x15 -> x16, waiting for transfers between devices: 63 us -> 63.8 us  [shift(): return lax.ppermute(value, axis, [(i, (i + k) % n) for i in range(n)])]
  transfers between devices with their start and end apart: 18 -> 19, of which waited for: 9 -> 10; matrix products, arithmetic and copies ran while one was open for 2% -> 2% of each run, Pallas kernels for 4% -> 7%
where the time goes in v2:
time: 146 us; the launch traced here: 145 us
  waiting for transfers between devices  71.6 us (49%)
  starting transfers between devices  51.1 us (35%)
  Pallas kernels  15 us (10%)
  local copies, waits for them, and re-layouts  3.29 us (2%)
  other arithmetic  3.01 us (2%)
    ppermute x16, waiting for transfers between devices, shift(): return lax.ppermute(value, axis, [(i, (i + k) % n) for i in range(n)])  63.8 us
    ppermute x16, starting transfers between devices, shift(): return lax.ppermute(value, axis, [(i, (i + k) % n) for i in range(n)])  19.6 us
    all_to_all x1, starting transfers between devices, shards(): lax.all_to_all(payload.reshape(nz * nx, rows, 2 * wide), DP, 0, 0, tiled=...  11.6 us
    all_to_all x1, starting transfers between devices, shards(): everyone = lax.all_to_all(local, ZXY, 0, 0, tiled=True)  10.1 us
    all_to_all x1, starting transfers between devices, shards(): lax.all_to_all(packed.reshape(nz * nx, rows, 2 * wide), DP, 0, 0, tiled=T...  9.73 us
    all_to_all x1, waiting for transfers between devices, shards(): everyone = lax.all_to_all(local, ZXY, 0, 0, tiled=True)  7.87 us
    pallas_call x2, Pallas kernels, run_groups(): pl.pallas_call(lambda *refs: groups_kernel(*refs, swapped=swapped, last=l...  7.19 us
    unnamed x27, local copies, waits for them, and re-layouts  3.29 us
  transfers between devices with their start and end apart: 19, of which 10 were waited for; matrix products, arithmetic and copies ran while one was open for 2% of the time, Pallas kernels for 7%

profile of v2, /device:TPU:2, one launch (start us, length us, event | category | flops | bytes accessed | tf_op | source)
XLA Modules:
  0.0 144.9 jit_solution(1571605556574688093)
XLA Ops:
  0.6 2.4 %prepare.1 = (bf16[208,1152]{1,0:T(8,128)(2,1)S(1)}, bf16[186,1152]{1,0:T(8,128)(2,1)S(1)}, bf16[8,4,24,384]{3,2,1,0:T(8,128)(2,1)}) custom-call(s32[1]{0:T(128)} %bitcast.core_ref.refs_0_, bf16[394,768]{1,0:T(8,128)(2,1)} %refs_3_.2, bf16[394,768]{1,0:T(8,128)(2,1)} %bitcast.15, f32[24,768]{1,0:T(8,128)} %mu_ref.3, f32[24,768]{1,0:T(8,128)} %refs_3_.3, ...), custom_call_target="tpu_custom_call" | custom-call | tf_op jit(solution)/shard_map/prepare/pallas_call | solution.py:293
  3.0 11.6 %all-to-all-start = ((bf16[32,24,384]{2,1,0:T(8,128)(2,1)}), bf16[32,24,384]{2,1,0:T(8,128)(2,1)S(1)}, u32[]{:S(2)}, u32[]{:S(2)}) async-start(bf16[32,24,384]{2,1,0:T(8,128)(2,1)} %bitcast.4), calls=%async_computation | async-start | bytes 1179648 | tf_op jit(solution)/shard_map/all_to_all | solution.py:319
  14.6 1.5 %collective-permute-start = (bf16[208,1152]{1,0:T(8,128)(2,1)S(1)}, bf16[208,1152]{1,0:T(8,128)(2,1)S(1)}, u32[]{:S(2)}, u32[]{:S(2)}) collective-permute-start(bf16[208,1152]{1,0:T(8,128)(2,1)S(1)} %get-tuple-element.27), channel_id=1, source_target_pairs={{0,8},{8,16},{16,24},{24,0},{1,9},{9,17},{17,25},{25,1},{2,10},{10... | collective-permute-start | bytes 1437704 | tf_op jit(solution)/shard_map/ppermute | solution.py:38
  16.2 0.6 collective-permute-start.5
  16.7 1.4 collective-permute-start.2
  18.2 0.6 collective-permute-start.6
  18.8 14.7 %collective-permute-done.refs_0_.refs_5_ = bf16[208,1152]{1,0:T(8,128)(2,1)S(1)} collective-permute-done((bf16[208,1152]{1,0:T(8,128)(2,1)S(1)}, bf16[208,1152]{1,0:T(8,128)(2,1)S(1)}, u32[]{:S(2)}, u32[]{:S(2)}) %collective-permute-start) | collective-permute-done | bytes 479264 | tf_op jit(solution)/shard_map/ppermute | solution.py:38
  33.5 1.5 %collective-permute-start.1 = (bf16[208,1152]{1,0:T(8,128)(2,1)S(1)}, bf16[208,1152]{1,0:T(8,128)(2,1)S(1)}, u32[]{:S(2)}, u32[]{:S(2)}) collective-permute-start(bf16[208,1152]{1,0:T(8,128)(2,1)S(1)} %collective-permute-done.refs_0_.refs_5_), channel_id=1, source_target_pairs={{0,8},{8,16},{16,24},{24,0},{1,9},{9,17},{17,25},{25,1},{2,10},{10... | collective-permute-start | bytes 1437704 | tf_op jit(solution)/shard_map/ppermute | solution.py:38
  35.0 8.4 %collective-permute-done.2.refs_3_.refs_8_ = bf16[186,1152]{1,0:T(8,128)(2,1)S(1)} collective-permute-done((bf16[186,1152]{1,0:T(8,128)(2,1)S(1)}, bf16[186,1152]{1,0:T(8,128)(2,1)S(1)}, u32[]{:S(2)}, u32[]{:S(2)}) %collective-permute-start.2) | collective-permute-done | bytes 428576 | tf_op jit(solution)/shard_map/ppermute | solution.py:38
  43.4 0.0 collective-permute-done.6.refs_2_.refs_6_
  43.5 0.0 collective-permute-done.5.refs_1_.refs_7_
  43.5 0.7 copy-done.11
  44.2 0.2 copy-done.12
  44.4 0.8 copy-done.10
  45.1 1.5 %shard_map.120 = bf16[800,384]{1,0:T(8,128)(2,1)S(1)} custom-call(bf16[208,1152]{1,0:T(8,128)(2,1)} %copy-done.9, bf16[208,1152]{1,0:T(8,128)(2,1)} %copy-done.10, bf16[186,1152]{1,0:T(8,128)(2,1)} %copy-done.12, bf16[186,1152]{1,0:T(8,128)(2,1)} %copy-done.11), custom_call_target="tpu_custom_call" | custom-call | tf_op jit(solution)/shard_map/pallas_call | solution.py:181
  46.6 0.1 collective-permute-start.7
  46.7 1.9 %collective-permute-start.3 = (bf16[186,1152]{1,0:T(8,128)(2,1)}, bf16[186,1152]{1,0:T(8,128)(2,1)S(1)}, u32[]{:S(2)}, u32[]{:S(2)}) collective-permute-start(bf16[186,1152]{1,0:T(8,128)(2,1)} %copy-done.11), channel_id=1, source_target_pairs={{0,24},{8,0},{16,8},{24,16},{1,25},{9,1},{17,9},{25,17},{2,26},{10... | collective-permute-start | bytes 1285640 | tf_op jit(solution)/shard_map/ppermute | solution.py:38
  48.6 10.9 %collective-permute-done.3.refs_1_.refs_3_ = bf16[186,1152]{1,0:T(8,128)(2,1)S(1)} collective-permute-done((bf16[186,1152]{1,0:T(8,128)(2,1)}, bf16[186,1152]{1,0:T(8,128)(2,1)S(1)}, u32[]{:S(2)}, u32[]{:S(2)}) %collective-permute-start.3) | collective-permute-done | bytes 428576 | tf_op jit(solution)/shard_map/ppermute | solution.py:38
  59.6 0.3 collective-permute-start.4
  59.9 5.5 %shard_map.121 = (f32[2,768,384]{2,1,0:T(8,128)S(1)}, bf16[394,192]{1,0:T(8,128)(2,1)S(1)}, bf16[592,384]{1,0:T(8,128)(2,1)S(1)}, bf16[592,384]{1,0:T(8,128)(2,1)S(1)}) custom-call(s32[1]{0:T(128)} %bitcast.core_ref.refs_0_, bf16[768,384]{1,0:T(8,128)(2,1)S(1)} %bitcast.12, bf16[800,384]{1,0:T(8,128)(2,1)S(1)} %collective-permute-done.7.refs_2_, ...), custom_call_target="tpu_custom_call" | custom-call | flops 1394343936 | bytes 6291456 | tf_op jit(solution)/shard_map/pallas_call | solution.py:210
  65.4 0.0 collective-permute-done.4.refs_4_
  65.4 1.7 %shard_map.122 = (f32[768,384]{1,0:T(8,128)S(1)}, f32[768,384]{1,0:T(8,128)S(1)}, bf16[592,384]{1,0:T(8,128)(2,1)S(1)}) custom-call(s32[1]{0:T(128)} %bitcast.core_ref.refs_0_, bf16[768,384]{1,0:T(8,128)(2,1)S(1)} %bitcast.13, bf16[208,1152]{1,0:T(8,128)(2,1)S(1)} %collective-permute-done.1.refs_0_.refs_2_, ...), custom_call_target="tpu_custom_call" | custom-call | flops 464781312 | bytes 6291456 | tf_op jit(solution)/shard_map/pallas_call | solution.py:210
  67.1 0.8 copy-done.8
  67.9 0.5 collective-permute-start.8
  68.4 2.5 %collective-permute-done.8 = f32[768,384]{1,0:T(8,128)S(1)} collective-permute-done((f32[768,384]{1,0:T(8,128)S(1)}, f32[768,384]{1,0:T(8,128)S(1)}, u32[]{:S(2)}, u32[]{:S(2)}) %collective-permute-start.8) | collective-permute-done | bytes 1179680 | tf_op jit(solution)/shard_map/ppermute | solution.py:38
  70.9 1.5 %fusion = f16[768,384]{1,0:T(8,128)(2,1)} fusion(f32[768,384]{1,0:T(8,128)S(1)} %get-tuple-element.30, f32[768,384]{1,0:T(8,128)S(1)} %collective-permute-done.8, f32[384]{0:T(512)S(1)} %broadcast_select_fusion), kind=kLoop, calls=%fused_computation.4 | loop fusion | flops 2064384 | bytes 2950656 | tf_op jit(solution)/shard_map/convert_element_type | solution.py:341
  72.3 9.7 %all-to-all-start.1 = ((f16[32,24,384]{2,1,0:T(8,128)(2,1)}), f16[32,24,384]{2,1,0:T(8,128)(2,1)}, u32[]{:S(2)}, u32[]{:S(2)}) async-start(f16[32,24,384]{2,1,0:T(8,128)(2,1)} %bitcast.6), calls=%async_computation.1 | async-start | bytes 1179648 | tf_op jit(solution)/shard_map/all_to_all | solution.py:342
  82.1 0.4 collective-permute-start.10
  82.4 1.7 %collective-permute-start.11 = (bf16[592,384]{1,0:T(8,128)(2,1)S(1)}, bf16[592,384]{1,0:T(8,128)(2,1)S(1)}, u32[]{:S(2)}, u32[]{:S(2)}) collective-permute-start(bf16[592,384]{1,0:T(8,128)(2,1)S(1)} %copy-done.5), channel_id=1, source_target_pairs={{0,8},{8,16},{16,24},{24,0},{1,9},{9,17},{17,25},{25,1},{2,10},{10... | collective-permute-start | bytes 1363976 | tf_op jit(solution)/shard_map/ppermute | solution.py:38
  84.2 3.3 %collective-permute-start.12 = (bf16[592,384]{1,0:T(8,128)(2,1)}, bf16[592,384]{1,0:T(8,128)(2,1)S(1)}, u32[]{:S(2)}, u32[]{:S(2)}) collective-permute-start(bf16[592,384]{1,0:T(8,128)(2,1)} %copy-done.8), channel_id=1, source_target_pairs={{0,16},{8,24},{16,0},{24,8},{1,17},{9,25},{17,1},{25,9},{2,18},{10... | collective-permute-start | bytes 1363976 | tf_op jit(solution)/shard_map/ppermute | solution.py:38
  87.5 13.0 %collective-permute-done.10.refs_0_ = bf16[592,384]{1,0:T(8,128)(2,1)S(1)} collective-permute-done((bf16[592,384]{1,0:T(8,128)(2,1)S(1)}, bf16[592,384]{1,0:T(8,128)(2,1)S(1)}, u32[]{:S(2)}, u32[]{:S(2)}) %collective-permute-start.10) | collective-permute-done | bytes 454688 | tf_op jit(solution)/shard_map/ppermute | solution.py:38
  100.4 1.0 collective-permute-done.11.refs_1_
  101.4 9.5 %collective-permute-done.12.refs_2_ = bf16[592,384]{1,0:T(8,128)(2,1)S(1)} collective-permute-done((bf16[592,384]{1,0:T(8,128)(2,1)}, bf16[592,384]{1,0:T(8,128)(2,1)S(1)}, u32[]{:S(2)}, u32[]{:S(2)}) %collective-permute-start.12) | collective-permute-done | bytes 454688 | tf_op jit(solution)/shard_map/ppermute | solution.py:38
  110.9 2.2 %input_grad.1 = (f32[394,192]{1,0:T(8,128)S(1)}, f32[394,192]{1,0:T(8,128)S(1)}, f32[394,192]{1,0:T(8,128)}, f32[394,192]{1,0:T(8,128)}) custom-call(s32[1]{0:T(128)} %bitcast.9.at_ref, bf16[394,192]{1,0:T(8,128)(2,1)S(1)} %get-tuple-element.39.pg_ref, bf16[768,384]{1,0:T(8,128)(2,1)S(1)} %bitcast.14, bf16[592,384]{1,0:T(8,128)(2,1)S(1)} %collective-permute-done.10.refs_0_, ...), custom_call_target="tpu_custom_call" | custom-call | flops 464781312 | bytes 4194304 | tf_op jit(solution)/shard_map/input_grad/pallas_call | solution.py:352
  113.0 1.6 %collective-permute-start.13 = (f32[394,192]{1,0:T(8,128)S(1)}, f32[394,192]{1,0:T(8,128)S(1)}, u32[]{:S(2)}, u32[]{:S(2)}) collective-permute-start(f32[394,192]{1,0:T(8,128)S(1)} %get-tuple-element.44), channel_id=1, source_target_pairs={{0,2},{2,4},{4,6},{6,0},{1,3},{3,5},{5,7},{7,1},{8,10},{10,12},{12... | collective-permute-start | bytes 907784 | tf_op jit(solution)/shard_map/ppermute | solution.py:38
  114.6 2.9 %collective-permute-start.14 = (f32[394,192]{1,0:T(8,128)}, f32[394,192]{1,0:T(8,128)S(1)}, u32[]{:S(2)}, u32[]{:S(2)}) collective-permute-start(f32[394,192]{1,0:T(8,128)} %get-tuple-element.45), channel_id=1, source_target_pairs={{0,4},{2,6},{4,0},{6,2},{1,5},{3,7},{5,1},{7,3},{8,12},{10,14},{12... | collective-permute-start | bytes 907784 | tf_op jit(solution)/shard_map/ppermute | solution.py:38
  117.5 1.3 collective-permute-start.15
  118.9 1.4 fusion.3.refs_1_
  120.3 0.1 collective-permute-start.9
  120.4 1.4 collective-permute-done.9.refs_2_
  121.7 0.8 statistics.1
  122.5 10.1 %all-to-all-start.2 = ((f32[128,1,128]{2,1,0:T(1,128)}), f32[128,1,128]{2,1,0:T(1,128)S(1)}, u32[]{:S(2)}, u32[]{:S(2)}) async-start(f32[128,1,128]{2,1,0:T(1,128)} %get-tuple-element.32), calls=%async_computation.2 | async-start | bytes 131072 | tf_op jit(solution)/shard_map/all_to_all | solution.py:381
  132.6 2.4 %collective-permute-done.14 = f32[394,192]{1,0:T(8,128)S(1)} collective-permute-done((f32[394,192]{1,0:T(8,128)}, f32[394,192]{1,0:T(8,128)S(1)}, u32[]{:S(2)}, u32[]{:S(2)}) %collective-permute-start.14) | collective-permute-done | bytes 302624 | tf_op jit(solution)/shard_map/ppermute | solution.py:38
  135.1 0.0 collective-permute-done.15
  135.1 0.2 fusion.5
  135.3 0.8 copy.13
  136.1 7.9 %all-to-all-done.2.sum_ref = f32[128,1,128]{2,1,0:T(1,128)S(1)} async-done(((f32[128,1,128]{2,1,0:T(1,128)}), f32[128,1,128]{2,1,0:T(1,128)S(1)}, u32[]{:S(2)}, u32[]{:S(2)}) %all-to-all-start.2) | async-done | bytes 65568 | tf_op jit(solution)/shard_map/all_to_all | solution.py:381
  143.9 0.9 update.1
  (30 shorter events, 0.1 us)
Async XLA Ops:
  3.0 56.8 %all-to-all-start = ((bf16[32,24,384]{2,1,0:T(8,128)(2,1)}), bf16[32,24,384]{2,1,0:T(8,128)(2,1)S(1)}, u32[]{:S(2)}, u32[]{:S(2)}) async-start(bf16[32,24,384]{2,1,0:T(8,128)(2,1)} %bitcast.4), calls=%async_computation | async-start | bytes 1179648 | tf_op jit(solution)/shard_map/all_to_all | solution.py:319
  14.6 18.9 %collective-permute-start = (bf16[208,1152]{1,0:T(8,128)(2,1)S(1)}, bf16[208,1152]{1,0:T(8,128)(2,1)S(1)}, u32[]{:S(2)}, u32[]{:S(2)}) collective-permute-start(bf16[208,1152]{1,0:T(8,128)(2,1)S(1)} %get-tuple-element.27), channel_id=1, source_target_pairs={{0,8},{8,16},{16,24},{24,0},{1,9},{9,17},{17,25},{25,1},{2,10},{10... | collective-permute-start | bytes 1437704 | tf_op jit(solution)/shard_map/ppermute | solution.py:38
  16.2 27.3 %collective-permute-start.5 = (bf16[208,1152]{1,0:T(8,128)(2,1)S(1)}, bf16[208,1152]{1,0:T(8,128)(2,1)S(1)}, u32[]{:S(2)}, u32[]{:S(2)}) collective-permute-start(bf16[208,1152]{1,0:T(8,128)(2,1)S(1)} %get-tuple-element.27), channel_id=1, source_target_pairs={{0,24},{8,0},{16,8},{24,16},{1,25},{9,1},{17,9},{25,17},{2,26},{10... | collective-permute-start | bytes 1437704 | tf_op jit(solution)/shard_map/ppermute | solution.py:38
  16.7 26.7 %collective-permute-start.2 = (bf16[186,1152]{1,0:T(8,128)(2,1)S(1)}, bf16[186,1152]{1,0:T(8,128)(2,1)S(1)}, u32[]{:S(2)}, u32[]{:S(2)}) collective-permute-start(bf16[186,1152]{1,0:T(8,128)(2,1)S(1)} %get-tuple-element.28), channel_id=1, source_target_pairs={{0,24},{8,0},{16,8},{24,16},{1,25},{9,1},{17,9},{25,17},{2,26},{10... | collective-permute-start | bytes 1285640 | tf_op jit(solution)/shard_map/ppermute | solution.py:38
  18.2 25.3 %collective-permute-start.6 = (bf16[186,1152]{1,0:T(8,128)(2,1)S(1)}, bf16[186,1152]{1,0:T(8,128)(2,1)S(1)}, u32[]{:S(2)}, u32[]{:S(2)}) collective-permute-start(bf16[186,1152]{1,0:T(8,128)(2,1)S(1)} %get-tuple-element.28), channel_id=1, source_target_pairs={{0,8},{8,16},{16,24},{24,0},{1,9},{9,17},{17,25},{25,1},{2,10},{10... | collective-permute-start | bytes 1285640 | tf_op jit(solution)/shard_map/ppermute | solution.py:38
  33.5 10.0 %copy-start.9 = (bf16[208,1152]{1,0:T(8,128)(2,1)}, bf16[208,1152]{1,0:T(8,128)(2,1)S(1)}, u32[]{:S(2)}) copy-start(bf16[208,1152]{1,0:T(8,128)(2,1)S(1)} %collective-permute-done.refs_0_.refs_5_) | copy-start | bytes 1437700
  33.5 26.0 %collective-permute-start.1 = (bf16[208,1152]{1,0:T(8,128)(2,1)S(1)}, bf16[208,1152]{1,0:T(8,128)(2,1)S(1)}, u32[]{:S(2)}, u32[]{:S(2)}) collective-permute-start(bf16[208,1152]{1,0:T(8,128)(2,1)S(1)} %collective-permute-done.refs_0_.refs_5_), channel_id=1, source_target_pairs={{0,8},{8,16},{16,24},{24,0},{1,9},{9,17},{17,25},{25,1},{2,10},{10... | collective-permute-start | bytes 1437704 | tf_op jit(solution)/shard_map/ppermute | solution.py:38
  43.4 0.8 copy-start.11
  43.5 0.9 copy-start.12
  44.4 0.8 copy-start.10
  46.6 13.2 %collective-permute-start.7 = (bf16[800,384]{1,0:T(8,128)(2,1)S(1)}, bf16[800,384]{1,0:T(8,128)(2,1)S(1)}, u32[]{:S(2)}, u32[]{:S(2)}) collective-permute-start(bf16[800,384]{1,0:T(8,128)(2,1)S(1)} %shard_map.120), channel_id=1, source_target_pairs={{0,1},{1,0},{2,3},{3,2},{4,5},{5,4},{6,7},{7,6},{8,9},{9,8},{10,11... | collective-permute-start | bytes 1843208 | tf_op jit(solution)/shard_map/ppermute | solution.py:38
  46.7 12.8 %collective-permute-start.3 = (bf16[186,1152]{1,0:T(8,128)(2,1)}, bf16[186,1152]{1,0:T(8,128)(2,1)S(1)}, u32[]{:S(2)}, u32[]{:S(2)}) collective-permute-start(bf16[186,1152]{1,0:T(8,128)(2,1)} %copy-done.11), channel_id=1, source_target_pairs={{0,24},{8,0},{16,8},{24,16},{1,25},{9,1},{17,9},{25,17},{2,26},{10... | collective-permute-start | bytes 1285640 | tf_op jit(solution)/shard_map/ppermute | solution.py:38
  59.6 5.8 %collective-permute-start.4 = (bf16[400,384]{1,0:T(8,128)(2,1)S(1)}, bf16[400,384]{1,0:T(8,128)(2,1)S(1)}, u32[]{:S(2)}, u32[]{:S(2)}) collective-permute-start(bf16[400,384]{1,0:T(8,128)(2,1)S(1)} %shard_map.119), channel_id=1, source_target_pairs={{0,1},{1,0},{2,3},{3,2},{4,5},{5,4},{6,7},{7,6},{8,9},{9,8},{10,11... | collective-permute-start | bytes 921608 | tf_op jit(solution)/shard_map/ppermute | solution.py:38
  65.4 1.7 %copy-start.4 = (bf16[592,384]{1,0:T(8,128)(2,1)}, bf16[592,384]{1,0:T(8,128)(2,1)S(1)}, u32[]{:S(2)}) copy-start(bf16[592,384]{1,0:T(8,128)(2,1)S(1)} %get-tuple-element.41) | copy-start | bytes 1363972
  65.4 1.7 %copy-start.6 = (bf16[592,384]{1,0:T(8,128)(2,1)}, bf16[592,384]{1,0:T(8,128)(2,1)S(1)}, u32[]{:S(2)}) copy-start(bf16[592,384]{1,0:T(8,128)(2,1)S(1)} %get-tuple-element.40) | copy-start | bytes 1363972
  67.1 0.8 copy-start.8
  67.9 3.0 %collective-permute-start.8 = (f32[768,384]{1,0:T(8,128)S(1)}, f32[768,384]{1,0:T(8,128)S(1)}, u32[]{:S(2)}, u32[]{:S(2)}) collective-permute-start(f32[768,384]{1,0:T(8,128)S(1)} %get-tuple-element.31), channel_id=1, source_target_pairs={{0,1},{1,0},{2,3},{3,2},{4,5},{5,4},{6,7},{7,6},{8,9},{9,8},{10,11... | collective-permute-start | bytes 3538952 | tf_op jit(solution)/shard_map/ppermute | solution.py:38
  72.3 9.7 %copy-start.7 = (bf16[592,384]{1,0:T(8,128)(2,1)S(1)}, bf16[592,384]{1,0:T(8,128)(2,1)}, u32[]{:S(2)}) copy-start(bf16[592,384]{1,0:T(8,128)(2,1)} %copy-done.6) | copy-start | bytes 1363972
  72.3 10.1 %copy-start.5 = (bf16[592,384]{1,0:T(8,128)(2,1)S(1)}, bf16[592,384]{1,0:T(8,128)(2,1)}, u32[]{:S(2)}) copy-start(bf16[592,384]{1,0:T(8,128)(2,1)} %copy-done.4) | copy-start | bytes 1363972
  72.3 46.6 %all-to-all-start.1 = ((f16[32,24,384]{2,1,0:T(8,128)(2,1)}), f16[32,24,384]{2,1,0:T(8,128)(2,1)}, u32[]{:S(2)}, u32[]{:S(2)}) async-start(f16[32,24,384]{2,1,0:T(8,128)(2,1)} %bitcast.6), calls=%async_computation.1 | async-start | bytes 1179648 | tf_op jit(solution)/shard_map/all_to_all | solution.py:342
  82.1 18.4 %collective-permute-start.10 = (bf16[592,384]{1,0:T(8,128)(2,1)S(1)}, bf16[592,384]{1,0:T(8,128)(2,1)S(1)}, u32[]{:S(2)}, u32[]{:S(2)}) collective-permute-start(bf16[592,384]{1,0:T(8,128)(2,1)S(1)} %copy-done.7), channel_id=1, source_target_pairs={{0,24},{8,0},{16,8},{24,16},{1,25},{9,1},{17,9},{25,17},{2,26},{10... | collective-permute-start | bytes 1363976 | tf_op jit(solution)/shard_map/ppermute | solution.py:38
  82.4 18.9 %collective-permute-start.11 = (bf16[592,384]{1,0:T(8,128)(2,1)S(1)}, bf16[592,384]{1,0:T(8,128)(2,1)S(1)}, u32[]{:S(2)}, u32[]{:S(2)}) collective-permute-start(bf16[592,384]{1,0:T(8,128)(2,1)S(1)} %copy-done.5), channel_id=1, source_target_pairs={{0,8},{8,16},{16,24},{24,0},{1,9},{9,17},{17,25},{25,1},{2,10},{10... | collective-permute-start | bytes 1363976 | tf_op jit(solution)/shard_map/ppermute | solution.py:38
  84.2 26.7 %collective-permute-start.12 = (bf16[592,384]{1,0:T(8,128)(2,1)}, bf16[592,384]{1,0:T(8,128)(2,1)S(1)}, u32[]{:S(2)}, u32[]{:S(2)}) collective-permute-start(bf16[592,384]{1,0:T(8,128)(2,1)} %copy-done.8), channel_id=1, source_target_pairs={{0,16},{8,24},{16,0},{24,8},{1,17},{9,25},{17,1},{25,9},{2,18},{10... | collective-permute-start | bytes 1363976 | tf_op jit(solution)/shard_map/ppermute | solution.py:38
  110.9 10.9 %copy-start = (f32[24,768]{1,0:T(8,128)S(1)}, f32[24,768]{1,0:T(8,128)}, u32[]{:S(2)}) copy-start(f32[24,768]{1,0:T(8,128)} %refs_3_.3) | copy-start | bytes 221188
  110.9 10.9 %copy-start.1 = (f32[24,768]{1,0:T(8,128)S(1)}, f32[24,768]{1,0:T(8,128)}, u32[]{:S(2)}) copy-start(f32[24,768]{1,0:T(8,128)} %refs_4_.1) | copy-start | bytes 221188
  113.0 19.6 %collective-permute-start.13 = (f32[394,192]{1,0:T(8,128)S(1)}, f32[394,192]{1,0:T(8,128)S(1)}, u32[]{:S(2)}, u32[]{:S(2)}) collective-permute-start(f32[394,192]{1,0:T(8,128)S(1)} %get-tuple-element.44), channel_id=1, source_target_pairs={{0,2},{2,4},{4,6},{6,0},{1,3},{3,5},{5,7},{7,1},{8,10},{10,12},{12... | collective-permute-start | bytes 907784 | tf_op jit(solution)/shard_map/ppermute | solution.py:38
  114.6 20.5 %collective-permute-start.14 = (f32[394,192]{1,0:T(8,128)}, f32[394,192]{1,0:T(8,128)S(1)}, u32[]{:S(2)}, u32[]{:S(2)}) collective-permute-start(f32[394,192]{1,0:T(8,128)} %get-tuple-element.45), channel_id=1, source_target_pairs={{0,4},{2,6},{4,0},{6,2},{1,5},{3,7},{5,1},{7,3},{8,12},{10,14},{12... | collective-permute-start | bytes 907784 | tf_op jit(solution)/shard_map/ppermute | solution.py:38
  117.5 17.6 %collective-permute-start.15 = (f32[394,192]{1,0:T(8,128)}, f32[394,192]{1,0:T(8,128)S(1)}, u32[]{:S(2)}, u32[]{:S(2)}) collective-permute-start(f32[394,192]{1,0:T(8,128)} %get-tuple-element.46), channel_id=1, source_target_pairs={{0,6},{2,0},{4,2},{6,4},{1,7},{3,1},{5,3},{7,5},{8,14},{10,8},{12,... | collective-permute-start | bytes 907784 | tf_op jit(solution)/shard_map/ppermute | solution.py:38
  120.3 1.5 %collective-permute-start.9 = (f32[4,24,384]{2,1,0:T(8,128)S(1)}, f32[4,24,384]{2,1,0:T(8,128)S(1)}, u32[]{:S(2)}, u32[]{:S(2)}) collective-permute-start(f32[4,24,384]{2,1,0:T(8,128)S(1)} %fusion.3.refs_1_), channel_id=1, source_target_pairs={{0,1},{1,0},{2,3},{3,2},{4,5},{5,4},{6,7},{7,6},{8,9},{9,8},{10,11... | collective-permute-start | bytes 442376 | tf_op jit(solution)/shard_map/ppermute | solution.py:38
  122.5 21.4 %copy-start.2 = (f32[24,768]{1,0:T(8,128)S(1)}, f32[24,768]{1,0:T(8,128)}, u32[]{:S(2)}) copy-start(f32[24,768]{1,0:T(8,128)} %mu_ref.3) | copy-start | bytes 221188
  122.5 21.4 %copy-start.3 = (f32[24,768]{1,0:T(8,128)S(1)}, f32[24,768]{1,0:T(8,128)}, u32[]{:S(2)}) copy-start(f32[24,768]{1,0:T(8,128)} %md_ref.3) | copy-start | bytes 221188
  122.5 21.4 %all-to-all-start.2 = ((f32[128,1,128]{2,1,0:T(1,128)}), f32[128,1,128]{2,1,0:T(1,128)S(1)}, u32[]{:S(2)}, u32[]{:S(2)}) async-start(f32[128,1,128]{2,1,0:T(1,128)} %get-tuple-element.32), calls=%async_computation.2 | async-start | bytes 131072 | tf_op jit(solution)/shard_map/all_to_all | solution.py:381

commit v3 on v2

--- a/solution.py
+++ b/solution.py
@@ -14,6 +14,8 @@
 HEAD = 208
 TAIL = ROWS - HEAD
 FULL = 400
+STEP = 48
+QUARTERS = STEP + HEAD - 3 * STEP
 HALF = D // 2
 DP = ("z", "x")
 ZXY = ("z", "x", "mp")
@@ -39,12 +41,18 @@
 
 
 def prepare_kernel(
-    core_ref, f_ref, c_ref, mu_ref, pu_ref, nu_ref, md_ref, pd_ref, nd_ref, head_ref, tail_ref, w_ref
+    at_ref, f_ref, c_ref, mu_ref, pu_ref, nu_ref, md_ref, pd_ref, nd_ref,
+    head_ref, tail_ref, right_ref, left_ref, w_ref, u_s,
 ):
-    first = core_ref[0] == 0
-    for out, cut in ((head_ref, slice(0, HEAD)), (tail_ref, slice(HEAD, ROWS))):
-        out[:, 0:HALF] = jnp.where(first, f_ref[cut, 0:HALF], f_ref[cut, HALF:D])
-        out[:, HALF:] = c_ref[cut, :]
+    first = at_ref[0] == 0
+    u_s[FULL - 16 : FULL] = jnp.zeros((16, HALF + D), jnp.bfloat16)
+    u_s[0:ROWS, 0:HALF] = jnp.where(first, f_ref[:, 0:HALF], f_ref[:, HALF:D])
+    u_s[0:ROWS, HALF:] = c_ref[...]
+    head_ref[...] = u_s[0:HEAD]
+    tail_ref[...] = u_s[HEAD:ROWS]
+    at = at_ref[1] * STEP
+    right_ref[...] = u_s[pl.ds(pl.multiple_of(HEAD + at, 16), STEP)]
+    left_ref[...] = u_s[pl.ds(pl.multiple_of(at, 16), HEAD - 3 * STEP)]
     nz, nx, _, width = w_ref.shape
 
     def drawn(m, p, n):
@@ -66,6 +74,11 @@
     )
 
 
+def join_kernel(right_ref, left_ref, out_ref):
+    out_ref[0:STEP] = right_ref[...]
+    out_ref[STEP:] = left_ref[...]
+
+
 def gather_kernel(*refs):
     at = 0
     for ref in refs[:-1]:
@@ -77,51 +90,62 @@
     return jnp.concatenate([value[:rows], value[value.shape[0] - rows :]], axis=1)
 
 
-def groups_kernel(core_ref, w_ref, *refs, swapped, last):
-    core = core_ref[0]
-    if last:
-        u0, u1, near, acc_in = refs[:4]
-        mine_ref, other_ref, parcel, f_s, c_s, wd_ref, acc = refs[4:]
-        pairs = [(u0, u1, swapped[0], parcel)]
+def groups_kernel(at_ref, w_ref, *refs, mode):
+    core, mp = at_ref[0], at_ref[1]
+    acc_in = None
+    if mode == "near":
+        near, sources, refs = refs[0], refs[1:9], refs[9:]
+        (acc, pg_ref, parcel_r, parcel_l), refs = refs[:4], refs[4:]
     else:
-        near, sources, refs = refs[0], refs[1:7], refs[7:]
-        (acc, pg_ref, parcel_r, parcel_l), refs = refs[:4], refs[4:]
-        held, (sems, f_s, c_s, wd_ref) = refs[:6], refs[6:]
+        (near, acc_in, f0, f1), sources, refs = refs[:4], (), refs[4:]
+        (mine_ref, other_ref, parcel_f, *refs) = refs
+    copies = []
+    if sources:
+        held, refs = refs[: len(sources)], refs[len(sources) :]
+        sems, *refs = refs
         copies = [
             pltpu.make_async_copy(source, place, sems.at[i])
             for i, (source, place) in enumerate(zip(sources, held))
         ]
         for copy in copies:
             copy.start()
-        f_ref, c_ref, r0, r1, l0, l1 = held
-        acc_in = None
+    f_s, c_s, wd_ref = refs[:3]
+    if mode == "near":
+        r0, l1, shared = held[2], held[3], held[4:]
+        right, left = [(0, r0, 0, HEAD, 0)], [(HEAD, l1, 0, TAIL, HEAD)]
+        for k, part in enumerate(shared):
+            turn = (mp + len(shared) - k) % len(shared)
+            here = FULL + k * QUARTERS
+            right.append((HEAD + turn * STEP, part, 0, STEP, here))
+            left.append((turn * STEP, part, STEP, QUARTERS - STEP, here + STEP))
         pairs = [
-            (None, None, None, pg_ref),
-            (r0, r1, swapped[0], parcel_r),
-            (l0, l1, swapped[1], parcel_l),
+            ((0, 1), None, pg_ref),
+            ((2, 4, 5, 6, 7), right, parcel_r),
+            ((3,), left, parcel_l),
         ]
+    else:
+        acc = refs[3]
+        pairs = [((), [(0, f0, 0, HEAD, 0), (HEAD, f1, 0, TAIL, HEAD)], parcel_f)]
     up_at, down_at = core, 1 - core
     wide = w_ref.shape[1] // 2
     wd_ref[...] = w_ref[:, wide:]
     row = lax.broadcasted_iota(jnp.int32, (HEAD, wide), 0)
     f_s[FULL - 16 : FULL, :] = jnp.zeros((16, D), jnp.bfloat16)
     c_s[FULL - 16 : FULL, :] = jnp.zeros((16, D), jnp.bfloat16)
-    for g, (u0, u1, spots, out) in enumerate(pairs):
-        if not last:
-            copies[2 * g].wait()
-            copies[2 * g + 1].wait()
-        if u0 is None:
-            f_s[0:ROWS, :] = f_ref[...]
-            c_s[0:ROWS, :] = c_ref[...]
+    for g, (needed, pieces, out) in enumerate(pairs):
+        for i in needed:
+            copies[i].wait()
+        if pieces is None:
+            f_s[0:ROWS, :] = held[0][...]
+            c_s[0:ROWS, :] = held[1][...]
             at = [0, HALF]
         else:
-            f_s[0:HEAD, 0:HALF] = u0[:, 0:HALF]
-            f_s[HEAD:ROWS, 0:HALF] = u1[:, 0:HALF]
-            f_s[0:HEAD, HALF:D] = near[spots[0] : spots[0] + HEAD, :]
-            f_s[HEAD:ROWS, HALF:D] = near[spots[1] : spots[1] + TAIL, :]
-            c_s[0:HEAD, :] = u0[:, HALF:]
-            c_s[HEAD:ROWS, :] = u1[:, HALF:]
             at = [pl.multiple_of(a, HALF) for a in (core * HALF, (1 - core) * HALF)]
+            for start, part, low, size, there in pieces:
+                span = pl.ds(start if isinstance(start, int) else pl.multiple_of(start, 16), size)
+                f_s[span, 0:HALF] = part[low : low + size, 0:HALF]
+                f_s[span, HALF:D] = near[there : there + size, :]
+                c_s[span, :] = part[low : low + size, HALF:]
         preact = sum(
             jnp.dot(
                 f_s[:, i * HALF : (i + 1) * HALF],
@@ -135,7 +159,7 @@
         hidden = (preact * cumulative).astype(jnp.bfloat16)
         back = jnp.dot(c_s[...], wd_ref[...], preferred_element_type=jnp.float32)
         pg = (back * (cumulative + preact * density)).astype(jnp.bfloat16)
-        if u0 is None:
+        if pieces is None:
             out[...] = pg[:ROWS]
         else:
             out[0:HALF, :] = pack_lanes(w_ref[:, 0:wide], HALF)
@@ -150,10 +174,10 @@
                 [each[0] + each[1], each[0] * each[0] + each[1] * each[1]], axis=1
             )
             span = pl.ds(at, HALF)
-            if g == 0 and last:
+            if g == 0 and acc_in is None:
+                acc[index, span, :] = total
+            elif g == 0:
                 acc[index, span, :] = acc_in[index, span, :] + total
-            elif g == 0:
-                acc[index, span, :] = total
             else:
                 acc[index, span, :] = acc[index, span, :] + total
 
@@ -164,7 +188,7 @@
             lanes = slice(i * HALF, (i + 1) * HALF)
             add(up_at, at[i], f_s, lanes, by_image[0])
             add(down_at, i * HALF, c_s, lanes, by_image[1])
-    if last:
+    if mode == "far":
         mine_ref[...] = acc[0]
         other_ref[...] = acc[1]
 
@@ -187,28 +211,23 @@
     )(*map(place, parts))
 
 
-def run_groups(core, weights, ins, far_ins, swapped, last):
+def run_groups(mode, at, weights, ins, far_ins):
     wide = weights.shape[1] // 2
     sums = pltpu.VMEM((D, 2 * wide), jnp.float32)
+    every = pltpu.VMEM((2, D, 2 * wide), jnp.float32)
     parcel = pltpu.VMEM((HALF + HEAD, 2 * wide), jnp.bfloat16)
     pair = pltpu.VMEM((FULL, D), jnp.bfloat16)
     scratch = [pltpu.VMEM(a.shape, a.dtype) for a in far_ins]
     if far_ins:
         scratch.append(pltpu.SemaphoreType.DMA((len(far_ins),)))
     scratch += [pair, pair, pltpu.VMEM((D, wide), jnp.bfloat16)]
-    if last:
-        out_shape = [sums, sums, parcel]
+    if mode == "near":
+        out_shape, groups = [every, pltpu.VMEM((ROWS, wide), jnp.bfloat16), parcel, parcel], 3
+    else:
+        out_shape, groups = [sums, sums, parcel], 1
         scratch.append(pltpu.VMEM((2, D, 2 * wide), jnp.float32))
-    else:
-        out_shape = [
-            pltpu.VMEM((2, D, 2 * wide), jnp.float32),
-            pltpu.VMEM((ROWS, wide), jnp.bfloat16),
-            parcel,
-            parcel,
-        ]
-    groups = 1 if last else 3
     return pl.pallas_call(
-        lambda *refs: groups_kernel(*refs, swapped=swapped, last=last),
+        lambda *refs: groups_kernel(*refs, mode=mode),
         out_shape=out_shape,
         in_specs=[SMEM] + [VMEM] * (len(ins) + 1) + [ANY] * len(far_ins),
         out_specs=[VMEM] * len(out_shape),
@@ -219,7 +238,7 @@
             transcendentals=2 * groups * ROWS * wide,
             bytes_accessed=6 << 20,
         ),
-    )(core, inside(weights), *map(inside, ins), *map(outside, far_ins))
+    )(at, inside(weights), *map(inside, ins), *map(outside, far_ins))
 
 
 def input_kernel(at_ref, pg_ref, w_ref, *refs):
@@ -287,22 +306,26 @@
     nz, nx, ny = lax.axis_size("z"), lax.axis_size("x"), lax.axis_size("mp")
     rows, cols = mean_up.shape
     wide = cols // nx
-    core_at = core.reshape(1)
+    mp = lax.axis_index("mp").astype(jnp.int32)
+    at = jnp.stack([core, mp])
     cotangent = out_cotangent[0]
 
-    u0, u1, payload = pl.pallas_call(
+    u0, u1, right, left, payload = pl.pallas_call(
         prepare_kernel,
         out_shape=[
             pltpu.VMEM((HEAD, HALF + D), jnp.bfloat16),
             pltpu.VMEM((TAIL, HALF + D), jnp.bfloat16),
+            pltpu.VMEM((STEP, HALF + D), jnp.bfloat16),
+            pltpu.VMEM((QUARTERS - STEP, HALF + D), jnp.bfloat16),
             pltpu.VMEM((nz, nx, rows, 2 * wide), jnp.bfloat16),
         ],
         in_specs=[SMEM] + [VMEM] * 8,
-        out_specs=[VMEM] * 3,
+        out_specs=[VMEM] * 5,
+        scratch_shapes=[pltpu.VMEM((FULL, HALF + D), jnp.bfloat16)],
         compiler_params=pltpu.CompilerParams(vmem_limit_bytes=16 << 20),
         name="prepare",
     )(
-        core_at,
+        at,
         *[
             pltpu.with_memory_space_constraint(a, pltpu.HBM)
             for a in (
@@ -311,28 +334,38 @@
             )
         ],
     )
+    right = shift(right, "x", 1)
+    left = shift(left, "x", -1)
     r0 = shift(u0, "x", 1)
     l1 = shift(u1, "x", -1)
-    r1 = shift(u1, "x", 1)
-    l0 = shift(u0, "x", -1)
 
     weights = lax.all_to_all(
         payload.reshape(nz * nx, rows, 2 * wide), DP, 0, 0, tiled=True
     ).reshape(D, 2 * wide)
 
+    joined = pl.pallas_call(
+        join_kernel,
+        out_shape=pltpu.VMEM((QUARTERS, HALF + D), jnp.bfloat16),
+        in_specs=[VMEM] * 2,
+        out_specs=VMEM,
+        compiler_params=pltpu.CompilerParams(vmem_limit_bytes=4 << 20),
+        name="join",
+    )(right, left)
+    shared = [joined]
+    for k in range(1, ny):
+        shared.append(shift(joined, "mp", k))
     f0 = shift(r0, "x", 1)
     f1 = shift(l1, "x", -1)
-    near = gathered([r0, l0, r1, l1], outside)
+    near = gathered([r0, l1, *shared], outside)
     near = shift(near, "mc", 1)
-    spots = ((0, 2 * HEAD), (HEAD, HEAD + FULL))
-    far = shift(gathered([f0, f1], inside), "mc", 1)
-
+    far = gathered([f0, f1], inside)
+    far = shift(far, "mc", 1)
     acc, pg, parcel_r, parcel_l = run_groups(
-        core_at, weights, [near], [features, cotangent, r0, r1, l0, l1], spots, False
+        "near", at, weights, [near], [features, cotangent, r0, l1, *shared]
     )
     parcel_r = shift(parcel_r, "x", -1)
     parcel_l = shift(parcel_l, "x", 1)
-    mine, other, parcel_f = run_groups(core_at, weights, [f0, f1, far, acc], [], ((0, HEAD),), True)
+    mine, other, parcel_f = run_groups("far", at, weights, [far, acc, f0, f1], [])
 
     both = mine + shift(other, "mc", 1)
     parcel_f = shift(parcel_f, "x", 2)
@@ -363,7 +396,7 @@
             flops=ROWS * D * cols * 2, transcendentals=0, bytes_accessed=4 << 20
         ),
         name="input_grad",
-    )(lax.axis_index("mp").astype(jnp.int32).reshape(1), *map(inside, (pg, weights, parcel_r, parcel_l, parcel_f)))
+    )(mp.reshape(1), *map(inside, (pg, weights, parcel_r, parcel_l, parcel_f)))
     tiles = [tiles[0]] + [shift(tiles[k], "mp", k) for k in range(1, ny)]
     input_grad = sum(tiles[1:], tiles[0]).astype(jnp.bfloat16)[None]
 

time: 146 us -> 154 us (1.055)
  starting transfers between devices: 51.1 us -> 55.8 us
  waiting for transfers between devices: 71.6 us -> 74.2 us
    ppermute x16 -> x19, starting transfers between devices: 19.6 us -> 23.7 us  [shift(): return lax.ppermute(value, axis, [(i, (i + k) % n) for i in range(n)])]
    ppermute x16 -> x19, waiting for transfers between devices: 63.8 us -> 67.2 us  [shift(): return lax.ppermute(value, axis, [(i, (i + k) % n) for i in range(n)])]
    pallas_call x2 -> x3, Pallas kernels: 7.19 us -> 8.41 us  [the longest x2 8.4 us: run_groups(): pl.pallas_call(lambda *refs: groups_kernel(*refs, mode=mode), out_shape=o...]
    unnamed x27 -> x29, local copies, waits for them, and re-layouts: 3.29 us -> 2.37 us
  transfers between devices with their start and end apart: 19 -> 22, of which waited for: 10 -> 13; matrix products, arithmetic and copies ran while one was open for 2% -> 2% of each run, Pallas kernels for 7% -> 6%
where the time goes in v3:
time: 154 us; the launch traced here: 153 us
  waiting for transfers between devices  74.2 us (48%)
  starting transfers between devices  55.8 us (36%)
  Pallas kernels  15.5 us (10%)
  other arithmetic  4.13 us (3%)
  local copies, waits for them, and re-layouts  2.37 us (2%)
    ppermute x19, waiting for transfers between devices, shift(): return lax.ppermute(value, axis, [(i, (i + k) % n) for i in range(n)])  67.2 us
    ppermute x19, starting transfers between devices, shift(): return lax.ppermute(value, axis, [(i, (i + k) % n) for i in range(n)])  23.7 us
    all_to_all x1, starting transfers between devices, shards(): lax.all_to_all(payload.reshape(nz * nx, rows, 2 * wide), DP, 0, 0, tiled=...  11.6 us
    all_to_all x1, starting transfers between devices, shards(): everyone = lax.all_to_all(local, ZXY, 0, 0, tiled=True)  10.5 us
    all_to_all x1, starting transfers between devices, shards(): lax.all_to_all(packed.reshape(nz * nx, rows, 2 * wide), DP, 0, 0, tiled=T...  10.1 us
    pallas_call x2, Pallas kernels, run_groups(): pl.pallas_call(lambda *refs: groups_kernel(*refs, mode=mode), out_shape=o...  8.4 us
    all_to_all x1, waiting for transfers between devices, shards(): everyone = lax.all_to_all(local, ZXY, 0, 0, tiled=True)  6.97 us
  transfers between devices with their start and end apart: 22, of which 13 were waited for; matrix products, arithmetic and copies ran while one was open for 2% of the time, Pallas kernels for 6%

profile of v3, /device:TPU:2, one launch (start us, length us, event | category | flops | bytes accessed | tf_op | source)
XLA Modules:
  0.0 152.8 jit_solution(4341280752033946133)
XLA Ops:
  0.7 2.5 %prepare.1 = (bf16[208,1152]{1,0:T(8,128)(2,1)S(1)}, bf16[186,1152]{1,0:T(8,128)(2,1)S(1)}, bf16[48,1152]{1,0:T(8,128)(2,1)S(1)}, bf16[64,1152]{1,0:T(8,128)(2,1)S(1)}, bf16[8,4,24,384]{3,2,1,0:T(8,128)(2,1)}) custom-call(s32[2]{0:T(128)S(1)} %pad_add_fusion.at_ref.refs_0_, bf16[394,768]{1,0:T(8,128)(2,1)} %refs_3_.2, bf16[394,768]{1,0:T(8,128)(2,1)} %bitcast.15, ...), custom_call_target="tpu_custom_call" | custom-call | tf_op jit(solution)/shard_map/prepare/pallas_call | solution.py:313
  3.2 11.6 %all-to-all-start = ((bf16[32,24,384]{2,1,0:T(8,128)(2,1)}), bf16[32,24,384]{2,1,0:T(8,128)(2,1)S(1)}, u32[]{:S(2)}, u32[]{:S(2)}) async-start(bf16[32,24,384]{2,1,0:T(8,128)(2,1)} %bitcast.5), calls=%async_computation | async-start | bytes 1179648 | tf_op jit(solution)/shard_map/all_to_all | solution.py:342
  14.8 1.5 %collective-permute-start = (bf16[208,1152]{1,0:T(8,128)(2,1)S(1)}, bf16[208,1152]{1,0:T(8,128)(2,1)S(1)}, u32[]{:S(2)}, u32[]{:S(2)}) collective-permute-start(bf16[208,1152]{1,0:T(8,128)(2,1)S(1)} %get-tuple-element.29), channel_id=1, source_target_pairs={{0,8},{8,16},{16,24},{24,0},{1,9},{9,17},{17,25},{25,1},{2,10},{10... | collective-permute-start | bytes 1437704 | tf_op jit(solution)/shard_map/ppermute | solution.py:40
  16.3 0.6 collective-permute-start.2
  16.9 1.4 collective-permute-start.6
  18.4 0.6 collective-permute-start.5
  18.9 16.1 %collective-permute-done.5.right_ref = bf16[48,1152]{1,0:T(8,128)(2,1)S(1)} collective-permute-done((bf16[48,1152]{1,0:T(8,128)(2,1)S(1)}, bf16[48,1152]{1,0:T(8,128)(2,1)S(1)}, u32[]{:S(2)}, u32[]{:S(2)}) %collective-permute-start.5) | collective-permute-done | bytes 110624 | tf_op jit(solution)/shard_map/ppermute | solution.py:40
  35.0 1.4 collective-permute-done.6.left_ref
  36.5 1.7 %collective-permute-start.7 = (bf16[112,1152]{1,0:T(8,128)(2,1)S(1)}, bf16[112,1152]{1,0:T(8,128)(2,1)S(1)}, u32[]{:S(2)}, u32[]{:S(2)}) collective-permute-start(bf16[112,1152]{1,0:T(8,128)(2,1)S(1)} %join.1.refs_2_.refs_7_), channel_id=1, source_target_pairs={{0,2},{2,4},{4,6},{6,0},{1,3},{3,5},{5,7},{7,1},{8,10},{10,12},{12... | collective-permute-start | bytes 774152 | tf_op jit(solution)/shard_map/ppermute | solution.py:40
  38.2 2.9 %collective-permute-start.8 = (bf16[112,1152]{1,0:T(8,128)(2,1)S(1)}, bf16[112,1152]{1,0:T(8,128)(2,1)S(1)}, u32[]{:S(2)}, u32[]{:S(2)}) collective-permute-start(bf16[112,1152]{1,0:T(8,128)(2,1)S(1)} %join.1.refs_2_.refs_7_), channel_id=1, source_target_pairs={{0,4},{2,6},{4,0},{6,2},{1,5},{3,7},{5,1},{7,3},{8,12},{10,14},{12... | collective-permute-start | bytes 774152 | tf_op jit(solution)/shard_map/ppermute | solution.py:40
  41.1 1.3 collective-permute-start.9
  42.4 1.1 collective-permute-start.1
  43.6 2.2 %collective-permute-done.7.refs_3_.refs_8_ = bf16[112,1152]{1,0:T(8,128)(2,1)S(1)} collective-permute-done((bf16[112,1152]{1,0:T(8,128)(2,1)S(1)}, bf16[112,1152]{1,0:T(8,128)(2,1)S(1)}, u32[]{:S(2)}, u32[]{:S(2)}) %collective-permute-start.7) | collective-permute-done | bytes 258080 | tf_op jit(solution)/shard_map/ppermute | solution.py:40
  45.8 6.0 %collective-permute-done.8.refs_4_.refs_9_ = bf16[112,1152]{1,0:T(8,128)(2,1)S(1)} collective-permute-done((bf16[112,1152]{1,0:T(8,128)(2,1)S(1)}, bf16[112,1152]{1,0:T(8,128)(2,1)S(1)}, u32[]{:S(2)}, u32[]{:S(2)}) %collective-permute-start.8) | collective-permute-done | bytes 258080 | tf_op jit(solution)/shard_map/ppermute | solution.py:40
  51.8 0.6 copy-done.12
  52.5 0.1 copy-done.13
  52.6 0.8 copy-done.10
  53.3 1.6 %shard_map.120 = bf16[848,384]{1,0:T(8,128)(2,1)S(1)} custom-call(bf16[208,1152]{1,0:T(8,128)(2,1)} %copy-done.9, bf16[186,1152]{1,0:T(8,128)(2,1)} %copy-done.10, bf16[112,1152]{1,0:T(8,128)(2,1)} %copy-done, bf16[112,1152]{1,0:T(8,128)(2,1)} %copy-done.11, bf16[112,1152]{1,0:T(8,128)(2,1)} %copy-done.12, bf16[112,1152]{1,0:T(8,128)(2,1)} %copy-done.13), custom_call_target="tpu_custom_call" | custom-call | tf_op jit(solution)/shard_map/pallas_call | solution.py:205
  55.0 0.9 collective-permute-start.3
  55.9 11.9 %collective-permute-done.3.refs_1_.refs_5_ = bf16[186,1152]{1,0:T(8,128)(2,1)S(1)} collective-permute-done((bf16[186,1152]{1,0:T(8,128)(2,1)}, bf16[186,1152]{1,0:T(8,128)(2,1)S(1)}, u32[]{:S(2)}, u32[]{:S(2)}) %collective-permute-start.3) | collective-permute-done | bytes 428576 | tf_op jit(solution)/shard_map/ppermute | solution.py:40
  67.8 0.3 collective-permute-start.4
  68.1 6.2 %shard_map.121 = (f32[2,768,384]{2,1,0:T(8,128)S(1)}, bf16[394,192]{1,0:T(8,128)(2,1)S(1)}, bf16[592,384]{1,0:T(8,128)(2,1)S(1)}, bf16[592,384]{1,0:T(8,128)(2,1)S(1)}) custom-call(s32[2]{0:T(128)S(1)} %pad_add_fusion.at_ref.refs_0_, bf16[768,384]{1,0:T(8,128)(2,1)S(1)} %bitcast.12, bf16[848,384]{1,0:T(8,128)(2,1)S(1)} %collective-permute-done.10.refs_2_, ...), custom_call_target="tpu_custom_call" | custom-call | flops 1394343936 | bytes 6291456 | tf_op jit(solution)/shard_map/pallas_call | solution.py:229
  74.3 2.2 %shard_map.122 = (f32[768,384]{1,0:T(8,128)S(1)}, f32[768,384]{1,0:T(8,128)S(1)}, bf16[592,384]{1,0:T(8,128)(2,1)S(1)}) custom-call(s32[2]{0:T(128)S(1)} %pad_add_fusion.at_ref.refs_0_, bf16[768,384]{1,0:T(8,128)(2,1)S(1)} %bitcast.13, bf16[400,384]{1,0:T(8,128)(2,1)S(1)} %collective-permute-done.4.refs_2_, f32[2,768,384]{2,1,0:T(8,128)S(1)} %get-tuple-element.33.refs_3_, ...), custom_call_target="tpu_custom_call" | custom-call | flops 464781312 | bytes 6291456 | tf_op jit(solution)/shard_map/pallas_call | solution.py:229
  76.6 0.6 collective-permute-start.11
  77.1 2.5 %collective-permute-done.11 = f32[768,384]{1,0:T(8,128)S(1)} collective-permute-done((f32[768,384]{1,0:T(8,128)S(1)}, f32[768,384]{1,0:T(8,128)S(1)}, u32[]{:S(2)}, u32[]{:S(2)}) %collective-permute-start.11) | collective-permute-done | bytes 1179680 | tf_op jit(solution)/shard_map/ppermute | solution.py:40
  79.6 1.4 fusion
  81.1 10.1 %all-to-all-start.1 = ((f16[32,24,384]{2,1,0:T(8,128)(2,1)}), f16[32,24,384]{2,1,0:T(8,128)(2,1)}, u32[]{:S(2)}, u32[]{:S(2)}) async-start(f16[32,24,384]{2,1,0:T(8,128)(2,1)} %bitcast.7), calls=%async_computation.1 | async-start | bytes 1179648 | tf_op jit(solution)/shard_map/all_to_all | solution.py:375
  91.1 0.4 collective-permute-start.13
  91.5 1.7 %collective-permute-start.14 = (bf16[592,384]{1,0:T(8,128)(2,1)S(1)}, bf16[592,384]{1,0:T(8,128)(2,1)S(1)}, u32[]{:S(2)}, u32[]{:S(2)}) collective-permute-start(bf16[592,384]{1,0:T(8,128)(2,1)S(1)} %get-tuple-element.45), channel_id=1, source_target_pairs={{0,8},{8,16},{16,24},{24,0},{1,9},{9,17},{17,25},{25,1},{2,10},{10... | collective-permute-start | bytes 1363976 | tf_op jit(solution)/shard_map/ppermute | solution.py:40
  93.3 3.3 %collective-permute-start.15 = (bf16[592,384]{1,0:T(8,128)(2,1)S(1)}, bf16[592,384]{1,0:T(8,128)(2,1)S(1)}, u32[]{:S(2)}, u32[]{:S(2)}) collective-permute-start(bf16[592,384]{1,0:T(8,128)(2,1)S(1)} %copy-done.8), channel_id=1, source_target_pairs={{0,16},{8,24},{16,0},{24,8},{1,17},{9,25},{17,1},{25,9},{2,18},{10... | collective-permute-start | bytes 1363976 | tf_op jit(solution)/shard_map/ppermute | solution.py:40
  96.5 13.0 %collective-permute-done.13.refs_0_ = bf16[592,384]{1,0:T(8,128)(2,1)S(1)} collective-permute-done((bf16[592,384]{1,0:T(8,128)(2,1)S(1)}, bf16[592,384]{1,0:T(8,128)(2,1)S(1)}, u32[]{:S(2)}, u32[]{:S(2)}) %collective-permute-start.13) | collective-permute-done | bytes 454688 | tf_op jit(solution)/shard_map/ppermute | solution.py:40
  109.5 1.0 collective-permute-done.14.refs_1_
  110.5 9.5 %collective-permute-done.15.refs_2_ = bf16[592,384]{1,0:T(8,128)(2,1)S(1)} collective-permute-done((bf16[592,384]{1,0:T(8,128)(2,1)S(1)}, bf16[592,384]{1,0:T(8,128)(2,1)S(1)}, u32[]{:S(2)}, u32[]{:S(2)}) %collective-permute-start.15) | collective-permute-done | bytes 454688 | tf_op jit(solution)/shard_map/ppermute | solution.py:40
  119.9 1.3 input_grad.1
  121.2 1.2 collective-permute-start.16
  122.4 2.4 %collective-permute-start.17 = (f32[394,192]{1,0:T(8,128)S(1)}, f32[394,192]{1,0:T(8,128)}, u32[]{:S(2)}, u32[]{:S(2)}) collective-permute-start(f32[394,192]{1,0:T(8,128)S(1)} %get-tuple-element.49), channel_id=1, source_target_pairs={{0,4},{2,6},{4,0},{6,2},{1,5},{3,7},{5,1},{7,3},{8,12},{10,14},{12... | collective-permute-start | bytes 907784 | tf_op jit(solution)/shard_map/ppermute | solution.py:40
  124.8 1.6 %collective-permute-start.18 = (f32[394,192]{1,0:T(8,128)S(1)}, f32[394,192]{1,0:T(8,128)}, u32[]{:S(2)}, u32[]{:S(2)}) collective-permute-start(f32[394,192]{1,0:T(8,128)S(1)} %get-tuple-element.50), channel_id=1, source_target_pairs={{0,6},{2,0},{4,2},{6,4},{1,7},{3,1},{5,3},{7,5},{8,14},{10,8},{12,... | collective-permute-start | bytes 907784 | tf_op jit(solution)/shard_map/ppermute | solution.py:40
  126.4 1.4 fusion.3.refs_1_
  127.8 0.1 collective-permute-start.12
  127.9 1.4 collective-permute-done.12.refs_2_
  129.3 0.8 statistics.1
  130.1 10.5 %all-to-all-start.2 = ((f32[128,1,128]{2,1,0:T(1,128)}), f32[128,1,128]{2,1,0:T(1,128)S(1)}, u32[]{:S(2)}, u32[]{:S(2)}) async-start(f32[128,1,128]{2,1,0:T(1,128)} %get-tuple-element.36), calls=%async_computation.2 | async-start | bytes 131072 | tf_op jit(solution)/shard_map/all_to_all | solution.py:414
  140.6 2.0 %collective-permute-done.17 = f32[394,192]{1,0:T(8,128)} collective-permute-done((f32[394,192]{1,0:T(8,128)S(1)}, f32[394,192]{1,0:T(8,128)}, u32[]{:S(2)}, u32[]{:S(2)}) %collective-permute-start.17) | collective-permute-done | bytes 302624 | tf_op jit(solution)/shard_map/ppermute | solution.py:40
  142.5 0.3 collective-permute-done.18
  142.9 1.2 fusion.5
  144.1 0.8 copy.13
  144.9 7.0 %all-to-all-done.2.sum_ref = f32[128,1,128]{2,1,0:T(1,128)S(1)} async-done(((f32[128,1,128]{2,1,0:T(1,128)}), f32[128,1,128]{2,1,0:T(1,128)S(1)}, u32[]{:S(2)}, u32[]{:S(2)}) %all-to-all-start.2) | async-done | bytes 65568 | tf_op jit(solution)/shard_map/all_to_all | solution.py:414
  151.9 0.9 update.1
  (40 shorter events, 0.3 us)
Async XLA Ops:
  3.2 64.9 %all-to-all-start = ((bf16[32,24,384]{2,1,0:T(8,128)(2,1)}), bf16[32,24,384]{2,1,0:T(8,128)(2,1)S(1)}, u32[]{:S(2)}, u32[]{:S(2)}) async-start(bf16[32,24,384]{2,1,0:T(8,128)(2,1)} %bitcast.5), calls=%async_computation | async-start | bytes 1179648 | tf_op jit(solution)/shard_map/all_to_all | solution.py:342
  14.8 27.6 %collective-permute-start = (bf16[208,1152]{1,0:T(8,128)(2,1)S(1)}, bf16[208,1152]{1,0:T(8,128)(2,1)S(1)}, u32[]{:S(2)}, u32[]{:S(2)}) collective-permute-start(bf16[208,1152]{1,0:T(8,128)(2,1)S(1)} %get-tuple-element.29), channel_id=1, source_target_pairs={{0,8},{8,16},{16,24},{24,0},{1,9},{9,17},{17,25},{25,1},{2,10},{10... | collective-permute-start | bytes 1437704 | tf_op jit(solution)/shard_map/ppermute | solution.py:40
  16.3 35.4 %collective-permute-start.2 = (bf16[186,1152]{1,0:T(8,128)(2,1)S(1)}, bf16[186,1152]{1,0:T(8,128)(2,1)S(1)}, u32[]{:S(2)}, u32[]{:S(2)}) collective-permute-start(bf16[186,1152]{1,0:T(8,128)(2,1)S(1)} %get-tuple-element.30), channel_id=1, source_target_pairs={{0,24},{8,0},{16,8},{24,16},{1,25},{9,1},{17,9},{25,17},{2,26},{10... | collective-permute-start | bytes 1285640 | tf_op jit(solution)/shard_map/ppermute | solution.py:40
  16.9 19.6 %collective-permute-start.6 = (bf16[64,1152]{1,0:T(8,128)(2,1)S(1)}, bf16[64,1152]{1,0:T(8,128)(2,1)S(1)}, u32[]{:S(2)}, u32[]{:S(2)}) collective-permute-start(bf16[64,1152]{1,0:T(8,128)(2,1)S(1)} %get-tuple-element.32), channel_id=1, source_target_pairs={{0,24},{8,0},{16,8},{24,16},{1,25},{9,1},{17,9},{25,17},{2,26},{10... | collective-permute-start | bytes 442376 | tf_op jit(solution)/shard_map/ppermute | solution.py:40
  18.4 16.7 %collective-permute-start.5 = (bf16[48,1152]{1,0:T(8,128)(2,1)S(1)}, bf16[48,1152]{1,0:T(8,128)(2,1)S(1)}, u32[]{:S(2)}, u32[]{:S(2)}) collective-permute-start(bf16[48,1152]{1,0:T(8,128)(2,1)S(1)} %get-tuple-element.31), channel_id=1, source_target_pairs={{0,8},{8,16},{16,24},{24,0},{1,9},{9,17},{17,25},{25,1},{2,10},{10... | collective-permute-start | bytes 331784 | tf_op jit(solution)/shard_map/ppermute | solution.py:40
  36.5 15.3 %copy-start = (bf16[112,1152]{1,0:T(8,128)(2,1)}, bf16[112,1152]{1,0:T(8,128)(2,1)S(1)}, u32[]{:S(2)}) copy-start(bf16[112,1152]{1,0:T(8,128)(2,1)S(1)} %join.1.refs_2_.refs_7_) | copy-start | bytes 774148
  36.5 9.3 %collective-permute-start.7 = (bf16[112,1152]{1,0:T(8,128)(2,1)S(1)}, bf16[112,1152]{1,0:T(8,128)(2,1)S(1)}, u32[]{:S(2)}, u32[]{:S(2)}) collective-permute-start(bf16[112,1152]{1,0:T(8,128)(2,1)S(1)} %join.1.refs_2_.refs_7_), channel_id=1, source_target_pairs={{0,2},{2,4},{4,6},{6,0},{1,3},{3,5},{5,7},{7,1},{8,10},{10,12},{12... | collective-permute-start | bytes 774152 | tf_op jit(solution)/shard_map/ppermute | solution.py:40
  38.2 13.6 %collective-permute-start.8 = (bf16[112,1152]{1,0:T(8,128)(2,1)S(1)}, bf16[112,1152]{1,0:T(8,128)(2,1)S(1)}, u32[]{:S(2)}, u32[]{:S(2)}) collective-permute-start(bf16[112,1152]{1,0:T(8,128)(2,1)S(1)} %join.1.refs_2_.refs_7_), channel_id=1, source_target_pairs={{0,4},{2,6},{4,0},{6,2},{1,5},{3,7},{5,1},{7,3},{8,12},{10,14},{12... | collective-permute-start | bytes 774152 | tf_op jit(solution)/shard_map/ppermute | solution.py:40
  41.1 10.7 %collective-permute-start.9 = (bf16[112,1152]{1,0:T(8,128)(2,1)S(1)}, bf16[112,1152]{1,0:T(8,128)(2,1)S(1)}, u32[]{:S(2)}, u32[]{:S(2)}) collective-permute-start(bf16[112,1152]{1,0:T(8,128)(2,1)S(1)} %join.1.refs_2_.refs_7_), channel_id=1, source_target_pairs={{0,6},{2,0},{4,2},{6,4},{1,7},{3,1},{5,3},{7,5},{8,14},{10,8},{12,... | collective-permute-start | bytes 774152 | tf_op jit(solution)/shard_map/ppermute | solution.py:40
  42.4 9.3 %copy-start.9 = (bf16[208,1152]{1,0:T(8,128)(2,1)}, bf16[208,1152]{1,0:T(8,128)(2,1)S(1)}, u32[]{:S(2)}) copy-start(bf16[208,1152]{1,0:T(8,128)(2,1)S(1)} %collective-permute-done.refs_0_.refs_5_) | copy-start | bytes 1437700
  42.4 25.3 %collective-permute-start.1 = (bf16[208,1152]{1,0:T(8,128)(2,1)S(1)}, bf16[208,1152]{1,0:T(8,128)(2,1)S(1)}, u32[]{:S(2)}, u32[]{:S(2)}) collective-permute-start(bf16[208,1152]{1,0:T(8,128)(2,1)S(1)} %collective-permute-done.refs_0_.refs_5_), channel_id=1, source_target_pairs={{0,8},{8,16},{16,24},{24,0},{1,9},{9,17},{17,25},{25,1},{2,10},{10... | collective-permute-start | bytes 1437704 | tf_op jit(solution)/shard_map/ppermute | solution.py:40
  45.8 6.0 %copy-start.11 = (bf16[112,1152]{1,0:T(8,128)(2,1)}, bf16[112,1152]{1,0:T(8,128)(2,1)S(1)}, u32[]{:S(2)}) copy-start(bf16[112,1152]{1,0:T(8,128)(2,1)S(1)} %collective-permute-done.7.refs_3_.refs_8_) | copy-start | bytes 774148
  51.8 0.7 copy-start.12
  51.8 0.8 copy-start.13
  52.6 0.8 copy-start.10
  54.9 13.2 %collective-permute-start.10 = (bf16[848,384]{1,0:T(8,128)(2,1)S(1)}, bf16[848,384]{1,0:T(8,128)(2,1)S(1)}, u32[]{:S(2)}, u32[]{:S(2)}) collective-permute-start(bf16[848,384]{1,0:T(8,128)(2,1)S(1)} %shard_map.120), channel_id=1, source_target_pairs={{0,1},{1,0},{2,3},{3,2},{4,5},{5,4},{6,7},{7,6},{8,9},{9,8},{10,11... | collective-permute-start | bytes 1953800 | tf_op jit(solution)/shard_map/ppermute | solution.py:40
  55.0 12.8 %collective-permute-start.3 = (bf16[186,1152]{1,0:T(8,128)(2,1)}, bf16[186,1152]{1,0:T(8,128)(2,1)S(1)}, u32[]{:S(2)}, u32[]{:S(2)}) collective-permute-start(bf16[186,1152]{1,0:T(8,128)(2,1)} %copy-done.10), channel_id=1, source_target_pairs={{0,24},{8,0},{16,8},{24,16},{1,25},{9,1},{17,9},{25,17},{2,26},{10... | collective-permute-start | bytes 1285640 | tf_op jit(solution)/shard_map/ppermute | solution.py:40
  67.8 6.5 %collective-permute-start.4 = (bf16[400,384]{1,0:T(8,128)(2,1)S(1)}, bf16[400,384]{1,0:T(8,128)(2,1)S(1)}, u32[]{:S(2)}, u32[]{:S(2)}) collective-permute-start(bf16[400,384]{1,0:T(8,128)(2,1)S(1)} %shard_map.119), channel_id=1, source_target_pairs={{0,1},{1,0},{2,3},{3,2},{4,5},{5,4},{6,7},{7,6},{8,9},{9,8},{10,11... | collective-permute-start | bytes 921608 | tf_op jit(solution)/shard_map/ppermute | solution.py:40
  74.3 2.3 %copy-start.5 = (bf16[592,384]{1,0:T(8,128)(2,1)}, bf16[592,384]{1,0:T(8,128)(2,1)S(1)}, u32[]{:S(2)}) copy-start(bf16[592,384]{1,0:T(8,128)(2,1)S(1)} %get-tuple-element.44) | copy-start | bytes 1363972
  76.6 4.5 %copy-start.7 = (bf16[592,384]{1,0:T(8,128)(2,1)}, bf16[592,384]{1,0:T(8,128)(2,1)S(1)}, u32[]{:S(2)}) copy-start(bf16[592,384]{1,0:T(8,128)(2,1)S(1)} %get-tuple-element.46) | copy-start | bytes 1363972
  76.6 3.0 %collective-permute-start.11 = (f32[768,384]{1,0:T(8,128)S(1)}, f32[768,384]{1,0:T(8,128)S(1)}, u32[]{:S(2)}, u32[]{:S(2)}) collective-permute-start(f32[768,384]{1,0:T(8,128)S(1)} %get-tuple-element.35), channel_id=1, source_target_pairs={{0,1},{1,0},{2,3},{3,2},{4,5},{5,4},{6,7},{7,6},{8,9},{9,8},{10,11... | collective-permute-start | bytes 3538952 | tf_op jit(solution)/shard_map/ppermute | solution.py:40
  81.0 10.1 %copy-start.6 = (bf16[592,384]{1,0:T(8,128)(2,1)S(1)}, bf16[592,384]{1,0:T(8,128)(2,1)}, u32[]{:S(2)}) copy-start(bf16[592,384]{1,0:T(8,128)(2,1)} %copy-done.5) | copy-start | bytes 1363972
  81.1 12.2 %copy-start.8 = (bf16[592,384]{1,0:T(8,128)(2,1)S(1)}, bf16[592,384]{1,0:T(8,128)(2,1)}, u32[]{:S(2)}) copy-start(bf16[592,384]{1,0:T(8,128)(2,1)} %copy-done.7) | copy-start | bytes 1363972
  81.1 45.4 %all-to-all-start.1 = ((f16[32,24,384]{2,1,0:T(8,128)(2,1)}), f16[32,24,384]{2,1,0:T(8,128)(2,1)}, u32[]{:S(2)}, u32[]{:S(2)}) async-start(f16[32,24,384]{2,1,0:T(8,128)(2,1)} %bitcast.7), calls=%async_computation.1 | async-start | bytes 1179648 | tf_op jit(solution)/shard_map/all_to_all | solution.py:375
  91.1 18.4 %collective-permute-start.13 = (bf16[592,384]{1,0:T(8,128)(2,1)S(1)}, bf16[592,384]{1,0:T(8,128)(2,1)S(1)}, u32[]{:S(2)}, u32[]{:S(2)}) collective-permute-start(bf16[592,384]{1,0:T(8,128)(2,1)S(1)} %copy-done.6), channel_id=1, source_target_pairs={{0,24},{8,0},{16,8},{24,16},{1,25},{9,1},{17,9},{25,17},{2,26},{10... | collective-permute-start | bytes 1363976 | tf_op jit(solution)/shard_map/ppermute | solution.py:40
  91.5 18.9 %collective-permute-start.14 = (bf16[592,384]{1,0:T(8,128)(2,1)S(1)}, bf16[592,384]{1,0:T(8,128)(2,1)S(1)}, u32[]{:S(2)}, u32[]{:S(2)}) collective-permute-start(bf16[592,384]{1,0:T(8,128)(2,1)S(1)} %get-tuple-element.45), channel_id=1, source_target_pairs={{0,8},{8,16},{16,24},{24,0},{1,9},{9,17},{17,25},{25,1},{2,10},{10... | collective-permute-start | bytes 1363976 | tf_op jit(solution)/shard_map/ppermute | solution.py:40
  93.3 26.7 %collective-permute-start.15 = (bf16[592,384]{1,0:T(8,128)(2,1)S(1)}, bf16[592,384]{1,0:T(8,128)(2,1)S(1)}, u32[]{:S(2)}, u32[]{:S(2)}) collective-permute-start(bf16[592,384]{1,0:T(8,128)(2,1)S(1)} %copy-done.8), channel_id=1, source_target_pairs={{0,16},{8,24},{16,0},{24,8},{1,17},{9,25},{17,1},{25,9},{2,18},{10... | collective-permute-start | bytes 1363976 | tf_op jit(solution)/shard_map/ppermute | solution.py:40
  119.9 9.3 %copy-start.1 = (f32[24,768]{1,0:T(8,128)S(1)}, f32[24,768]{1,0:T(8,128)}, u32[]{:S(2)}) copy-start(f32[24,768]{1,0:T(8,128)} %refs_3_.3) | copy-start | bytes 221188
  119.9 9.3 %copy-start.2 = (f32[24,768]{1,0:T(8,128)S(1)}, f32[24,768]{1,0:T(8,128)}, u32[]{:S(2)}) copy-start(f32[24,768]{1,0:T(8,128)} %refs_4_.1) | copy-start | bytes 221188
  121.2 19.3 %collective-permute-start.16 = (f32[394,192]{1,0:T(8,128)S(1)}, f32[394,192]{1,0:T(8,128)S(1)}, u32[]{:S(2)}, u32[]{:S(2)}) collective-permute-start(f32[394,192]{1,0:T(8,128)S(1)} %get-tuple-element.48), channel_id=1, source_target_pairs={{0,2},{2,4},{4,6},{6,0},{1,3},{3,5},{5,7},{7,1},{8,10},{10,12},{12... | collective-permute-start | bytes 907784 | tf_op jit(solution)/shard_map/ppermute | solution.py:40
  122.4 20.1 %collective-permute-start.17 = (f32[394,192]{1,0:T(8,128)S(1)}, f32[394,192]{1,0:T(8,128)}, u32[]{:S(2)}, u32[]{:S(2)}) collective-permute-start(f32[394,192]{1,0:T(8,128)S(1)} %get-tuple-element.49), channel_id=1, source_target_pairs={{0,4},{2,6},{4,0},{6,2},{1,5},{3,7},{5,1},{7,3},{8,12},{10,14},{12... | collective-permute-start | bytes 907784 | tf_op jit(solution)/shard_map/ppermute | solution.py:40
  124.8 18.0 %collective-permute-start.18 = (f32[394,192]{1,0:T(8,128)S(1)}, f32[394,192]{1,0:T(8,128)}, u32[]{:S(2)}, u32[]{:S(2)}) collective-permute-start(f32[394,192]{1,0:T(8,128)S(1)} %get-tuple-element.50), channel_id=1, source_target_pairs={{0,6},{2,0},{4,2},{6,4},{1,7},{3,1},{5,3},{7,5},{8,14},{10,8},{12,... | collective-permute-start | bytes 907784 | tf_op jit(solution)/shard_map/ppermute | solution.py:40
  127.8 1.5 collective-permute-start.12
  130.1 21.8 %copy-start.3 = (f32[24,768]{1,0:T(8,128)S(1)}, f32[24,768]{1,0:T(8,128)}, u32[]{:S(2)}) copy-start(f32[24,768]{1,0:T(8,128)} %mu_ref.3) | copy-start | bytes 221188
  130.1 21.8 %copy-start.4 = (f32[24,768]{1,0:T(8,128)S(1)}, f32[24,768]{1,0:T(8,128)}, u32[]{:S(2)}) copy-start(f32[24,768]{1,0:T(8,128)} %md_ref.3) | copy-start | bytes 221188
  130.1 21.8 %all-to-all-start.2 = ((f32[128,1,128]{2,1,0:T(1,128)}), f32[128,1,128]{2,1,0:T(1,128)S(1)}, u32[]{:S(2)}, u32[]{:S(2)}) async-start(f32[128,1,128]{2,1,0:T(1,128)} %get-tuple-element.36), calls=%async_computation.2 | async-start | bytes 131072 | tf_op jit(solution)/shard_map/all_to_all | solution.py:414

commit v4 on v3

--- a/solution.py
+++ b/solution.py
@@ -94,7 +94,7 @@
     core, mp = at_ref[0], at_ref[1]
     acc_in = None
     if mode == "near":
-        near, sources, refs = refs[0], refs[1:9], refs[9:]
+        sources, refs = refs[:9], refs[9:]
         (acc, pg_ref, parcel_r, parcel_l), refs = refs[:4], refs[4:]
     else:
         (near, acc_in, f0, f1), sources, refs = refs[:4], (), refs[4:]
@@ -111,7 +111,8 @@
             copy.start()
     f_s, c_s, wd_ref = refs[:3]
     if mode == "near":
-        r0, l1, shared = held[2], held[3], held[4:]
+        f_ref, c_ref, near, r0, l1 = held[:5]
+        shared = held[5:]
         right, left = [(0, r0, 0, HEAD, 0)], [(HEAD, l1, 0, TAIL, HEAD)]
         for k, part in enumerate(shared):
             turn = (mp + len(shared) - k) % len(shared)
@@ -120,8 +121,8 @@
             left.append((turn * STEP, part, STEP, QUARTERS - STEP, here + STEP))
         pairs = [
             ((0, 1), None, pg_ref),
-            ((2, 4, 5, 6, 7), right, parcel_r),
-            ((3,), left, parcel_l),
+            ((2, 3, 5, 6, 7, 8), right, parcel_r),
+            ((4,), left, parcel_l),
         ]
     else:
         acc = refs[3]
@@ -136,8 +137,8 @@
         for i in needed:
             copies[i].wait()
         if pieces is None:
-            f_s[0:ROWS, :] = held[0][...]
-            c_s[0:ROWS, :] = held[1][...]
+            f_s[0:ROWS, :] = f_ref[...]
+            c_s[0:ROWS, :] = c_ref[...]
             at = [0, HALF]
         else:
             at = [pl.multiple_of(a, HALF) for a in (core * HALF, (1 - core) * HALF)]
@@ -201,14 +202,14 @@
     return pltpu.with_memory_space_constraint(array, pltpu.HBM)
 
 
-def gathered(parts, place):
+def gathered(parts, places):
     return pl.pallas_call(
         gather_kernel,
         out_shape=pltpu.VMEM((sum(-(-p.shape[0] // 16) * 16 for p in parts), HALF), jnp.bfloat16),
         in_specs=[VMEM] * len(parts),
         out_specs=VMEM,
         compiler_params=pltpu.CompilerParams(vmem_limit_bytes=4 << 20),
-    )(*map(place, parts))
+    )(*[place(p) for place, p in zip(places, parts)])
 
 
 def run_groups(mode, at, weights, ins, far_ins):
@@ -356,12 +357,12 @@
         shared.append(shift(joined, "mp", k))
     f0 = shift(r0, "x", 1)
     f1 = shift(l1, "x", -1)
-    near = gathered([r0, l1, *shared], outside)
+    near = gathered([r0, l1, *shared], [outside] * 2 + [inside] * ny)
     near = shift(near, "mc", 1)
-    far = gathered([f0, f1], inside)
+    far = gathered([f0, f1], [inside] * 2)
     far = shift(far, "mc", 1)
     acc, pg, parcel_r, parcel_l = run_groups(
-        "near", at, weights, [near], [features, cotangent, r0, l1, *shared]
+        "near", at, weights, [], [features, cotangent, near, r0, l1, *shared]
     )
     parcel_r = shift(parcel_r, "x", -1)
     parcel_l = shift(parcel_l, "x", 1)
@@ -396,7 +397,7 @@
             flops=ROWS * D * cols * 2, transcendentals=0, bytes_accessed=4 << 20
         ),
         name="input_grad",
-    )(mp.reshape(1), *map(inside, (pg, weights, parcel_r, parcel_l, parcel_f)))
+    )(mp.reshape(1), inside(pg), inside(weights), outside(parcel_r), outside(parcel_l), inside(parcel_f))
     tiles = [tiles[0]] + [shift(tiles[k], "mp", k) for k in range(1, ny)]
     input_grad = sum(tiles[1:], tiles[0]).astype(jnp.bfloat16)[None]
 

time: 154 us -> 155 us (level)
  transfers between devices with their start and end apart: 22 -> 22, of which waited for: 13 -> 13; matrix products, arithmetic and copies ran while one was open for 2% -> 2% of each run, Pallas kernels for 6% -> 7%
where the time goes in v4:
time: 155 us; the launch traced here: 154 us
  waiting for transfers between devices  74.1 us (48%)
  starting transfers between devices  56.5 us (36%)
  Pallas kernels  16.3 us (11%)
  other arithmetic  4.13 us (3%)
  local copies, waits for them, and re-layouts  1.67 us (1%)
    ppermute x19, waiting for transfers between devices, shift(): return lax.ppermute(value, axis, [(i, (i + k) % n) for i in range(n)])  66.4 us
    ppermute x19, starting transfers between devices, shift(): return lax.ppermute(value, axis, [(i, (i + k) % n) for i in range(n)])  23.7 us
    all_to_all x1, starting transfers between devices, shards(): lax.all_to_all(payload.reshape(nz * nx, rows, 2 * wide), DP, 0, 0, tiled=...  11.6 us
    all_to_all x1, starting transfers between devices, shards(): everyone = lax.all_to_all(local, ZXY, 0, 0, tiled=True)  11.1 us
    all_to_all x1, starting transfers between devices, shards(): lax.all_to_all(packed.reshape(nz * nx, rows, 2 * wide), DP, 0, 0, tiled=T...  10.1 us
    pallas_call x2, Pallas kernels, run_groups(): pl.pallas_call(lambda *refs: groups_kernel(*refs, mode=mode), out_shape=o...  8.39 us
    all_to_all x1, waiting for transfers between devices, shards(): everyone = lax.all_to_all(local, ZXY, 0, 0, tiled=True)  7.72 us
  transfers between devices with their start and end apart: 22, of which 13 were waited for; matrix products, arithmetic and copies ran while one was open for 2% of the time, Pallas kernels for 7%

profile of v4, /device:TPU:2, one launch (start us, length us, event | category | flops | bytes accessed | tf_op | source)
XLA Modules:
  0.0 153.6 jit_solution(12032655302729705584)
XLA Ops:
  0.6 0.1 pad_add_fusion.at_ref.refs_0_
  0.7 2.5 %prepare.1 = (bf16[208,1152]{1,0:T(8,128)(2,1)S(1)}, bf16[186,1152]{1,0:T(8,128)(2,1)S(1)}, bf16[48,1152]{1,0:T(8,128)(2,1)S(1)}, bf16[64,1152]{1,0:T(8,128)(2,1)S(1)}, bf16[8,4,24,384]{3,2,1,0:T(8,128)(2,1)}) custom-call(s32[2]{0:T(128)S(1)} %pad_add_fusion.at_ref.refs_0_, bf16[394,768]{1,0:T(8,128)(2,1)} %refs_2_.1, bf16[394,768]{1,0:T(8,128)(2,1)} %bitcast.15, ...), custom_call_target="tpu_custom_call" | custom-call | tf_op jit(solution)/shard_map/prepare/pallas_call | solution.py:314
  3.2 11.6 %all-to-all-start = ((bf16[32,24,384]{2,1,0:T(8,128)(2,1)}), bf16[32,24,384]{2,1,0:T(8,128)(2,1)S(1)}, u32[]{:S(2)}, u32[]{:S(2)}) async-start(bf16[32,24,384]{2,1,0:T(8,128)(2,1)} %bitcast.5), calls=%async_computation | async-start | bytes 1179648 | tf_op jit(solution)/shard_map/all_to_all | solution.py:343
  14.8 1.5 %collective-permute-start = (bf16[208,1152]{1,0:T(8,128)(2,1)S(1)}, bf16[208,1152]{1,0:T(8,128)(2,1)S(1)}, u32[]{:S(2)}, u32[]{:S(2)}) collective-permute-start(bf16[208,1152]{1,0:T(8,128)(2,1)S(1)} %get-tuple-element.29), channel_id=1, source_target_pairs={{0,8},{8,16},{16,24},{24,0},{1,9},{9,17},{17,25},{25,1},{2,10},{10... | collective-permute-start | bytes 1437704 | tf_op jit(solution)/shard_map/ppermute | solution.py:40
  16.3 0.6 collective-permute-start.2
  16.9 1.4 collective-permute-start.6
  18.4 0.6 collective-permute-start.5
  18.9 16.1 %collective-permute-done.5.right_ref = bf16[48,1152]{1,0:T(8,128)(2,1)S(1)} collective-permute-done((bf16[48,1152]{1,0:T(8,128)(2,1)S(1)}, bf16[48,1152]{1,0:T(8,128)(2,1)S(1)}, u32[]{:S(2)}, u32[]{:S(2)}) %collective-permute-start.5) | collective-permute-done | bytes 110624 | tf_op jit(solution)/shard_map/ppermute | solution.py:40
  35.1 1.4 collective-permute-done.6.left_ref
  36.5 1.7 %collective-permute-start.7 = (bf16[112,1152]{1,0:T(8,128)(2,1)S(1)}, bf16[112,1152]{1,0:T(8,128)(2,1)S(1)}, u32[]{:S(2)}, u32[]{:S(2)}) collective-permute-start(bf16[112,1152]{1,0:T(8,128)(2,1)S(1)} %join.1.refs_2_.refs_7_), channel_id=1, source_target_pairs={{0,2},{2,4},{4,6},{6,0},{1,3},{3,5},{5,7},{7,1},{8,10},{10,12},{12... | collective-permute-start | bytes 774152 | tf_op jit(solution)/shard_map/ppermute | solution.py:40
  38.2 2.9 %collective-permute-start.8 = (bf16[112,1152]{1,0:T(8,128)(2,1)S(1)}, bf16[112,1152]{1,0:T(8,128)(2,1)S(1)}, u32[]{:S(2)}, u32[]{:S(2)}) collective-permute-start(bf16[112,1152]{1,0:T(8,128)(2,1)S(1)} %join.1.refs_2_.refs_7_), channel_id=1, source_target_pairs={{0,4},{2,6},{4,0},{6,2},{1,5},{3,7},{5,1},{7,3},{8,12},{10,14},{12... | collective-permute-start | bytes 774152 | tf_op jit(solution)/shard_map/ppermute | solution.py:40
  41.1 1.3 collective-permute-start.9
  42.4 1.1 collective-permute-start.1
  43.6 2.2 %collective-permute-done.7.refs_3_.refs_8_ = bf16[112,1152]{1,0:T(8,128)(2,1)S(1)} collective-permute-done((bf16[112,1152]{1,0:T(8,128)(2,1)S(1)}, bf16[112,1152]{1,0:T(8,128)(2,1)S(1)}, u32[]{:S(2)}, u32[]{:S(2)}) %collective-permute-start.7) | collective-permute-done | bytes 258080 | tf_op jit(solution)/shard_map/ppermute | solution.py:40
  45.8 6.0 %collective-permute-done.8.refs_4_.refs_9_ = bf16[112,1152]{1,0:T(8,128)(2,1)S(1)} collective-permute-done((bf16[112,1152]{1,0:T(8,128)(2,1)S(1)}, bf16[112,1152]{1,0:T(8,128)(2,1)S(1)}, u32[]{:S(2)}, u32[]{:S(2)}) %collective-permute-start.8) | collective-permute-done | bytes 258080 | tf_op jit(solution)/shard_map/ppermute | solution.py:40
  51.8 0.8 copy-done.13
  52.6 1.2 shard_map.120
  53.9 0.1 collective-permute-start.10
  54.0 0.9 collective-permute-start.3
  54.8 11.9 %collective-permute-done.3.refs_1_.refs_5_ = bf16[186,1152]{1,0:T(8,128)(2,1)S(1)} collective-permute-done((bf16[186,1152]{1,0:T(8,128)(2,1)}, bf16[186,1152]{1,0:T(8,128)(2,1)S(1)}, u32[]{:S(2)}, u32[]{:S(2)}) %collective-permute-start.3) | collective-permute-done | bytes 428576 | tf_op jit(solution)/shard_map/ppermute | solution.py:40
  66.8 0.3 collective-permute-start.4
  67.1 6.2 %shard_map.121 = (f32[2,768,384]{2,1,0:T(8,128)S(1)}, bf16[394,192]{1,0:T(8,128)(2,1)S(1)}, bf16[592,384]{1,0:T(8,128)(2,1)S(1)}, bf16[592,384]{1,0:T(8,128)(2,1)S(1)}) custom-call(s32[2]{0:T(128)S(1)} %pad_add_fusion.at_ref.refs_0_, bf16[768,384]{1,0:T(8,128)(2,1)S(1)} %bitcast.12, bf16[394,768]{1,0:T(8,128)(2,1)} %refs_2_.1, bf16[394,768]{1,0:T(8,128)(2,1)} %bitcast.16, ...), custom_call_target="tpu_custom_call" | custom-call | flops 1394343936 | bytes 6291456 | tf_op jit(solution)/shard_map/pallas_call | solution.py:230
  73.3 2.2 %shard_map.122 = (f32[768,384]{1,0:T(8,128)S(1)}, f32[768,384]{1,0:T(8,128)S(1)}, bf16[592,384]{1,0:T(8,128)(2,1)S(1)}) custom-call(s32[2]{0:T(128)S(1)} %pad_add_fusion.at_ref.refs_0_, bf16[768,384]{1,0:T(8,128)(2,1)S(1)} %bitcast.13, bf16[400,384]{1,0:T(8,128)(2,1)S(1)} %collective-permute-done.4.refs_2_, f32[2,768,384]{2,1,0:T(8,128)S(1)} %get-tuple-element.33.refs_3_, ...), custom_call_target="tpu_custom_call" | custom-call | flops 464781312 | bytes 6291456 | tf_op jit(solution)/shard_map/pallas_call | solution.py:230
  75.5 0.6 collective-permute-start.11
  76.1 2.5 %collective-permute-done.11 = f32[768,384]{1,0:T(8,128)S(1)} collective-permute-done((f32[768,384]{1,0:T(8,128)S(1)}, f32[768,384]{1,0:T(8,128)S(1)}, u32[]{:S(2)}, u32[]{:S(2)}) %collective-permute-start.11) | collective-permute-done | bytes 1179680 | tf_op jit(solution)/shard_map/ppermute | solution.py:40
  78.6 1.4 fusion
  80.0 10.1 %all-to-all-start.1 = ((f16[32,24,384]{2,1,0:T(8,128)(2,1)}), f16[32,24,384]{2,1,0:T(8,128)(2,1)}, u32[]{:S(2)}, u32[]{:S(2)}) async-start(f16[32,24,384]{2,1,0:T(8,128)(2,1)} %bitcast.7), calls=%async_computation.1 | async-start | bytes 1179648 | tf_op jit(solution)/shard_map/all_to_all | solution.py:376
  90.1 0.4 collective-permute-start.13
  90.5 1.7 %collective-permute-start.14 = (bf16[592,384]{1,0:T(8,128)(2,1)S(1)}, bf16[592,384]{1,0:T(8,128)(2,1)S(1)}, u32[]{:S(2)}, u32[]{:S(2)}) collective-permute-start(bf16[592,384]{1,0:T(8,128)(2,1)S(1)} %get-tuple-element.45), channel_id=1, source_target_pairs={{0,8},{8,16},{16,24},{24,0},{1,9},{9,17},{17,25},{25,1},{2,10},{10... | collective-permute-start | bytes 1363976 | tf_op jit(solution)/shard_map/ppermute | solution.py:40
  92.2 3.3 %collective-permute-start.15 = (bf16[592,384]{1,0:T(8,128)(2,1)S(1)}, bf16[592,384]{1,0:T(8,128)(2,1)S(1)}, u32[]{:S(2)}, u32[]{:S(2)}) collective-permute-start(bf16[592,384]{1,0:T(8,128)(2,1)S(1)} %copy-done.9), channel_id=1, source_target_pairs={{0,16},{8,24},{16,0},{24,8},{1,17},{9,25},{17,1},{25,9},{2,18},{10... | collective-permute-start | bytes 1363976 | tf_op jit(solution)/shard_map/ppermute | solution.py:40
  95.5 13.0 %collective-permute-done.13.refs_0_ = bf16[592,384]{1,0:T(8,128)(2,1)S(1)} collective-permute-done((bf16[592,384]{1,0:T(8,128)(2,1)S(1)}, bf16[592,384]{1,0:T(8,128)(2,1)S(1)}, u32[]{:S(2)}, u32[]{:S(2)}) %collective-permute-start.13) | collective-permute-done | bytes 454688 | tf_op jit(solution)/shard_map/ppermute | solution.py:40
  108.4 1.0 collective-permute-done.14.refs_1_
  109.4 9.5 %collective-permute-done.15.refs_2_ = bf16[592,384]{1,0:T(8,128)(2,1)S(1)} collective-permute-done((bf16[592,384]{1,0:T(8,128)(2,1)S(1)}, bf16[592,384]{1,0:T(8,128)(2,1)S(1)}, u32[]{:S(2)}, u32[]{:S(2)}) %collective-permute-start.15) | collective-permute-done | bytes 454688 | tf_op jit(solution)/shard_map/ppermute | solution.py:40
  118.9 2.5 %input_grad.1 = (f32[394,192]{1,0:T(8,128)S(1)}, f32[394,192]{1,0:T(8,128)S(1)}, f32[394,192]{1,0:T(8,128)S(1)}, f32[394,192]{1,0:T(8,128)S(1)}) custom-call(s32[1]{0:T(128)} %bitcast.1.at_ref, bf16[394,192]{1,0:T(8,128)(2,1)S(1)} %get-tuple-element.43.pg_ref, bf16[768,384]{1,0:T(8,128)(2,1)S(1)} %bitcast.14, bf16[592,384]{1,0:T(8,128)(2,1)} %copy-done.11, ...), custom_call_target="tpu_custom_call" | custom-call | flops 464781312 | bytes 4194304 | tf_op jit(solution)/shard_map/input_grad/pallas_call | solution.py:386
  121.3 1.3 collective-permute-start.16
  122.6 2.4 %collective-permute-start.17 = (f32[394,192]{1,0:T(8,128)S(1)}, f32[394,192]{1,0:T(8,128)}, u32[]{:S(2)}, u32[]{:S(2)}) collective-permute-start(f32[394,192]{1,0:T(8,128)S(1)} %get-tuple-element.49), channel_id=1, source_target_pairs={{0,4},{2,6},{4,0},{6,2},{1,5},{3,7},{5,1},{7,3},{8,12},{10,14},{12... | collective-permute-start | bytes 907784 | tf_op jit(solution)/shard_map/ppermute | solution.py:40
  125.0 1.6 %collective-permute-start.18 = (f32[394,192]{1,0:T(8,128)S(1)}, f32[394,192]{1,0:T(8,128)}, u32[]{:S(2)}, u32[]{:S(2)}) collective-permute-start(f32[394,192]{1,0:T(8,128)S(1)} %get-tuple-element.50), channel_id=1, source_target_pairs={{0,6},{2,0},{4,2},{6,4},{1,7},{3,1},{5,3},{7,5},{8,14},{10,8},{12,... | collective-permute-start | bytes 907784 | tf_op jit(solution)/shard_map/ppermute | solution.py:40
  126.6 1.4 fusion.3.refs_1_
  128.0 0.1 collective-permute-start.12
  128.1 1.4 collective-permute-done.12.refs_2_
  129.5 0.8 statistics.1
  130.3 11.1 %all-to-all-start.2 = ((f32[128,1,128]{2,1,0:T(1,128)}), f32[128,1,128]{2,1,0:T(1,128)S(1)}, u32[]{:S(2)}, u32[]{:S(2)}) async-start(f32[128,1,128]{2,1,0:T(1,128)} %get-tuple-element.36), calls=%async_computation.2 | async-start | bytes 131072 | tf_op jit(solution)/shard_map/all_to_all | solution.py:415
  141.4 1.3 collective-permute-done.17
  142.7 0.3 collective-permute-done.18
  143.0 1.2 fusion.5
  144.2 0.8 copy.13
  145.0 7.7 %all-to-all-done.2.sum_ref = f32[128,1,128]{2,1,0:T(1,128)S(1)} async-done(((f32[128,1,128]{2,1,0:T(1,128)}), f32[128,1,128]{2,1,0:T(1,128)S(1)}, u32[]{:S(2)}, u32[]{:S(2)}) %all-to-all-start.2) | async-done | bytes 65568 | tf_op jit(solution)/shard_map/all_to_all | solution.py:415
  152.7 0.9 update.1
  (40 shorter events, 0.1 us)
Async XLA Ops:
  3.2 63.9 %all-to-all-start = ((bf16[32,24,384]{2,1,0:T(8,128)(2,1)}), bf16[32,24,384]{2,1,0:T(8,128)(2,1)S(1)}, u32[]{:S(2)}, u32[]{:S(2)}) async-start(bf16[32,24,384]{2,1,0:T(8,128)(2,1)} %bitcast.5), calls=%async_computation | async-start | bytes 1179648 | tf_op jit(solution)/shard_map/all_to_all | solution.py:343
  14.8 27.6 %collective-permute-start = (bf16[208,1152]{1,0:T(8,128)(2,1)S(1)}, bf16[208,1152]{1,0:T(8,128)(2,1)S(1)}, u32[]{:S(2)}, u32[]{:S(2)}) collective-permute-start(bf16[208,1152]{1,0:T(8,128)(2,1)S(1)} %get-tuple-element.29), channel_id=1, source_target_pairs={{0,8},{8,16},{16,24},{24,0},{1,9},{9,17},{17,25},{25,1},{2,10},{10... | collective-permute-start | bytes 1437704 | tf_op jit(solution)/shard_map/ppermute | solution.py:40
  16.3 35.4 %collective-permute-start.2 = (bf16[186,1152]{1,0:T(8,128)(2,1)S(1)}, bf16[186,1152]{1,0:T(8,128)(2,1)S(1)}, u32[]{:S(2)}, u32[]{:S(2)}) collective-permute-start(bf16[186,1152]{1,0:T(8,128)(2,1)S(1)} %get-tuple-element.30), channel_id=1, source_target_pairs={{0,24},{8,0},{16,8},{24,16},{1,25},{9,1},{17,9},{25,17},{2,26},{10... | collective-permute-start | bytes 1285640 | tf_op jit(solution)/shard_map/ppermute | solution.py:40
  16.9 19.6 %collective-permute-start.6 = (bf16[64,1152]{1,0:T(8,128)(2,1)S(1)}, bf16[64,1152]{1,0:T(8,128)(2,1)S(1)}, u32[]{:S(2)}, u32[]{:S(2)}) collective-permute-start(bf16[64,1152]{1,0:T(8,128)(2,1)S(1)} %get-tuple-element.32), channel_id=1, source_target_pairs={{0,24},{8,0},{16,8},{24,16},{1,25},{9,1},{17,9},{25,17},{2,26},{10... | collective-permute-start | bytes 442376 | tf_op jit(solution)/shard_map/ppermute | solution.py:40
  18.4 16.7 %collective-permute-start.5 = (bf16[48,1152]{1,0:T(8,128)(2,1)S(1)}, bf16[48,1152]{1,0:T(8,128)(2,1)S(1)}, u32[]{:S(2)}, u32[]{:S(2)}) collective-permute-start(bf16[48,1152]{1,0:T(8,128)(2,1)S(1)} %get-tuple-element.31), channel_id=1, source_target_pairs={{0,8},{8,16},{16,24},{24,0},{1,9},{9,17},{17,25},{25,1},{2,10},{10... | collective-permute-start | bytes 331784 | tf_op jit(solution)/shard_map/ppermute | solution.py:40
  36.5 17.3 %copy-start = (bf16[112,1152]{1,0:T(8,128)(2,1)}, bf16[112,1152]{1,0:T(8,128)(2,1)S(1)}, u32[]{:S(2)}) copy-start(bf16[112,1152]{1,0:T(8,128)(2,1)S(1)} %join.1.refs_2_.refs_7_) | copy-start | bytes 774148
  36.5 9.3 %collective-permute-start.7 = (bf16[112,1152]{1,0:T(8,128)(2,1)S(1)}, bf16[112,1152]{1,0:T(8,128)(2,1)S(1)}, u32[]{:S(2)}, u32[]{:S(2)}) collective-permute-start(bf16[112,1152]{1,0:T(8,128)(2,1)S(1)} %join.1.refs_2_.refs_7_), channel_id=1, source_target_pairs={{0,2},{2,4},{4,6},{6,0},{1,3},{3,5},{5,7},{7,1},{8,10},{10,12},{12... | collective-permute-start | bytes 774152 | tf_op jit(solution)/shard_map/ppermute | solution.py:40
  38.2 13.6 %collective-permute-start.8 = (bf16[112,1152]{1,0:T(8,128)(2,1)S(1)}, bf16[112,1152]{1,0:T(8,128)(2,1)S(1)}, u32[]{:S(2)}, u32[]{:S(2)}) collective-permute-start(bf16[112,1152]{1,0:T(8,128)(2,1)S(1)} %join.1.refs_2_.refs_7_), channel_id=1, source_target_pairs={{0,4},{2,6},{4,0},{6,2},{1,5},{3,7},{5,1},{7,3},{8,12},{10,14},{12... | collective-permute-start | bytes 774152 | tf_op jit(solution)/shard_map/ppermute | solution.py:40
  41.1 10.7 %collective-permute-start.9 = (bf16[112,1152]{1,0:T(8,128)(2,1)S(1)}, bf16[112,1152]{1,0:T(8,128)(2,1)S(1)}, u32[]{:S(2)}, u32[]{:S(2)}) collective-permute-start(bf16[112,1152]{1,0:T(8,128)(2,1)S(1)} %join.1.refs_2_.refs_7_), channel_id=1, source_target_pairs={{0,6},{2,0},{4,2},{6,4},{1,7},{3,1},{5,3},{7,5},{8,14},{10,8},{12,... | collective-permute-start | bytes 774152 | tf_op jit(solution)/shard_map/ppermute | solution.py:40
  42.4 9.3 %copy-start.10 = (bf16[208,1152]{1,0:T(8,128)(2,1)}, bf16[208,1152]{1,0:T(8,128)(2,1)S(1)}, u32[]{:S(2)}) copy-start(bf16[208,1152]{1,0:T(8,128)(2,1)S(1)} %collective-permute-done.refs_0_.refs_5_) | copy-start | bytes 1437700
  42.4 24.3 %collective-permute-start.1 = (bf16[208,1152]{1,0:T(8,128)(2,1)S(1)}, bf16[208,1152]{1,0:T(8,128)(2,1)S(1)}, u32[]{:S(2)}, u32[]{:S(2)}) collective-permute-start(bf16[208,1152]{1,0:T(8,128)(2,1)S(1)} %collective-permute-done.refs_0_.refs_5_), channel_id=1, source_target_pairs={{0,8},{8,16},{16,24},{24,0},{1,9},{9,17},{17,25},{25,1},{2,10},{10... | collective-permute-start | bytes 1437704 | tf_op jit(solution)/shard_map/ppermute | solution.py:40
  45.8 8.0 %copy-start.5 = (bf16[112,1152]{1,0:T(8,128)(2,1)}, bf16[112,1152]{1,0:T(8,128)(2,1)S(1)}, u32[]{:S(2)}) copy-start(bf16[112,1152]{1,0:T(8,128)(2,1)S(1)} %collective-permute-done.7.refs_3_.refs_8_) | copy-start | bytes 774148
  51.8 2.1 %copy-start.6 = (bf16[112,1152]{1,0:T(8,128)(2,1)}, bf16[112,1152]{1,0:T(8,128)(2,1)S(1)}, u32[]{:S(2)}) copy-start(bf16[112,1152]{1,0:T(8,128)(2,1)S(1)} %collective-permute-done.8.refs_4_.refs_9_) | copy-start | bytes 774148
  51.8 2.1 %copy-start.7 = (bf16[112,1152]{1,0:T(8,128)(2,1)}, bf16[112,1152]{1,0:T(8,128)(2,1)S(1)}, u32[]{:S(2)}) copy-start(bf16[112,1152]{1,0:T(8,128)(2,1)S(1)} %collective-permute-done.9.refs_5_.refs_10_) | copy-start | bytes 774148
  51.8 0.8 copy-start.13
  53.9 13.2 %collective-permute-start.10 = (bf16[848,384]{1,0:T(8,128)(2,1)S(1)}, bf16[848,384]{1,0:T(8,128)(2,1)}, u32[]{:S(2)}, u32[]{:S(2)}) collective-permute-start(bf16[848,384]{1,0:T(8,128)(2,1)S(1)} %shard_map.120), channel_id=1, source_target_pairs={{0,1},{1,0},{2,3},{3,2},{4,5},{5,4},{6,7},{7,6},{8,9},{9,8},{10,11... | collective-permute-start | bytes 1953800 | tf_op jit(solution)/shard_map/ppermute | solution.py:40
  54.0 12.8 %collective-permute-start.3 = (bf16[186,1152]{1,0:T(8,128)(2,1)}, bf16[186,1152]{1,0:T(8,128)(2,1)S(1)}, u32[]{:S(2)}, u32[]{:S(2)}) collective-permute-start(bf16[186,1152]{1,0:T(8,128)(2,1)} %copy-done.13), channel_id=1, source_target_pairs={{0,24},{8,0},{16,8},{24,16},{1,25},{9,1},{17,9},{25,17},{2,26},{10... | collective-permute-start | bytes 1285640 | tf_op jit(solution)/shard_map/ppermute | solution.py:40
  66.8 6.5 %collective-permute-start.4 = (bf16[400,384]{1,0:T(8,128)(2,1)S(1)}, bf16[400,384]{1,0:T(8,128)(2,1)S(1)}, u32[]{:S(2)}, u32[]{:S(2)}) collective-permute-start(bf16[400,384]{1,0:T(8,128)(2,1)S(1)} %shard_map.119), channel_id=1, source_target_pairs={{0,1},{1,0},{2,3},{3,2},{4,5},{5,4},{6,7},{7,6},{8,9},{9,8},{10,11... | collective-permute-start | bytes 921608 | tf_op jit(solution)/shard_map/ppermute | solution.py:40
  75.5 4.5 %copy-start.8 = (bf16[592,384]{1,0:T(8,128)(2,1)}, bf16[592,384]{1,0:T(8,128)(2,1)S(1)}, u32[]{:S(2)}) copy-start(bf16[592,384]{1,0:T(8,128)(2,1)S(1)} %get-tuple-element.46) | copy-start | bytes 1363972
  75.5 3.0 %collective-permute-start.11 = (f32[768,384]{1,0:T(8,128)S(1)}, f32[768,384]{1,0:T(8,128)S(1)}, u32[]{:S(2)}, u32[]{:S(2)}) collective-permute-start(f32[768,384]{1,0:T(8,128)S(1)} %get-tuple-element.35), channel_id=1, source_target_pairs={{0,1},{1,0},{2,3},{3,2},{4,5},{5,4},{6,7},{7,6},{8,9},{9,8},{10,11... | collective-permute-start | bytes 3538952 | tf_op jit(solution)/shard_map/ppermute | solution.py:40
  80.0 12.2 %copy-start.9 = (bf16[592,384]{1,0:T(8,128)(2,1)S(1)}, bf16[592,384]{1,0:T(8,128)(2,1)}, u32[]{:S(2)}) copy-start(bf16[592,384]{1,0:T(8,128)(2,1)} %copy-done.8) | copy-start | bytes 1363972
  80.0 46.6 %all-to-all-start.1 = ((f16[32,24,384]{2,1,0:T(8,128)(2,1)}), f16[32,24,384]{2,1,0:T(8,128)(2,1)}, u32[]{:S(2)}, u32[]{:S(2)}) async-start(f16[32,24,384]{2,1,0:T(8,128)(2,1)} %bitcast.7), calls=%async_computation.1 | async-start | bytes 1179648 | tf_op jit(solution)/shard_map/all_to_all | solution.py:376
  90.1 18.4 %collective-permute-start.13 = (bf16[592,384]{1,0:T(8,128)(2,1)S(1)}, bf16[592,384]{1,0:T(8,128)(2,1)S(1)}, u32[]{:S(2)}, u32[]{:S(2)}) collective-permute-start(bf16[592,384]{1,0:T(8,128)(2,1)S(1)} %get-tuple-element.44), channel_id=1, source_target_pairs={{0,24},{8,0},{16,8},{24,16},{1,25},{9,1},{17,9},{25,17},{2,26},{10... | collective-permute-start | bytes 1363976 | tf_op jit(solution)/shard_map/ppermute | solution.py:40
  90.5 18.9 %collective-permute-start.14 = (bf16[592,384]{1,0:T(8,128)(2,1)S(1)}, bf16[592,384]{1,0:T(8,128)(2,1)S(1)}, u32[]{:S(2)}, u32[]{:S(2)}) collective-permute-start(bf16[592,384]{1,0:T(8,128)(2,1)S(1)} %get-tuple-element.45), channel_id=1, source_target_pairs={{0,8},{8,16},{16,24},{24,0},{1,9},{9,17},{17,25},{25,1},{2,10},{10... | collective-permute-start | bytes 1363976 | tf_op jit(solution)/shard_map/ppermute | solution.py:40
  92.2 26.7 %collective-permute-start.15 = (bf16[592,384]{1,0:T(8,128)(2,1)S(1)}, bf16[592,384]{1,0:T(8,128)(2,1)S(1)}, u32[]{:S(2)}, u32[]{:S(2)}) collective-permute-start(bf16[592,384]{1,0:T(8,128)(2,1)S(1)} %copy-done.9), channel_id=1, source_target_pairs={{0,16},{8,24},{16,0},{24,8},{1,17},{9,25},{17,1},{25,9},{2,18},{10... | collective-permute-start | bytes 1363976 | tf_op jit(solution)/shard_map/ppermute | solution.py:40
  108.4 10.4 %copy-start.11 = (bf16[592,384]{1,0:T(8,128)(2,1)}, bf16[592,384]{1,0:T(8,128)(2,1)S(1)}, u32[]{:S(2)}) copy-start(bf16[592,384]{1,0:T(8,128)(2,1)S(1)} %collective-permute-done.13.refs_0_) | copy-start | bytes 1363972
  109.4 9.5 %copy-start.12 = (bf16[592,384]{1,0:T(8,128)(2,1)}, bf16[592,384]{1,0:T(8,128)(2,1)S(1)}, u32[]{:S(2)}) copy-start(bf16[592,384]{1,0:T(8,128)(2,1)S(1)} %collective-permute-done.14.refs_1_) | copy-start | bytes 1363972
  118.9 10.6 %copy-start.1 = (f32[24,768]{1,0:T(8,128)S(1)}, f32[24,768]{1,0:T(8,128)}, u32[]{:S(2)}) copy-start(f32[24,768]{1,0:T(8,128)} %refs_3_.1) | copy-start | bytes 221188
  118.9 10.6 %copy-start.2 = (f32[24,768]{1,0:T(8,128)S(1)}, f32[24,768]{1,0:T(8,128)}, u32[]{:S(2)}) copy-start(f32[24,768]{1,0:T(8,128)} %refs_4_.1) | copy-start | bytes 221188
  121.3 20.1 %collective-permute-start.16 = (f32[394,192]{1,0:T(8,128)S(1)}, f32[394,192]{1,0:T(8,128)S(1)}, u32[]{:S(2)}, u32[]{:S(2)}) collective-permute-start(f32[394,192]{1,0:T(8,128)S(1)} %get-tuple-element.48), channel_id=1, source_target_pairs={{0,2},{2,4},{4,6},{6,0},{1,3},{3,5},{5,7},{7,1},{8,10},{10,12},{12... | collective-permute-start | bytes 907784 | tf_op jit(solution)/shard_map/ppermute | solution.py:40
  122.6 20.1 %collective-permute-start.17 = (f32[394,192]{1,0:T(8,128)S(1)}, f32[394,192]{1,0:T(8,128)}, u32[]{:S(2)}, u32[]{:S(2)}) collective-permute-start(f32[394,192]{1,0:T(8,128)S(1)} %get-tuple-element.49), channel_id=1, source_target_pairs={{0,4},{2,6},{4,0},{6,2},{1,5},{3,7},{5,1},{7,3},{8,12},{10,14},{12... | collective-permute-start | bytes 907784 | tf_op jit(solution)/shard_map/ppermute | solution.py:40
  125.0 17.9 %collective-permute-start.18 = (f32[394,192]{1,0:T(8,128)S(1)}, f32[394,192]{1,0:T(8,128)}, u32[]{:S(2)}, u32[]{:S(2)}) collective-permute-start(f32[394,192]{1,0:T(8,128)S(1)} %get-tuple-element.50), channel_id=1, source_target_pairs={{0,6},{2,0},{4,2},{6,4},{1,7},{3,1},{5,3},{7,5},{8,14},{10,8},{12,... | collective-permute-start | bytes 907784 | tf_op jit(solution)/shard_map/ppermute | solution.py:40
  128.0 1.5 collective-permute-start.12
  130.3 22.4 %copy-start.3 = (f32[24,768]{1,0:T(8,128)S(1)}, f32[24,768]{1,0:T(8,128)}, u32[]{:S(2)}) copy-start(f32[24,768]{1,0:T(8,128)} %mu_ref.3) | copy-start | bytes 221188
  130.3 22.4 %copy-start.4 = (f32[24,768]{1,0:T(8,128)S(1)}, f32[24,768]{1,0:T(8,128)}, u32[]{:S(2)}) copy-start(f32[24,768]{1,0:T(8,128)} %md_ref.3) | copy-start | bytes 221188
  130.3 22.4 %all-to-all-start.2 = ((f32[128,1,128]{2,1,0:T(1,128)}), f32[128,1,128]{2,1,0:T(1,128)S(1)}, u32[]{:S(2)}, u32[]{:S(2)}) async-start(f32[128,1,128]{2,1,0:T(1,128)} %get-tuple-element.36), calls=%async_computation.2 | async-start | bytes 131072 | tf_op jit(solution)/shard_map/all_to_all | solution.py:415

commit v5 on v4

--- a/solution.py
+++ b/solution.py
@@ -41,8 +41,7 @@
 
 
 def prepare_kernel(
-    at_ref, f_ref, c_ref, mu_ref, pu_ref, nu_ref, md_ref, pd_ref, nd_ref,
-    head_ref, tail_ref, right_ref, left_ref, w_ref, u_s,
+    at_ref, f_ref, c_ref, head_ref, tail_ref, right_ref, left_ref, u_s
 ):
     first = at_ref[0] == 0
     u_s[FULL - 16 : FULL] = jnp.zeros((16, HALF + D), jnp.bfloat16)
@@ -53,6 +52,9 @@
     at = at_ref[1] * STEP
     right_ref[...] = u_s[pl.ds(pl.multiple_of(HEAD + at, 16), STEP)]
     left_ref[...] = u_s[pl.ds(pl.multiple_of(at, 16), HEAD - 3 * STEP)]
+
+
+def sample_kernel(mu_ref, pu_ref, nu_ref, md_ref, pd_ref, nd_ref, w_ref):
     nz, nx, _, width = w_ref.shape
 
     def drawn(m, p, n):
@@ -311,29 +313,32 @@
     at = jnp.stack([core, mp])
     cotangent = out_cotangent[0]
 
-    u0, u1, right, left, payload = pl.pallas_call(
+    u0, u1, right, left = pl.pallas_call(
         prepare_kernel,
         out_shape=[
             pltpu.VMEM((HEAD, HALF + D), jnp.bfloat16),
             pltpu.VMEM((TAIL, HALF + D), jnp.bfloat16),
             pltpu.VMEM((STEP, HALF + D), jnp.bfloat16),
             pltpu.VMEM((QUARTERS - STEP, HALF + D), jnp.bfloat16),
-            pltpu.VMEM((nz, nx, rows, 2 * wide), jnp.bfloat16),
         ],
-        in_specs=[SMEM] + [VMEM] * 8,
-        out_specs=[VMEM] * 5,
+        in_specs=[SMEM] + [VMEM] * 2,
+        out_specs=[VMEM] * 4,
         scratch_shapes=[pltpu.VMEM((FULL, HALF + D), jnp.bfloat16)],
         compiler_params=pltpu.CompilerParams(vmem_limit_bytes=16 << 20),
         name="prepare",
+    )(at, outside(features), outside(cotangent))
+    payload = pl.pallas_call(
+        sample_kernel,
+        out_shape=pltpu.VMEM((nz, nx, rows, 2 * wide), jnp.bfloat16),
+        in_specs=[VMEM] * 6,
+        out_specs=VMEM,
+        compiler_params=pltpu.CompilerParams(vmem_limit_bytes=16 << 20),
+        name="sample",
     )(
-        at,
-        *[
-            pltpu.with_memory_space_constraint(a, pltpu.HBM)
-            for a in (
-                features, cotangent, mean_up, precision_up, noise_up[0],
-                mean_down, precision_down, noise_down[0],
-            )
-        ],
+        *map(
+            outside,
+            (mean_up, precision_up, noise_up[0], mean_down, precision_down, noise_down[0]),
+        )
     )
     right = shift(right, "x", 1)
     left = shift(left, "x", -1)

time: 155 us -> 154 us (level)
    pallas_call x0 -> x1, Pallas kernels: none -> 2.03 us  [shards(): pl.pallas_call(sample_kernel, out_shape=pltpu.VMEM((nz, nx, rows, 2 * wid...]
  transfers between devices with their start and end apart: 22 -> 22, of which waited for: 13 -> 13; matrix products, arithmetic and copies ran while one was open for 2% -> 2% of each run, Pallas kernels for 7% -> 8%
where the time goes in v5:
time: 154 us; the launch traced here: 153 us
  waiting for transfers between devices  73.2 us (48%)
  starting transfers between devices  56.1 us (36%)
  Pallas kernels  17.3 us (11%)
  other arithmetic  4.13 us (3%)
  local copies, waits for them, and re-layouts  1.67 us (1%)
    ppermute x19, waiting for transfers between devices, shift(): return lax.ppermute(value, axis, [(i, (i + k) % n) for i in range(n)])  65.4 us
    ppermute x19, starting transfers between devices, shift(): return lax.ppermute(value, axis, [(i, (i + k) % n) for i in range(n)])  24 us
    all_to_all x1, starting transfers between devices, shards(): lax.all_to_all(payload.reshape(nz * nx, rows, 2 * wide), DP, 0, 0, tiled=...  11.6 us
    all_to_all x1, starting transfers between devices, shards(): everyone = lax.all_to_all(local, ZXY, 0, 0, tiled=True)  11.1 us
    all_to_all x1, starting transfers between devices, shards(): lax.all_to_all(packed.reshape(nz * nx, rows, 2 * wide), DP, 0, 0, tiled=T...  9.37 us
    pallas_call x2, Pallas kernels, run_groups(): pl.pallas_call(lambda *refs: groups_kernel(*refs, mode=mode), out_shape=o...  8.39 us
    all_to_all x1, waiting for transfers between devices, shards(): everyone = lax.all_to_all(local, ZXY, 0, 0, tiled=True)  7.73 us
  transfers between devices with their start and end apart: 22, of which 13 were waited for; matrix products, arithmetic and copies ran while one was open for 2% of the time, Pallas kernels for 8%

profile of v5, /device:TPU:2, one launch (start us, length us, event | category | flops | bytes accessed | tf_op | source)
XLA Modules:
  0.0 153.2 jit_solution(13026978827814841599)
XLA Ops:
  0.6 2.0 %sample.1 = bf16[8,4,24,384]{3,2,1,0:T(8,128)(2,1)} custom-call(f32[24,768]{1,0:T(8,128)} %mu_ref.3, f32[24,768]{1,0:T(8,128)} %refs_3_.1, f32[24,768]{1,0:T(8,128)} %bitcast.17, f32[24,768]{1,0:T(8,128)} %md_ref.3, f32[24,768]{1,0:T(8,128)} %refs_4_.1, f32[24,768]{1,0:T(8,128)} %bitcast.18), custom_call_target="tpu_custom_call" | custom-call | tf_op jit(solution)/shard_map/sample/pallas_call | solution.py:330
  2.7 11.6 %all-to-all-start = ((bf16[32,24,384]{2,1,0:T(8,128)(2,1)}), bf16[32,24,384]{2,1,0:T(8,128)(2,1)S(1)}, u32[]{:S(2)}, u32[]{:S(2)}) async-start(bf16[32,24,384]{2,1,0:T(8,128)(2,1)} %bitcast.4), calls=%async_computation | async-start | bytes 1179648 | tf_op jit(solution)/shard_map/all_to_all | solution.py:348
  14.4 1.4 prepare.1
  15.8 1.5 %collective-permute-start = (bf16[208,1152]{1,0:T(8,128)(2,1)S(1)}, bf16[208,1152]{1,0:T(8,128)(2,1)S(1)}, u32[]{:S(2)}, u32[]{:S(2)}) collective-permute-start(bf16[208,1152]{1,0:T(8,128)(2,1)S(1)} %get-tuple-element.27), channel_id=1, source_target_pairs={{0,8},{8,16},{16,24},{24,0},{1,9},{9,17},{17,25},{25,1},{2,10},{10... | collective-permute-start | bytes 1437704 | tf_op jit(solution)/shard_map/ppermute | solution.py:40
  17.3 0.6 collective-permute-start.2
  17.9 1.4 collective-permute-start.6
  19.4 0.6 collective-permute-start.5
  19.9 15.6 %collective-permute-done.5.right_ref = bf16[48,1152]{1,0:T(8,128)(2,1)S(1)} collective-permute-done((bf16[48,1152]{1,0:T(8,128)(2,1)S(1)}, bf16[48,1152]{1,0:T(8,128)(2,1)S(1)}, u32[]{:S(2)}, u32[]{:S(2)}) %collective-permute-start.5) | collective-permute-done | bytes 110624 | tf_op jit(solution)/shard_map/ppermute | solution.py:40
  35.5 1.4 collective-permute-done.6.left_ref
  36.9 1.7 %collective-permute-start.7 = (bf16[112,1152]{1,0:T(8,128)(2,1)S(1)}, bf16[112,1152]{1,0:T(8,128)(2,1)S(1)}, u32[]{:S(2)}, u32[]{:S(2)}) collective-permute-start(bf16[112,1152]{1,0:T(8,128)(2,1)S(1)} %join.1.refs_2_.refs_7_), channel_id=1, source_target_pairs={{0,2},{2,4},{4,6},{6,0},{1,3},{3,5},{5,7},{7,1},{8,10},{10,12},{12... | collective-permute-start | bytes 774152 | tf_op jit(solution)/shard_map/ppermute | solution.py:40
  38.6 2.9 %collective-permute-start.8 = (bf16[112,1152]{1,0:T(8,128)(2,1)S(1)}, bf16[112,1152]{1,0:T(8,128)(2,1)S(1)}, u32[]{:S(2)}, u32[]{:S(2)}) collective-permute-start(bf16[112,1152]{1,0:T(8,128)(2,1)S(1)} %join.1.refs_2_.refs_7_), channel_id=1, source_target_pairs={{0,4},{2,6},{4,0},{6,2},{1,5},{3,7},{5,1},{7,3},{8,12},{10,14},{12... | collective-permute-start | bytes 774152 | tf_op jit(solution)/shard_map/ppermute | solution.py:40
  41.5 1.3 collective-permute-start.9
  42.8 1.0 collective-permute-start.1
  43.8 2.4 %collective-permute-done.7.refs_3_.refs_8_ = bf16[112,1152]{1,0:T(8,128)(2,1)S(1)} collective-permute-done((bf16[112,1152]{1,0:T(8,128)(2,1)S(1)}, bf16[112,1152]{1,0:T(8,128)(2,1)S(1)}, u32[]{:S(2)}, u32[]{:S(2)}) %collective-permute-start.7) | collective-permute-done | bytes 258080 | tf_op jit(solution)/shard_map/ppermute | solution.py:40
  46.2 5.9 %collective-permute-done.8.refs_4_.refs_9_ = bf16[112,1152]{1,0:T(8,128)(2,1)S(1)} collective-permute-done((bf16[112,1152]{1,0:T(8,128)(2,1)S(1)}, bf16[112,1152]{1,0:T(8,128)(2,1)S(1)}, u32[]{:S(2)}, u32[]{:S(2)}) %collective-permute-start.8) | collective-permute-done | bytes 258080 | tf_op jit(solution)/shard_map/ppermute | solution.py:40
  52.1 0.8 copy-done.13
  52.9 1.2 shard_map.120
  54.2 0.1 collective-permute-start.10
  54.3 1.3 collective-permute-start.3
  55.6 11.4 %collective-permute-done.3.refs_1_.refs_5_ = bf16[186,1152]{1,0:T(8,128)(2,1)S(1)} collective-permute-done((bf16[186,1152]{1,0:T(8,128)(2,1)}, bf16[186,1152]{1,0:T(8,128)(2,1)S(1)}, u32[]{:S(2)}, u32[]{:S(2)}) %collective-permute-start.3) | collective-permute-done | bytes 428576 | tf_op jit(solution)/shard_map/ppermute | solution.py:40
  67.1 0.3 collective-permute-start.4
  67.4 6.2 %shard_map.121 = (f32[2,768,384]{2,1,0:T(8,128)S(1)}, bf16[394,192]{1,0:T(8,128)(2,1)S(1)}, bf16[592,384]{1,0:T(8,128)(2,1)S(1)}, bf16[592,384]{1,0:T(8,128)(2,1)S(1)}) custom-call(s32[2]{0:T(128)S(1)} %pad_add_fusion.at_ref.refs_0_, bf16[768,384]{1,0:T(8,128)(2,1)S(1)} %bitcast.12, bf16[394,768]{1,0:T(8,128)(2,1)} %refs_2_.1, bf16[394,768]{1,0:T(8,128)(2,1)} %bitcast.16, ...), custom_call_target="tpu_custom_call" | custom-call | flops 1394343936 | bytes 6291456 | tf_op jit(solution)/shard_map/pallas_call | solution.py:232
  73.6 2.2 %shard_map.122 = (f32[768,384]{1,0:T(8,128)S(1)}, f32[768,384]{1,0:T(8,128)S(1)}, bf16[592,384]{1,0:T(8,128)(2,1)S(1)}) custom-call(s32[2]{0:T(128)S(1)} %pad_add_fusion.at_ref.refs_0_, bf16[768,384]{1,0:T(8,128)(2,1)S(1)} %bitcast.13, bf16[400,384]{1,0:T(8,128)(2,1)S(1)} %collective-permute-done.4.refs_2_, f32[2,768,384]{2,1,0:T(8,128)S(1)} %get-tuple-element.31.refs_3_, ...), custom_call_target="tpu_custom_call" | custom-call | flops 464781312 | bytes 6291456 | tf_op jit(solution)/shard_map/pallas_call | solution.py:232
  75.8 0.6 collective-permute-start.11
  76.4 2.5 %collective-permute-done.11 = f32[768,384]{1,0:T(8,128)S(1)} collective-permute-done((f32[768,384]{1,0:T(8,128)S(1)}, f32[768,384]{1,0:T(8,128)S(1)}, u32[]{:S(2)}, u32[]{:S(2)}) %collective-permute-start.11) | collective-permute-done | bytes 1179680 | tf_op jit(solution)/shard_map/ppermute | solution.py:40
  78.8 1.4 fusion
  80.3 9.4 %all-to-all-start.1 = ((f16[32,24,384]{2,1,0:T(8,128)(2,1)}), f16[32,24,384]{2,1,0:T(8,128)(2,1)}, u32[]{:S(2)}, u32[]{:S(2)}) async-start(f16[32,24,384]{2,1,0:T(8,128)(2,1)} %bitcast.7), calls=%async_computation.1 | async-start | bytes 1179648 | tf_op jit(solution)/shard_map/all_to_all | solution.py:381
  89.7 0.4 collective-permute-start.13
  90.0 1.7 %collective-permute-start.14 = (bf16[592,384]{1,0:T(8,128)(2,1)S(1)}, bf16[592,384]{1,0:T(8,128)(2,1)S(1)}, u32[]{:S(2)}, u32[]{:S(2)}) collective-permute-start(bf16[592,384]{1,0:T(8,128)(2,1)S(1)} %get-tuple-element.43), channel_id=1, source_target_pairs={{0,8},{8,16},{16,24},{24,0},{1,9},{9,17},{17,25},{25,1},{2,10},{10... | collective-permute-start | bytes 1363976 | tf_op jit(solution)/shard_map/ppermute | solution.py:40
  91.8 3.3 %collective-permute-start.15 = (bf16[592,384]{1,0:T(8,128)(2,1)S(1)}, bf16[592,384]{1,0:T(8,128)(2,1)S(1)}, u32[]{:S(2)}, u32[]{:S(2)}) collective-permute-start(bf16[592,384]{1,0:T(8,128)(2,1)S(1)} %copy-done.9), channel_id=1, source_target_pairs={{0,16},{8,24},{16,0},{24,8},{1,17},{9,25},{17,1},{25,9},{2,18},{10... | collective-permute-start | bytes 1363976 | tf_op jit(solution)/shard_map/ppermute | solution.py:40
  95.1 13.0 %collective-permute-done.13.refs_0_ = bf16[592,384]{1,0:T(8,128)(2,1)S(1)} collective-permute-done((bf16[592,384]{1,0:T(8,128)(2,1)S(1)}, bf16[592,384]{1,0:T(8,128)(2,1)S(1)}, u32[]{:S(2)}, u32[]{:S(2)}) %collective-permute-start.13) | collective-permute-done | bytes 454688 | tf_op jit(solution)/shard_map/ppermute | solution.py:40
  108.0 1.0 collective-permute-done.14.refs_1_
  109.0 9.5 %collective-permute-done.15.refs_2_ = bf16[592,384]{1,0:T(8,128)(2,1)S(1)} collective-permute-done((bf16[592,384]{1,0:T(8,128)(2,1)S(1)}, bf16[592,384]{1,0:T(8,128)(2,1)S(1)}, u32[]{:S(2)}, u32[]{:S(2)}) %collective-permute-start.15) | collective-permute-done | bytes 454688 | tf_op jit(solution)/shard_map/ppermute | solution.py:40
  118.5 2.5 %input_grad.1 = (f32[394,192]{1,0:T(8,128)S(1)}, f32[394,192]{1,0:T(8,128)S(1)}, f32[394,192]{1,0:T(8,128)S(1)}, f32[394,192]{1,0:T(8,128)S(1)}) custom-call(s32[1]{0:T(128)} %bitcast.1.at_ref, bf16[394,192]{1,0:T(8,128)(2,1)S(1)} %get-tuple-element.41.pg_ref, bf16[768,384]{1,0:T(8,128)(2,1)S(1)} %bitcast.14, bf16[592,384]{1,0:T(8,128)(2,1)} %copy-done.11, ...), custom_call_target="tpu_custom_call" | custom-call | flops 464781312 | bytes 4194304 | tf_op jit(solution)/shard_map/input_grad/pallas_call | solution.py:391
  120.9 1.3 collective-permute-start.16
  122.2 2.4 %collective-permute-start.17 = (f32[394,192]{1,0:T(8,128)S(1)}, f32[394,192]{1,0:T(8,128)}, u32[]{:S(2)}, u32[]{:S(2)}) collective-permute-start(f32[394,192]{1,0:T(8,128)S(1)} %get-tuple-element.47), channel_id=1, source_target_pairs={{0,4},{2,6},{4,0},{6,2},{1,5},{3,7},{5,1},{7,3},{8,12},{10,14},{12... | collective-permute-start | bytes 907784 | tf_op jit(solution)/shard_map/ppermute | solution.py:40
  124.6 1.6 %collective-permute-start.18 = (f32[394,192]{1,0:T(8,128)S(1)}, f32[394,192]{1,0:T(8,128)}, u32[]{:S(2)}, u32[]{:S(2)}) collective-permute-start(f32[394,192]{1,0:T(8,128)S(1)} %get-tuple-element.48), channel_id=1, source_target_pairs={{0,6},{2,0},{4,2},{6,4},{1,7},{3,1},{5,3},{7,5},{8,14},{10,8},{12,... | collective-permute-start | bytes 907784 | tf_op jit(solution)/shard_map/ppermute | solution.py:40
  126.2 1.4 fusion.3.refs_1_
  127.6 0.1 collective-permute-start.12
  127.7 1.4 collective-permute-done.12.refs_2_
  129.1 0.8 statistics.1
  129.9 11.1 %all-to-all-start.2 = ((f32[128,1,128]{2,1,0:T(1,128)}), f32[128,1,128]{2,1,0:T(1,128)S(1)}, u32[]{:S(2)}, u32[]{:S(2)}) async-start(f32[128,1,128]{2,1,0:T(1,128)} %get-tuple-element.34), calls=%async_computation.2 | async-start | bytes 131072 | tf_op jit(solution)/shard_map/all_to_all | solution.py:420
  141.0 1.3 collective-permute-done.17
  142.3 0.2 collective-permute-done.18
  142.5 1.2 fusion.5
  143.8 0.8 copy.13
  144.6 7.7 %all-to-all-done.2.sum_ref = f32[128,1,128]{2,1,0:T(1,128)S(1)} async-done(((f32[128,1,128]{2,1,0:T(1,128)}), f32[128,1,128]{2,1,0:T(1,128)S(1)}, u32[]{:S(2)}, u32[]{:S(2)}) %all-to-all-start.2) | async-done | bytes 65568 | tf_op jit(solution)/shard_map/all_to_all | solution.py:420
  152.3 0.9 update.1
  (41 shorter events, 0.2 us)
Async XLA Ops:
  2.7 64.7 %all-to-all-start = ((bf16[32,24,384]{2,1,0:T(8,128)(2,1)}), bf16[32,24,384]{2,1,0:T(8,128)(2,1)S(1)}, u32[]{:S(2)}, u32[]{:S(2)}) async-start(bf16[32,24,384]{2,1,0:T(8,128)(2,1)} %bitcast.4), calls=%async_computation | async-start | bytes 1179648 | tf_op jit(solution)/shard_map/all_to_all | solution.py:348
  15.8 27.0 %collective-permute-start = (bf16[208,1152]{1,0:T(8,128)(2,1)S(1)}, bf16[208,1152]{1,0:T(8,128)(2,1)S(1)}, u32[]{:S(2)}, u32[]{:S(2)}) collective-permute-start(bf16[208,1152]{1,0:T(8,128)(2,1)S(1)} %get-tuple-element.27), channel_id=1, source_target_pairs={{0,8},{8,16},{16,24},{24,0},{1,9},{9,17},{17,25},{25,1},{2,10},{10... | collective-permute-start | bytes 1437704 | tf_op jit(solution)/shard_map/ppermute | solution.py:40
  17.3 34.7 %collective-permute-start.2 = (bf16[186,1152]{1,0:T(8,128)(2,1)S(1)}, bf16[186,1152]{1,0:T(8,128)(2,1)S(1)}, u32[]{:S(2)}, u32[]{:S(2)}) collective-permute-start(bf16[186,1152]{1,0:T(8,128)(2,1)S(1)} %get-tuple-element.28), channel_id=1, source_target_pairs={{0,24},{8,0},{16,8},{24,16},{1,25},{9,1},{17,9},{25,17},{2,26},{10... | collective-permute-start | bytes 1285640 | tf_op jit(solution)/shard_map/ppermute | solution.py:40
  17.9 19.0 %collective-permute-start.6 = (bf16[64,1152]{1,0:T(8,128)(2,1)S(1)}, bf16[64,1152]{1,0:T(8,128)(2,1)S(1)}, u32[]{:S(2)}, u32[]{:S(2)}) collective-permute-start(bf16[64,1152]{1,0:T(8,128)(2,1)S(1)} %get-tuple-element.30), channel_id=1, source_target_pairs={{0,24},{8,0},{16,8},{24,16},{1,25},{9,1},{17,9},{25,17},{2,26},{10... | collective-permute-start | bytes 442376 | tf_op jit(solution)/shard_map/ppermute | solution.py:40
  19.4 16.2 %collective-permute-start.5 = (bf16[48,1152]{1,0:T(8,128)(2,1)S(1)}, bf16[48,1152]{1,0:T(8,128)(2,1)S(1)}, u32[]{:S(2)}, u32[]{:S(2)}) collective-permute-start(bf16[48,1152]{1,0:T(8,128)(2,1)S(1)} %get-tuple-element.29), channel_id=1, source_target_pairs={{0,8},{8,16},{16,24},{24,0},{1,9},{9,17},{17,25},{25,1},{2,10},{10... | collective-permute-start | bytes 331784 | tf_op jit(solution)/shard_map/ppermute | solution.py:40
  36.9 17.2 %copy-start = (bf16[112,1152]{1,0:T(8,128)(2,1)}, bf16[112,1152]{1,0:T(8,128)(2,1)S(1)}, u32[]{:S(2)}) copy-start(bf16[112,1152]{1,0:T(8,128)(2,1)S(1)} %join.1.refs_2_.refs_7_) | copy-start | bytes 774148
  36.9 9.3 %collective-permute-start.7 = (bf16[112,1152]{1,0:T(8,128)(2,1)S(1)}, bf16[112,1152]{1,0:T(8,128)(2,1)S(1)}, u32[]{:S(2)}, u32[]{:S(2)}) collective-permute-start(bf16[112,1152]{1,0:T(8,128)(2,1)S(1)} %join.1.refs_2_.refs_7_), channel_id=1, source_target_pairs={{0,2},{2,4},{4,6},{6,0},{1,3},{3,5},{5,7},{7,1},{8,10},{10,12},{12... | collective-permute-start | bytes 774152 | tf_op jit(solution)/shard_map/ppermute | solution.py:40
  38.6 13.5 %collective-permute-start.8 = (bf16[112,1152]{1,0:T(8,128)(2,1)S(1)}, bf16[112,1152]{1,0:T(8,128)(2,1)S(1)}, u32[]{:S(2)}, u32[]{:S(2)}) collective-permute-start(bf16[112,1152]{1,0:T(8,128)(2,1)S(1)} %join.1.refs_2_.refs_7_), channel_id=1, source_target_pairs={{0,4},{2,6},{4,0},{6,2},{1,5},{3,7},{5,1},{7,3},{8,12},{10,14},{12... | collective-permute-start | bytes 774152 | tf_op jit(solution)/shard_map/ppermute | solution.py:40
  41.5 10.6 %collective-permute-start.9 = (bf16[112,1152]{1,0:T(8,128)(2,1)S(1)}, bf16[112,1152]{1,0:T(8,128)(2,1)S(1)}, u32[]{:S(2)}, u32[]{:S(2)}) collective-permute-start(bf16[112,1152]{1,0:T(8,128)(2,1)S(1)} %join.1.refs_2_.refs_7_), channel_id=1, source_target_pairs={{0,6},{2,0},{4,2},{6,4},{1,7},{3,1},{5,3},{7,5},{8,14},{10,8},{12,... | collective-permute-start | bytes 774152 | tf_op jit(solution)/shard_map/ppermute | solution.py:40
  42.8 9.2 %copy-start.10 = (bf16[208,1152]{1,0:T(8,128)(2,1)}, bf16[208,1152]{1,0:T(8,128)(2,1)S(1)}, u32[]{:S(2)}) copy-start(bf16[208,1152]{1,0:T(8,128)(2,1)S(1)} %collective-permute-done.refs_0_.refs_5_) | copy-start | bytes 1437700
  42.8 24.2 %collective-permute-start.1 = (bf16[208,1152]{1,0:T(8,128)(2,1)S(1)}, bf16[208,1152]{1,0:T(8,128)(2,1)S(1)}, u32[]{:S(2)}, u32[]{:S(2)}) collective-permute-start(bf16[208,1152]{1,0:T(8,128)(2,1)S(1)} %collective-permute-done.refs_0_.refs_5_), channel_id=1, source_target_pairs={{0,8},{8,16},{16,24},{24,0},{1,9},{9,17},{17,25},{25,1},{2,10},{10... | collective-permute-start | bytes 1437704 | tf_op jit(solution)/shard_map/ppermute | solution.py:40
  46.2 7.9 %copy-start.5 = (bf16[112,1152]{1,0:T(8,128)(2,1)}, bf16[112,1152]{1,0:T(8,128)(2,1)S(1)}, u32[]{:S(2)}) copy-start(bf16[112,1152]{1,0:T(8,128)(2,1)S(1)} %collective-permute-done.7.refs_3_.refs_8_) | copy-start | bytes 774148
  52.1 2.1 %copy-start.6 = (bf16[112,1152]{1,0:T(8,128)(2,1)}, bf16[112,1152]{1,0:T(8,128)(2,1)S(1)}, u32[]{:S(2)}) copy-start(bf16[112,1152]{1,0:T(8,128)(2,1)S(1)} %collective-permute-done.8.refs_4_.refs_9_) | copy-start | bytes 774148
  52.1 2.1 %copy-start.7 = (bf16[112,1152]{1,0:T(8,128)(2,1)}, bf16[112,1152]{1,0:T(8,128)(2,1)S(1)}, u32[]{:S(2)}) copy-start(bf16[112,1152]{1,0:T(8,128)(2,1)S(1)} %collective-permute-done.9.refs_5_.refs_10_) | copy-start | bytes 774148
  52.1 0.8 copy-start.13
  54.2 13.2 %collective-permute-start.10 = (bf16[848,384]{1,0:T(8,128)(2,1)S(1)}, bf16[848,384]{1,0:T(8,128)(2,1)}, u32[]{:S(2)}, u32[]{:S(2)}) collective-permute-start(bf16[848,384]{1,0:T(8,128)(2,1)S(1)} %shard_map.120), channel_id=1, source_target_pairs={{0,1},{1,0},{2,3},{3,2},{4,5},{5,4},{6,7},{7,6},{8,9},{9,8},{10,11... | collective-permute-start | bytes 1953800 | tf_op jit(solution)/shard_map/ppermute | solution.py:40
  54.3 12.8 %collective-permute-start.3 = (bf16[186,1152]{1,0:T(8,128)(2,1)}, bf16[186,1152]{1,0:T(8,128)(2,1)S(1)}, u32[]{:S(2)}, u32[]{:S(2)}) collective-permute-start(bf16[186,1152]{1,0:T(8,128)(2,1)} %copy-done.13), channel_id=1, source_target_pairs={{0,24},{8,0},{16,8},{24,16},{1,25},{9,1},{17,9},{25,17},{2,26},{10... | collective-permute-start | bytes 1285640 | tf_op jit(solution)/shard_map/ppermute | solution.py:40
  67.1 6.5 %collective-permute-start.4 = (bf16[400,384]{1,0:T(8,128)(2,1)S(1)}, bf16[400,384]{1,0:T(8,128)(2,1)S(1)}, u32[]{:S(2)}, u32[]{:S(2)}) collective-permute-start(bf16[400,384]{1,0:T(8,128)(2,1)S(1)} %shard_map.119), channel_id=1, source_target_pairs={{0,1},{1,0},{2,3},{3,2},{4,5},{5,4},{6,7},{7,6},{8,9},{9,8},{10,11... | collective-permute-start | bytes 921608 | tf_op jit(solution)/shard_map/ppermute | solution.py:40
  75.8 4.5 %copy-start.8 = (bf16[592,384]{1,0:T(8,128)(2,1)}, bf16[592,384]{1,0:T(8,128)(2,1)S(1)}, u32[]{:S(2)}) copy-start(bf16[592,384]{1,0:T(8,128)(2,1)S(1)} %get-tuple-element.44) | copy-start | bytes 1363972
  75.8 3.0 %collective-permute-start.11 = (f32[768,384]{1,0:T(8,128)S(1)}, f32[768,384]{1,0:T(8,128)S(1)}, u32[]{:S(2)}, u32[]{:S(2)}) collective-permute-start(f32[768,384]{1,0:T(8,128)S(1)} %get-tuple-element.33), channel_id=1, source_target_pairs={{0,1},{1,0},{2,3},{3,2},{4,5},{5,4},{6,7},{7,6},{8,9},{9,8},{10,11... | collective-permute-start | bytes 3538952 | tf_op jit(solution)/shard_map/ppermute | solution.py:40
  80.3 11.5 %copy-start.9 = (bf16[592,384]{1,0:T(8,128)(2,1)S(1)}, bf16[592,384]{1,0:T(8,128)(2,1)}, u32[]{:S(2)}) copy-start(bf16[592,384]{1,0:T(8,128)(2,1)} %copy-done.8) | copy-start | bytes 1363972
  80.3 45.9 %all-to-all-start.1 = ((f16[32,24,384]{2,1,0:T(8,128)(2,1)}), f16[32,24,384]{2,1,0:T(8,128)(2,1)}, u32[]{:S(2)}, u32[]{:S(2)}) async-start(f16[32,24,384]{2,1,0:T(8,128)(2,1)} %bitcast.7), calls=%async_computation.1 | async-start | bytes 1179648 | tf_op jit(solution)/shard_map/all_to_all | solution.py:381
  89.7 18.4 %collective-permute-start.13 = (bf16[592,384]{1,0:T(8,128)(2,1)S(1)}, bf16[592,384]{1,0:T(8,128)(2,1)S(1)}, u32[]{:S(2)}, u32[]{:S(2)}) collective-permute-start(bf16[592,384]{1,0:T(8,128)(2,1)S(1)} %get-tuple-element.42), channel_id=1, source_target_pairs={{0,24},{8,0},{16,8},{24,16},{1,25},{9,1},{17,9},{25,17},{2,26},{10... | collective-permute-start | bytes 1363976 | tf_op jit(solution)/shard_map/ppermute | solution.py:40
  90.0 18.9 %collective-permute-start.14 = (bf16[592,384]{1,0:T(8,128)(2,1)S(1)}, bf16[592,384]{1,0:T(8,128)(2,1)S(1)}, u32[]{:S(2)}, u32[]{:S(2)}) collective-permute-start(bf16[592,384]{1,0:T(8,128)(2,1)S(1)} %get-tuple-element.43), channel_id=1, source_target_pairs={{0,8},{8,16},{16,24},{24,0},{1,9},{9,17},{17,25},{25,1},{2,10},{10... | collective-permute-start | bytes 1363976 | tf_op jit(solution)/shard_map/ppermute | solution.py:40
  91.8 26.7 %collective-permute-start.15 = (bf16[592,384]{1,0:T(8,128)(2,1)S(1)}, bf16[592,384]{1,0:T(8,128)(2,1)S(1)}, u32[]{:S(2)}, u32[]{:S(2)}) collective-permute-start(bf16[592,384]{1,0:T(8,128)(2,1)S(1)} %copy-done.9), channel_id=1, source_target_pairs={{0,16},{8,24},{16,0},{24,8},{1,17},{9,25},{17,1},{25,9},{2,18},{10... | collective-permute-start | bytes 1363976 | tf_op jit(solution)/shard_map/ppermute | solution.py:40
  108.0 10.4 %copy-start.11 = (bf16[592,384]{1,0:T(8,128)(2,1)}, bf16[592,384]{1,0:T(8,128)(2,1)S(1)}, u32[]{:S(2)}) copy-start(bf16[592,384]{1,0:T(8,128)(2,1)S(1)} %collective-permute-done.13.refs_0_) | copy-start | bytes 1363972
  109.0 9.5 %copy-start.12 = (bf16[592,384]{1,0:T(8,128)(2,1)}, bf16[592,384]{1,0:T(8,128)(2,1)S(1)}, u32[]{:S(2)}) copy-start(bf16[592,384]{1,0:T(8,128)(2,1)S(1)} %collective-permute-done.14.refs_1_) | copy-start | bytes 1363972
  118.5 10.6 %copy-start.1 = (f32[24,768]{1,0:T(8,128)S(1)}, f32[24,768]{1,0:T(8,128)}, u32[]{:S(2)}) copy-start(f32[24,768]{1,0:T(8,128)} %refs_3_.1) | copy-start | bytes 221188
  118.5 10.6 %copy-start.2 = (f32[24,768]{1,0:T(8,128)S(1)}, f32[24,768]{1,0:T(8,128)}, u32[]{:S(2)}) copy-start(f32[24,768]{1,0:T(8,128)} %refs_4_.1) | copy-start | bytes 221188
  120.9 20.1 %collective-permute-start.16 = (f32[394,192]{1,0:T(8,128)S(1)}, f32[394,192]{1,0:T(8,128)S(1)}, u32[]{:S(2)}, u32[]{:S(2)}) collective-permute-start(f32[394,192]{1,0:T(8,128)S(1)} %get-tuple-element.46), channel_id=1, source_target_pairs={{0,2},{2,4},{4,6},{6,0},{1,3},{3,5},{5,7},{7,1},{8,10},{10,12},{12... | collective-permute-start | bytes 907784 | tf_op jit(solution)/shard_map/ppermute | solution.py:40
  122.2 20.1 %collective-permute-start.17 = (f32[394,192]{1,0:T(8,128)S(1)}, f32[394,192]{1,0:T(8,128)}, u32[]{:S(2)}, u32[]{:S(2)}) collective-permute-start(f32[394,192]{1,0:T(8,128)S(1)} %get-tuple-element.47), channel_id=1, source_target_pairs={{0,4},{2,6},{4,0},{6,2},{1,5},{3,7},{5,1},{7,3},{8,12},{10,14},{12... | collective-permute-start | bytes 907784 | tf_op jit(solution)/shard_map/ppermute | solution.py:40
  124.6 17.9 %collective-permute-start.18 = (f32[394,192]{1,0:T(8,128)S(1)}, f32[394,192]{1,0:T(8,128)}, u32[]{:S(2)}, u32[]{:S(2)}) collective-permute-start(f32[394,192]{1,0:T(8,128)S(1)} %get-tuple-element.48), channel_id=1, source_target_pairs={{0,6},{2,0},{4,2},{6,4},{1,7},{3,1},{5,3},{7,5},{8,14},{10,8},{12,... | collective-permute-start | bytes 907784 | tf_op jit(solution)/shard_map/ppermute | solution.py:40
  127.6 1.5 collective-permute-start.12
  129.9 22.4 %copy-start.3 = (f32[24,768]{1,0:T(8,128)S(1)}, f32[24,768]{1,0:T(8,128)}, u32[]{:S(2)}) copy-start(f32[24,768]{1,0:T(8,128)} %mu_ref.3) | copy-start | bytes 221188
  129.9 22.4 %copy-start.4 = (f32[24,768]{1,0:T(8,128)S(1)}, f32[24,768]{1,0:T(8,128)}, u32[]{:S(2)}) copy-start(f32[24,768]{1,0:T(8,128)} %md_ref.3) | copy-start | bytes 221188
  129.9 22.4 %all-to-all-start.2 = ((f32[128,1,128]{2,1,0:T(1,128)}), f32[128,1,128]{2,1,0:T(1,128)S(1)}, u32[]{:S(2)}, u32[]{:S(2)}) async-start(f32[128,1,128]{2,1,0:T(1,128)} %get-tuple-element.34), calls=%async_computation.2 | async-start | bytes 131072 | tf_op jit(solution)/shard_map/all_to_all | solution.py:420
